TPU v7x, 1024 devices: a whole 4x8x16 slice. The times are simulated.
1024 devices in a mesh: section: 16 (over z), node: 8 (over x, core), local: 8 (over y).
Axes of the slice: x: 4, y: 8, z: 16, core: 2. Of those that a mesh axis runs over, the one named last changes fastest.
Arguments:
- tokens: bfloat16 [16, 6144, 7168], P('section', ('node', 'local')), may hold values from -6 to 6
- routes: int32 [16, 6144, 8], P('section', ('node', 'local')), may hold values from 0 to 383, as said below
- route_gates: float32 [16, 6144, 8], P('section', ('node', 'local')), may hold values from 0.2 to 1
- replica_table: int32 [8], replicated, may hold values from 0 to 5, as said below
- w_gate: bfloat16 [8, 7168, 1024], P('node', None, 'local')
- w_up: bfloat16 [8, 7168, 1024], P('node', None, 'local')
- w_down: bfloat16 [8, 1024, 7168], P('node', 'local')
Outputs:
- section_input: bfloat16 [16, 6144, 7168], P('section', ('node', 'local'))
Inputs may be any that keep to these rules, and one draw needn't show every extreme that they name: `replica_table`: each of the experts 0 to 5 is held by one or two slots; slots that hold the same expert hold equal weights in w_gate, w_up and w_down. `routes`: each row names 8 different experts. Within the rows of one device, expert e < 6 is named by at least one row and by at most 2 times its number of slots in replica_table; in every draw some expert with one slot is named by exactly 2 rows of every device.
All inputs are finite; a program needn't handle non-finite values.
Results may differ from a plain program's by a relative error of at most 0.015.
Values may be sent and summed in bfloat16 or wider, within the bound.
No kernel may reach another device: no remote copies, remote signals or barrier semaphores. Data moves between devices by JAX's collectives and lax.ppermute only.
A program may use at most 32 MiB of HBM per device.

v0:
```python
import jax
import jax.numpy as jnp
from jax import lax
from jax.sharding import PartitionSpec as P

TOPK = 8
CAP = 2


def cut_along(value, dim, size):
    before, after = (value.shape[:dim], value.shape[dim + 1 :])
    return jnp.moveaxis(value.reshape(*before, size, -1, *after), dim, 0)


def summed_on_arrival(value, axis, dim):
    tiles = cut_along(value, dim, lax.axis_size(axis))
    arrived = lax.all_to_all(tiles, axis, split_axis=0, concat_axis=0, tiled=True)
    return arrived.astype(jnp.float32).sum(axis=0)


def passed_along(block, axis, distance):
    devices = range(lax.axis_size(axis))
    route = [(i - distance, i) for i in devices if i - distance in devices]
    return lax.ppermute(block, axis, route)


def expert_rows(rows_in, gate_mat, up_mat):
    flat_rows = rows_in.reshape(-1, rows_in.shape[-1])
    gate_proj = jnp.dot(flat_rows, gate_mat, preferred_element_type=jnp.float32)
    up_proj = jnp.dot(flat_rows, up_mat, preferred_element_type=jnp.float32)
    hidden = (jax.nn.silu(gate_proj) * up_proj).astype(jnp.bfloat16)
    return hidden.reshape(rows_in.shape[:-1] + (gate_mat.shape[1],))


def shards(tokens, routes, route_gates, replica_table, w_gate, w_up, w_down):
    n_node = lax.axis_size("node")
    n_local = lax.axis_size("local")
    experts = n_node * 3 // 4
    rows_in = tokens[0]
    tok_dev = rows_in.shape[0]
    width = rows_in.shape[1]
    pick_ids = routes[0].reshape(-1)
    gate_vals = route_gates[0]
    expert_ids = jnp.arange(experts, dtype=jnp.int32)
    slot_match = replica_table[:, None] == expert_ids[None, :]
    copies = jnp.sum(slot_match.astype(jnp.int32), axis=0)
    slot_rank = jnp.cumsum(slot_match.astype(jnp.int32), axis=0) - 1
    pick_match = pick_ids[:, None] == expert_ids[None, :]
    pick_rank = jnp.cumsum(pick_match.astype(jnp.int32), axis=0) - 1
    own_rank = jnp.sum(jnp.where(pick_match, pick_rank, 0), axis=1)
    own_copies = jnp.sum(jnp.where(pick_match, copies[None, :], 0), axis=1)
    in_flight = jnp.any(pick_match, axis=1)
    safe_copies = jnp.maximum(own_copies, 1)
    replica = own_rank % safe_copies
    position = own_rank // safe_copies
    slot_hit = (
        pick_match[:, None, :]
        & slot_match[None, :, :]
        & (slot_rank[None, :, :] == replica[:, None, None])
    )
    slot_ids = jnp.arange(n_node, dtype=jnp.int32)
    slot_of = jnp.sum(jnp.where(jnp.any(slot_hit, axis=2), slot_ids[None, :], 0), axis=1)
    target = jnp.where(in_flight, slot_of * CAP + position, -1)
    buffer_ids = jnp.arange(n_node * CAP, dtype=jnp.int32)
    select = (target[None, :] == buffer_ids[:, None]).reshape(n_node * CAP, tok_dev, TOPK)
    dispatch = jnp.any(select, axis=2).astype(jnp.bfloat16)
    combine = jnp.sum(jnp.where(select, gate_vals[None, :, :], 0.0), axis=2)
    outgoing = jnp.dot(dispatch, rows_in, preferred_element_type=jnp.float32).astype(jnp.bfloat16)
    outgoing = outgoing.reshape(n_node, CAP, width)
    gate_mat = w_gate[0]
    up_mat = w_up[0]
    down_mat = w_down[0]
    spread = jnp.broadcast_to(outgoing[:, None], (n_node, n_local, CAP, width)).reshape(
        n_node * n_local, CAP, width
    )
    hidden = expert_rows(
        lax.all_to_all(spread, ("node", "local"), split_axis=0, concat_axis=0, tiled=True),
        gate_mat,
        up_mat,
    )
    hidden = jnp.transpose(hidden.reshape(n_node, n_local, CAP, -1), (1, 0, 2, 3))
    flat_hidden = hidden.reshape(n_local * n_node * CAP, -1)
    summed = summed_on_arrival(
        jnp.dot(flat_hidden, down_mat, preferred_element_type=jnp.float32).astype(jnp.bfloat16),
        "local",
        0,
    )
    expert_out = summed.astype(jnp.bfloat16).reshape(n_node, CAP, width)
    returned_rows = lax.all_to_all(
        expert_out, "node", split_axis=0, concat_axis=0, tiled=True
    ).reshape(n_node * CAP, width)
    combined = jnp.einsum(
        "ct,cd->td", combine, returned_rows.astype(jnp.float32), precision=lax.Precision.HIGHEST
    )
    layer_out = combined.astype(jnp.bfloat16)
    handed = passed_along(layer_out, "section", 1)
    return handed[None]


def solution(mesh):
    placed = (
        P("section", ("node", "local"), None),
        P("section", ("node", "local"), None),
        P("section", ("node", "local"), None),
        P(),
        P("node", None, "local"),
        P("node", None, "local"),
        P("node", "local", None),
    )
    return jax.shard_map(
        shards,
        mesh=mesh,
        in_specs=placed,
        out_specs=P("section", ("node", "local"), None),
        check_vma=False,
    )
```

profile of v0, /device:TPU:64, one launch (start us, length us, event | category | flops | bytes accessed | tf_op | source)
XLA Modules:
  0.0 177.0 jit_solution(17835012942823446084)
XLA Ops:
  0.0 0.0 copy-start
  0.0 0.9 copy.15
  0.9 0.1 eq.93
  1.0 0.1 eq.85
  1.1 0.7 convert_reduce_fusion
  1.8 0.7 iota_compare_fusion.3
  2.6 1.7 reduce-window.6
  4.3 0.2 slice_reduce_fusion
  4.5 0.2 reduce-window.9
  4.7 0.1 add_bitcast_fusion
  4.8 0.1 select_reduce_fusion.2
  4.9 0.1 maximum_divide_fusion
  5.0 0.1 fusion.19
  5.2 0.1 copy.17
  5.2 0.1 copy.16
  5.3 0.1 and_reduce_fusion
  5.5 0.1 mul.22
  5.6 0.1 div.16
  5.7 0.1 and.41
  5.8 0.1 reduce_or.30
  5.9 0.1 copy.19
  5.9 0.1 fusion.12
  6.0 1.6 convolution_convert_fusion.2
  7.6 0.1 broadcast_in_dim.72
  7.7 0.9 broadcast_in_dim.73
  8.7 55.3 %all_to_all.15 = bf16[64,2,7168]{2,1,0:T(2,128)(2,1)} all-to-all(bf16[64,2,7168]{2,1,0:T(2,128)(2,1)S(1)} %bitcast.46), channel_id=1, replica_groups=mesh['section'=16,'node'=8,'local'=8] {'node','local'}, dimensions={0} | all-to-all | bytes 3670016 | tf_op jit(solution)/shard_map/all_to_all | solution.py:77
  64.0 4.9 %reshape.157 = bf16[128,7168]{1,0:T(8,128)(2,1)} reshape(bf16[64,2,7168]{2,1,0:T(2,128)(2,1)} %all_to_all.15) | data formatting | bytes 3670016 | tf_op jit(solution)/shard_map/reshape | solution.py:28
  68.9 0.0 copy-start.1
  68.9 0.0 copy-start.2
  68.9 2.8 %fusion.3 = f32[128,128]{1,0:T(8,128)S(1)} fusion(bf16[128,7168]{1,0:T(8,128)(2,1)} %reshape.157, bf16[1,7168,128]{2,1,0:T(8,128)(2,1)} %param.11), kind=kOutput, calls=%fused_computation.6 | convolution fusion | flops 234881024 | bytes 3735552 | tf_op jit(solution)/shard_map/dot_general | solution.py:29
  71.7 0.0 copy-done.1
  71.8 0.3 copy-done.2
  72.1 0.6 fusion.9
  72.7 0.0 copy-done
  72.7 0.6 convolution_convert_fusion
  73.4 50.6 %all_to_all.16 = bf16[8,16,7168]{2,1,0:T(8,128)(2,1)} all-to-all(bf16[8,16,7168]{2,1,0:T(8,128)(2,1)S(1)} %bitcast.45), channel_id=1, replica_groups=mesh['section'=16,'node'=8,'local'=8] {'local'}, dimensions={0} | all-to-all | bytes 3670016 | tf_op jit(solution)/shard_map/all_to_all | solution.py:17
  124.0 0.0 copy-start.3
  124.0 1.8 %reduce_sum.62 = bf16[16,7168]{1,0:T(8,128)(2,1)S(1)} reduce(bf16[8,16,7168]{2,1,0:T(8,128)(2,1)} %all_to_all.16, bf16[]{:T(256)} %constant.36.clone.1), dimensions={0}, to_apply=%region_11.12 | reduce | flops 802816 | bytes 2064386 | tf_op jit(solution)/shard_map/reduce_sum | solution.py:18
  125.9 0.8 reshape.160
  126.6 3.4 %all-to-all-start.2 = ((bf16[8,2,7168]{2,1,0:T(2,128)(2,1)}), bf16[8,2,7168]{2,1,0:T(2,128)(2,1)S(1)}, u32[]{:S(2)}, u32[]{:S(2)}) async-start(bf16[8,2,7168]{2,1,0:T(2,128)(2,1)} %reshape.160), calls=%async_computation.2 | async-start | bytes 458752 | tf_op jit(solution)/shard_map/all_to_all | solution.py:89
  130.1 0.0 copy-done.3
  130.1 7.0 %all-to-all-done.2 = bf16[8,2,7168]{2,1,0:T(2,128)(2,1)S(1)} async-done(((bf16[8,2,7168]{2,1,0:T(2,128)(2,1)}), bf16[8,2,7168]{2,1,0:T(2,128)(2,1)S(1)}, u32[]{:S(2)}, u32[]{:S(2)}) %all-to-all-start.2) | async-done | bytes 229408 | tf_op jit(solution)/shard_map/all_to_all | solution.py:89
  137.1 0.1 reshape.161
  137.2 1.3 convolution_convert_fusion.1
  138.5 4.3 %collective-permute-start = (bf16[96,7168]{1,0:T(8,128)(2,1)S(1)}, bf16[96,7168]{1,0:T(8,128)(2,1)S(1)}, u32[]{:S(2)}, u32[]{:S(2)}) collective-permute-start(bf16[96,7168]{1,0:T(8,128)(2,1)S(1)} %convolution_convert_fusion.1), channel_id=1, source_target_pairs={{0,64},{64,128},{128,192},{192,256},{256,320},{320,384},{384,448},... | collective-permute-start | bytes 4128776 | tf_op jit(solution)/shard_map/ppermute | solution.py:24
  142.8 33.1 %collective-permute-done = bf16[96,7168]{1,0:T(8,128)(2,1)S(1)} collective-permute-done((bf16[96,7168]{1,0:T(8,128)(2,1)S(1)}, bf16[96,7168]{1,0:T(8,128)(2,1)S(1)}, u32[]{:S(2)}, u32[]{:S(2)}) %collective-permute-start) | collective-permute-done | bytes 1376288 | tf_op jit(solution)/shard_map/ppermute | solution.py:24
  175.9 1.1 copy.24
  (9 shorter events, 0.2 us)
Async XLA Ops:
  0.0 72.7 %copy-start = (bf16[1,128,7168]{2,1,0:T(8,128)(2,1)S(1)}, bf16[1,128,7168]{2,1,0:T(8,128)(2,1)}, u32[]{:S(2)}) copy-start(bf16[1,128,7168]{2,1,0:T(8,128)(2,1)} %param.13) | copy-start | bytes 5505028
  68.9 2.8 %copy-start.1 = (bf16[128,7168]{1,0:T(8,128)(2,1)S(1)}, bf16[128,7168]{1,0:T(8,128)(2,1)}, u32[]{:S(2)}) copy-start(bf16[128,7168]{1,0:T(8,128)(2,1)} %reshape.157) | copy-start | bytes 5505028
  68.9 3.2 %copy-start.2 = (bf16[1,7168,128]{2,1,0:T(8,128)(2,1)S(1)}, bf16[1,7168,128]{2,1,0:T(8,128)(2,1)}, u32[]{:S(2)}) copy-start(bf16[1,7168,128]{2,1,0:T(8,128)(2,1)} %param.12) | copy-start | bytes 5505028
  124.0 6.0 %copy-start.3 = (f32[1,96,8]{1,2,0:T(8,128)S(1)}, f32[1,96,8]{1,2,0:T(8,128)}, u32[]{:S(2)}) copy-start(f32[1,96,8]{1,2,0:T(8,128)} %param.9) | copy-start | bytes 9220
  126.6 10.5 %all-to-all-start.2 = ((bf16[8,2,7168]{2,1,0:T(2,128)(2,1)}), bf16[8,2,7168]{2,1,0:T(2,128)(2,1)S(1)}, u32[]{:S(2)}, u32[]{:S(2)}) async-start(bf16[8,2,7168]{2,1,0:T(2,128)(2,1)} %reshape.160), calls=%async_computation.2 | async-start | bytes 458752 | tf_op jit(solution)/shard_map/all_to_all | solution.py:89
  138.5 37.4 %collective-permute-start = (bf16[96,7168]{1,0:T(8,128)(2,1)S(1)}, bf16[96,7168]{1,0:T(8,128)(2,1)S(1)}, u32[]{:S(2)}, u32[]{:S(2)}) collective-permute-start(bf16[96,7168]{1,0:T(8,128)(2,1)S(1)} %convolution_convert_fusion.1), channel_id=1, source_target_pairs={{0,64},{64,128},{128,192},{192,256},{256,320},{320,384},{384,448},... | collective-permute-start | bytes 4128776 | tf_op jit(solution)/shard_map/ppermute | solution.py:24
where the time goes:
time: 177 us
  blocking collectives  106 us (60%)
  waiting for transfers between devices  40.2 us (23%)
  local copies, waits for them, and re-layouts  10.2 us (6%)
  starting transfers between devices  7.68 us (4%)
  matrix products  6.98 us (4%)
  other arithmetic  5.85 us (3%)
    all_to_all x1, blocking collectives, shards(): lax.all_to_all(spread, ('node', 'local'), split_axis=0, concat_axis=0, ti...  55.3 us
    all_to_all x1, blocking collectives, summed_on_arrival(): lax.all_to_all(tiles, axis, split_axis=0, concat_axis=0, tiled=True)  50.6 us
    ppermute x1, waiting for transfers between devices, passed_along(): return lax.ppermute(block, axis, route)  33.1 us
    all_to_all x1, waiting for transfers between devices, shards(): lax.all_to_all(expert_out, 'node', split_axis=0, concat_axis=0, tiled=True)  7.04 us
    reshape x1, local copies, waits for them, and re-layouts, expert_rows(): flat_rows = rows_in.reshape(-1, rows_in.shape[-1])  4.91 us
    ppermute x1, starting transfers between devices, passed_along(): return lax.ppermute(block, axis, route)  4.28 us
  transfers between devices with their start and end apart: 2, of which 2 were waited for; matrix products, arithmetic and copies ran while one was open for 0% of the time, Pallas kernels for 0%

commit v1 on v0

v1 whole, which is shorter than its diff:
```python
import jax
import jax.numpy as jnp
from jax import lax
from jax.sharding import PartitionSpec as P

TOPK = 8
CAP = 2


def passed_along(block, axis, distance):
    devices = range(lax.axis_size(axis))
    route = [(i - distance, i) for i in devices if i - distance in devices]
    return lax.ppermute(block, axis, route)


def routing(routes, route_gates, replica_table, n_node, tok_dev):
    experts = n_node * 3 // 4
    pick_ids = routes[0].reshape(-1)
    gate_vals = route_gates[0]
    expert_ids = jnp.arange(experts, dtype=jnp.int32)
    slot_match = replica_table[:, None] == expert_ids[None, :]
    copies = jnp.sum(slot_match.astype(jnp.int32), axis=0)
    slot_rank = jnp.cumsum(slot_match.astype(jnp.int32), axis=0) - 1
    pick_match = pick_ids[:, None] == expert_ids[None, :]
    pick_rank = jnp.cumsum(pick_match.astype(jnp.int32), axis=0) - 1
    own_rank = jnp.sum(jnp.where(pick_match, pick_rank, 0), axis=1)
    own_copies = jnp.sum(jnp.where(pick_match, copies[None, :], 0), axis=1)
    in_flight = jnp.any(pick_match, axis=1)
    safe_copies = jnp.maximum(own_copies, 1)
    replica = own_rank % safe_copies
    position = own_rank // safe_copies
    slot_hit = (
        pick_match[:, None, :]
        & slot_match[None, :, :]
        & (slot_rank[None, :, :] == replica[:, None, None])
    )
    slot_ids = jnp.arange(n_node, dtype=jnp.int32)
    slot_of = jnp.sum(jnp.where(jnp.any(slot_hit, axis=2), slot_ids[None, :], 0), axis=1)
    target = jnp.where(in_flight, slot_of * CAP + position, -1)
    buffer_ids = jnp.arange(n_node * CAP, dtype=jnp.int32)
    select = (target[None, :] == buffer_ids[:, None]).reshape(n_node * CAP, tok_dev, TOPK)
    dispatch = jnp.any(select, axis=2).astype(jnp.bfloat16)
    combine = jnp.sum(jnp.where(select, gate_vals[None, :, :], 0.0), axis=2)
    return dispatch, combine


def shards(tokens, routes, route_gates, replica_table, w_gate, w_up, w_down):
    n_node = lax.axis_size("node")
    n_local = lax.axis_size("local")
    rows_in = tokens[0]
    tok_dev, width = rows_in.shape
    rows_dev = n_node * CAP
    dispatch, combine = routing(routes, route_gates, replica_table, n_node, tok_dev)
    weights = passed_along(combine, "section", 1)
    outgoing = jnp.dot(dispatch, rows_in, preferred_element_type=jnp.float32).astype(jnp.bfloat16)
    arrived = lax.all_to_all(
        outgoing.reshape(n_node, CAP, width), "node", split_axis=0, concat_axis=0, tiled=True
    ).reshape(rows_dev, width)
    rows = lax.all_gather(arrived, "local", axis=0, tiled=True)
    gate_proj = jnp.dot(rows, w_gate[0], preferred_element_type=jnp.float32)
    up_proj = jnp.dot(rows, w_up[0], preferred_element_type=jnp.float32)
    hidden = (jax.nn.silu(gate_proj) * up_proj).astype(jnp.bfloat16)
    parts = jnp.dot(hidden, w_down[0], preferred_element_type=jnp.float32).astype(jnp.bfloat16)
    expert_out = lax.psum_scatter(parts, "local", scatter_dimension=0, tiled=True)
    returned = lax.all_to_all(
        expert_out.reshape(n_node, CAP, width), "node", split_axis=0, concat_axis=0, tiled=True
    ).reshape(rows_dev, width)
    handed = passed_along(returned, "section", 1)
    combined = jnp.einsum(
        "ct,cd->td", weights, handed.astype(jnp.float32), precision=lax.Precision.HIGHEST
    )
    return combined.astype(jnp.bfloat16)[None]


def solution(mesh):
    placed = (
        P("section", ("node", "local"), None),
        P("section", ("node", "local"), None),
        P("section", ("node", "local"), None),
        P(),
        P("node", None, "local"),
        P("node", None, "local"),
        P("node", "local", None),
    )
    return jax.shard_map(
        shards,
        mesh=mesh,
        in_specs=placed,
        out_specs=P("section", ("node", "local"), None),
        check_vma=False,
    )
```

time: 177 us -> 167 us (0.944)
  blocking collectives: 106 us -> 22.4 us
  waiting for transfers between devices: 40.2 us -> 104 us
  between operations: 0.2 us -> 13.6 us
  local copies, waits for them, and re-layouts: 10.2 us -> 3.91 us
  matrix products: 6.98 us -> 11.2 us
  other arithmetic: 5.85 us -> 4.02 us
    all_to_all x2, blocking collectives: 106 us -> 22.4 us  [the longest x1 11.3 us: shards(): lax.all_to_all(outgoing.reshape(n_node, CAP, width), 'node', split_axis=0...]
    all_gather x0 -> x1, waiting for transfers between devices: none -> 53.5 us  [shards(): rows = lax.all_gather(arrived, 'local', axis=0, tiled=True)]
    reduce_scatter x0 -> x1, waiting for transfers between devices: none -> 48.7 us  [shards(): lax.psum_scatter(parts, 'local', scatter_dimension=0, tiled=True)]
    ppermute x1 -> x2, waiting for transfers between devices: 33.1 us -> 1.99 us  [passed_along(): return lax.ppermute(block, axis, route)]
    all_to_all x1 -> x0, waiting for transfers between devices: 7.04 us -> none  [shards(): lax.all_to_all(expert_out, 'node', split_axis=0, concat_axis=0, tiled=True)]
    dot_general x4 -> x3, matrix products: 5.35 us -> 9.54 us  [the longest x1 4.52 us: shards(): jnp.dot(hidden, w_down[0], preferred_element_type=jnp.float32)]
    reshape x3 -> x4, local copies, waits for them, and re-layouts: 5.77 us -> 1.98 us  [the longest x1 1.02 us: shards(): expert_out.reshape(n_node, CAP, width)]
    all_to_all x1 -> x0, starting transfers between devices: 3.4 us -> none  [shards(): lax.all_to_all(expert_out, 'node', split_axis=0, concat_axis=0, tiled=True)]
  transfers between devices with their start and end apart: 2 -> 4, of which waited for: 2 -> 3; matrix products, arithmetic and copies ran while one was open for 0% -> 0% of each run, Pallas kernels for 0% -> 0%
where the time goes in v1:
time: 167 us; the launch traced here: 166 us
  waiting for transfers between devices  104 us (62%)
  blocking collectives  22.4 us (13%)
  between operations  13.6 us (8%)
  matrix products  11.2 us (7%)
  starting transfers between devices  7.15 us (4%)
  other arithmetic  4.02 us (2%)
  local copies, waits for them, and re-layouts  3.91 us (2%)
    all_gather x1, waiting for transfers between devices, shards(): rows = lax.all_gather(arrived, 'local', axis=0, tiled=True)  53.5 us
    reduce_scatter x1, waiting for transfers between devices, shards(): lax.psum_scatter(parts, 'local', scatter_dimension=0, tiled=True)  48.7 us
    all_to_all x1, blocking collectives, shards(): lax.all_to_all(outgoing.reshape(n_node, CAP, width), 'node', split_axis=0...  11.3 us
    all_to_all x1, blocking collectives, shards(): lax.all_to_all(expert_out.reshape(n_node, CAP, width), 'node', split_axis...  11.1 us
    ppermute x2, starting transfers between devices, passed_along(): return lax.ppermute(block, axis, route)  7.11 us
    dot_general x1, matrix products, shards(): jnp.dot(hidden, w_down[0], preferred_element_type=jnp.float32)  4.52 us
  transfers between devices with their start and end apart: 4, of which 3 were waited for; matrix products, arithmetic and copies ran while one was open for 0% of the time, Pallas kernels for 0%

profile of v1, /device:TPU:64, one launch (start us, length us, event | category | flops | bytes accessed | tf_op | source)
XLA Modules:
  0.0 166.4 jit_solution(2720120803523904901)
XLA Ops:
  6.5 0.0 copy-start
  6.5 0.0 all-gather.2.cloned.1.call-start
  6.5 0.9 copy.14
  7.5 0.1 eq.93
  7.5 0.1 eq.85
  7.6 0.7 convert_reduce_fusion
  8.4 0.7 iota_compare_fusion.3
  9.1 1.7 %reduce-window.6 = s32[6,6,128]{2,1,0:T(8,128)S(1)} reduce-window(s32[6,6,128]{2,1,0:T(8,128)S(1)} %fusion.26, s32[]{:T(128)} %constant.20.clone.1), window={size=1x1x128 pad=0_0x0_0x127_0}, to_apply=%region_2.3 | reduce-window | flops 585216 | bytes 36868 | tf_op jit(solution)/shard_map/reduce-window
  10.8 0.2 slice_reduce_fusion
  11.1 0.2 reduce-window.9
  11.2 0.1 add_bitcast_fusion
  11.3 0.1 select_reduce_fusion.2
  11.4 0.1 maximum_divide_fusion
  11.5 0.1 fusion.28
  11.7 0.1 copy.16
  11.8 0.1 copy.15
  11.9 0.1 and_reduce_fusion
  12.0 0.1 mul.22
  12.1 0.1 div.16
  12.2 0.1 and.41
  12.3 0.1 reduce_or.30
  12.4 0.1 copy.18
  12.5 0.1 fusion.20
  12.5 1.6 convolution_convert_fusion.2
  14.2 0.1 reshape.149
  14.3 11.3 %all_to_all.10 = bf16[8,2,7168]{2,1,0:T(2,128)(2,1)S(1)} all-to-all(bf16[8,2,7168]{2,1,0:T(2,128)(2,1)S(1)} %reshape.149), channel_id=1, replica_groups=mesh['section'=16,'node'=8,'local'=8] {'node'}, dimensions={0} | all-to-all | bytes 458752 | tf_op jit(solution)/shard_map/all_to_all | solution.py:56
  25.5 0.8 reshape.150
  26.3 0.0 all-gather.2.cloned.1.call-update
  26.3 0.0 reduce-scatter.2.cloned.1.call-start
  26.4 53.5 %all-gather.2.cloned.1.call-done = bf16[128,7168]{1,0:T(8,128)(2,1)} async-done(((bf16[16,7168]{1,0:T(8,128)(2,1)}), bf16[128,7168]{1,0:T(8,128)(2,1)}) %all-gather.2.cloned.1.call-update) | async-done | bytes 1835024 | tf_op jit(solution)/shard_map/all_gather | solution.py:59
  79.9 2.7 %fusion.4 = f32[128,128]{1,0:T(8,128)S(1)} fusion(bf16[128,7168]{1,0:T(8,128)(2,1)} %all-gather.2.cloned.1.call-done, bf16[1,7168,128]{2,1,0:T(8,128)(2,1)} %param.11), kind=kOutput, calls=%fused_computation.7 | convolution fusion | flops 234881024 | bytes 3735552 | tf_op jit(solution)/shard_map/dot_general | solution.py:60
  82.5 0.0 copy-done
  82.5 4.5 %convolution_convert_fusion = bf16[128,7168]{1,0:T(8,128)(2,1)} fusion(bf16[1,128,7168]{2,1,0:T(8,128)(2,1)S(1)} %copy-done, bf16[128,7168]{1,0:T(8,128)(2,1)} %all-gather.2.cloned.1.call-done, bf16[1,7168,128]{2,1,0:T(8,128)(2,1)} %param.12, f32[128,128]{1,0:T(8,128)S(1)} %fusion.4), kind=kOutput, calls=%fused_computation | convolution fusion | flops 470777856 | bytes 7405568 | tf_op jit(solution)/shard_map/dot_general | solution.py:63
  87.1 0.0 copy-start.1
  87.1 0.0 reduce-scatter.2.cloned.1.call-update
  87.1 48.7 %reduce-scatter.2.cloned.1.call-done = bf16[16,7168]{1,0:T(8,128)(2,1)} async-done(((bf16[128,7168]{1,0:T(8,128)(2,1)}), bf16[16,7168]{1,0:T(8,128)(2,1)}) %reduce-scatter.2.cloned.1.call-update) | async-done | bytes 229392 | tf_op jit(solution)/shard_map/reduce_scatter | solution.py:64
  135.8 1.0 reshape.151
  136.8 11.1 %all_to_all.11 = bf16[8,2,7168]{2,1,0:T(2,128)(2,1)S(1)} all-to-all(bf16[8,2,7168]{2,1,0:T(2,128)(2,1)S(1)} %reshape.151), channel_id=1, replica_groups=mesh['section'=16,'node'=8,'local'=8] {'node'}, dimensions={0} | all-to-all | bytes 458752 | tf_op jit(solution)/shard_map/all_to_all | solution.py:65
  148.0 0.1 reshape.152
  148.1 3.6 %collective-permute-start.1 = (bf16[16,7168]{1,0:T(8,128)(2,1)S(1)}, bf16[16,7168]{1,0:T(8,128)(2,1)S(1)}, u32[]{:S(2)}, u32[]{:S(2)}) collective-permute-start(bf16[16,7168]{1,0:T(8,128)(2,1)S(1)} %reshape.152), channel_id=1, source_target_pairs={{0,64},{64,128},{128,192},{192,256},{256,320},{320,384},{384,448},... | collective-permute-start | bytes 688136 | tf_op jit(solution)/shard_map/ppermute | solution.py:13
  151.6 0.0 copy-done.1
  151.7 3.6 %collective-permute-start = (f32[16,96]{1,0:T(8,128)S(1)}, f32[16,96]{1,0:T(8,128)S(1)}, u32[]{:S(2)}, u32[]{:S(2)}) collective-permute-start(f32[16,96]{1,0:T(8,128)S(1)} %select_reduce_fusion), channel_id=1, source_target_pairs={{0,64},{64,128},{128,192},{192,256},{256,320},{320,384},{384,448},... | collective-permute-start | bytes 18440 | tf_op jit(solution)/shard_map/ppermute | solution.py:13
  155.2 2.0 %collective-permute-done = f32[16,96]{1,0:T(8,128)S(1)} collective-permute-done((f32[16,96]{1,0:T(8,128)S(1)}, f32[16,96]{1,0:T(8,128)S(1)}, u32[]{:S(2)}, u32[]{:S(2)}) %collective-permute-start) | collective-permute-done | bytes 6176 | tf_op jit(solution)/shard_map/ppermute | solution.py:13
  157.2 0.0 collective-permute-done.1
  157.2 2.3 %fusion = bf16[1,96,7168]{2,1,0:T(8,128)(2,1)} fusion(f32[16,96]{1,0:T(8,128)S(1)} %collective-permute-done, bf16[16,7168]{1,0:T(8,128)(2,1)S(1)} %collective-permute-done.1), kind=kOutput, calls=%fused_computation.2 | convolution fusion | flops 132808704 | bytes 1611776 | tf_op jit(solution)/shard_map/ct,cd->td/dot_general | solution.py:69
  (8 shorter events, 0.1 us)
Async XLA Ops:
  6.5 76.0 %copy-start = (bf16[1,128,7168]{2,1,0:T(8,128)(2,1)S(1)}, bf16[1,128,7168]{2,1,0:T(8,128)(2,1)}, u32[]{:S(2)}) copy-start(bf16[1,128,7168]{2,1,0:T(8,128)(2,1)} %param.13) | copy-start | bytes 5505028
  6.5 73.3 %all-gather.2.cloned.1.call-start = ((), (), s32[]{:S(2)}) async-start(), calls=%async_computation.3 | async-start | bytes 2064384 | tf_op jit(solution)/shard_map/all_gather | solution.py:59
  26.3 109.5 %reduce-scatter.2.cloned.1.call-start = ((), (), s32[]{:S(2)}) async-start(), calls=%async_computation.4 | async-start | bytes 2064384 | tf_op jit(solution)/shard_map/reduce_scatter | solution.py:64
  87.1 64.6 %copy-start.1 = (f32[1,96,8]{1,2,0:T(8,128)S(1)}, f32[1,96,8]{1,2,0:T(8,128)}, u32[]{:S(2)}) copy-start(f32[1,96,8]{1,2,0:T(8,128)} %param.9) | copy-start | bytes 9220
  148.1 9.2 %collective-permute-start.1 = (bf16[16,7168]{1,0:T(8,128)(2,1)S(1)}, bf16[16,7168]{1,0:T(8,128)(2,1)S(1)}, u32[]{:S(2)}, u32[]{:S(2)}) collective-permute-start(bf16[16,7168]{1,0:T(8,128)(2,1)S(1)} %reshape.152), channel_id=1, source_target_pairs={{0,64},{64,128},{128,192},{192,256},{256,320},{320,384},{384,448},... | collective-permute-start | bytes 688136 | tf_op jit(solution)/shard_map/ppermute | solution.py:13
  151.7 5.5 %collective-permute-start = (f32[16,96]{1,0:T(8,128)S(1)}, f32[16,96]{1,0:T(8,128)S(1)}, u32[]{:S(2)}, u32[]{:S(2)}) collective-permute-start(f32[16,96]{1,0:T(8,128)S(1)} %select_reduce_fusion), channel_id=1, source_target_pairs={{0,64},{64,128},{128,192},{192,256},{256,320},{320,384},{384,448},... | collective-permute-start | bytes 18440 | tf_op jit(solution)/shard_map/ppermute | solution.py:13
Sparse Core Ops, SparseCore 0:
  26.4 53.3 all-gather.1
  87.2 48.5 reduce-scatter.1

commit v2 on v1

v2 whole, which is shorter than its diff:
```python
import jax
import jax.numpy as jnp
from jax import lax
from jax.experimental import pallas as pl
from jax.experimental.pallas import tpu as pltpu
from jax.sharding import PartitionSpec as P

CAP = 2
COLUMNS = 896
VMEM = pl.BlockSpec(memory_space=pltpu.VMEM)
ANY = pl.BlockSpec(memory_space=pl.ANY)


def grant(mib):
    return pltpu.CompilerParams(vmem_limit_bytes=mib * 1024 * 1024)


def cost(flops, moved):
    return pl.CostEstimate(flops=flops, bytes_accessed=moved, transcendentals=0)


def pick_kernel(table_ref, routes_ref, gates_ref, tokens_ref, rows_ref, combine_ref):
    slots = table_ref.shape[0]
    rows_dev = rows_ref.shape[0]
    tok_dev = tokens_ref.shape[0]
    picks = routes_ref[...]
    gates = gates_ref[...]
    row_slot = lax.broadcasted_iota(jnp.int32, (rows_dev, tok_dev), 0) // CAP
    row_pos = lax.broadcasted_iota(jnp.int32, (rows_dev, tok_dev), 0) % CAP
    named = jnp.zeros((rows_dev, tok_dev), jnp.float32)
    weight = jnp.zeros((rows_dev, tok_dev), jnp.float32)
    want = jnp.zeros((rows_dev, tok_dev), jnp.int32)
    for s in range(slots):
        expert = table_ref[s]
        copies = jnp.int32(0)
        earlier = jnp.int32(0)
        for other in range(slots):
            same = (table_ref[other] == expert).astype(jnp.int32)
            copies = copies + same
            if other < s:
                earlier = earlier + same
        match = picks == expert
        named_s = jnp.sum(match.astype(jnp.float32), axis=0, keepdims=True)
        weight_s = jnp.sum(jnp.where(match, gates, 0.0), axis=0, keepdims=True)
        here = row_slot == s
        named = jnp.where(here, named_s, named)
        weight = jnp.where(here, weight_s, weight)
        want = jnp.where(here, row_pos * copies + earlier, want)
    before = lax.broadcasted_iota(jnp.int32, (tok_dev, tok_dev), 0)
    after = lax.broadcasted_iota(jnp.int32, (tok_dev, tok_dev), 1)
    triangle = (before < after).astype(jnp.float32).astype(jnp.bfloat16)
    rank = jnp.dot(named.astype(jnp.bfloat16), triangle, preferred_element_type=jnp.float32)
    chosen = (named > 0.0) & (rank == want.astype(jnp.float32))
    combine_ref[...] = jnp.where(chosen, weight, 0.0)
    select = jnp.where(chosen, 1.0, 0.0).astype(jnp.bfloat16)
    rows_ref[...] = jnp.dot(select, tokens_ref[...], preferred_element_type=jnp.float32).astype(
        jnp.bfloat16
    )


def pick_rows(table, picks, gates, tokens, rows_dev):
    tok_dev, width = tokens.shape
    return pl.pallas_call(
        pick_kernel,
        out_shape=(
            jax.ShapeDtypeStruct((rows_dev, width), jnp.bfloat16),
            jax.ShapeDtypeStruct((rows_dev, tok_dev), jnp.float32),
        ),
        in_specs=[pl.BlockSpec(memory_space=pltpu.SMEM), VMEM, VMEM, VMEM],
        out_specs=(VMEM, VMEM),
        compiler_params=grant(8),
        cost_estimate=cost(2 * rows_dev * tok_dev * width, 2 * (tok_dev + rows_dev) * width),
        name="pick_rows",
    )(table, picks, gates, tokens)


def experts_kernel(n, *refs):
    blocks, (gate_ref, up_ref, down_ref), outs = refs[:n], refs[n : n + 3], refs[n + 4 :]
    rows_dev, width = blocks[0].shape
    hid = gate_ref.shape[1]
    gate_proj = jnp.zeros((n * rows_dev, hid), jnp.float32)
    up_proj = jnp.zeros((n * rows_dev, hid), jnp.float32)
    for c in range(0, width, COLUMNS):
        cols = slice(c, min(c + COLUMNS, width))
        rows = jnp.concatenate([b[:, cols] for b in blocks], axis=0)
        gate_proj += jnp.dot(rows, gate_ref[cols, :], preferred_element_type=jnp.float32)
        up_proj += jnp.dot(rows, up_ref[cols, :], preferred_element_type=jnp.float32)
    silu = gate_proj / (1.0 + jnp.exp(-gate_proj))
    hidden = (silu * up_proj).astype(jnp.bfloat16)
    for c in range(0, width, COLUMNS):
        cols = slice(c, min(c + COLUMNS, width))
        part = jnp.dot(hidden, down_ref[:, cols], preferred_element_type=jnp.float32)
        part = part.astype(jnp.bfloat16)
        for k in range(n):
            outs[k][:, cols] = part[k * rows_dev : (k + 1) * rows_dev]


def experts(blocks, w_gate, w_up, w_down, after):
    n = len(blocks)
    rows_dev, width = blocks[0].shape
    hid = w_gate.shape[1]
    return pl.pallas_call(
        lambda *refs: experts_kernel(n, *refs),
        out_shape=[jax.ShapeDtypeStruct((rows_dev, width), jnp.bfloat16)] * n,
        in_specs=[VMEM] * (n + 3) + [ANY],
        out_specs=[VMEM] * n,
        compiler_params=grant(24),
        cost_estimate=cost(6 * n * rows_dev * width * hid, 6 * width * hid),
        name="experts",
    )(*blocks, w_gate, w_up, w_down, after)


def plus_kernel(*refs):
    total = refs[0][...].astype(jnp.float32)
    for ref in refs[1:-1]:
        total = total + ref[...].astype(jnp.float32)
    refs[-1][...] = total.astype(jnp.bfloat16)


def plus(*terms, after=None):
    held = () if after is None else (after,)
    body = plus_kernel if after is None else (lambda *r: plus_kernel(*r[:-2], r[-1]))
    return pl.pallas_call(
        body,
        out_shape=jax.ShapeDtypeStruct(terms[0].shape, jnp.bfloat16),
        in_specs=[VMEM] * len(terms) + [ANY] * len(held),
        out_specs=VMEM,
        compiler_params=grant(4),
        cost_estimate=cost(len(terms) * terms[0].size, 2 * (len(terms) + 1) * terms[0].size),
        name="plus",
    )(*terms, *held)


def combine_kernel(weights_ref, rows_ref, out_ref):
    weights = weights_ref[...]
    high = weights.astype(jnp.bfloat16)
    rest = weights - high.astype(jnp.float32)
    middle = rest.astype(jnp.bfloat16)
    low = (rest - middle.astype(jnp.float32)).astype(jnp.bfloat16)
    split = jnp.concatenate([high, middle, low], axis=0)
    rows = rows_ref[...]
    rows = jnp.concatenate([rows, rows, rows], axis=0)
    out_ref[...] = lax.dot_general(
        split, rows, (((0,), (0,)), ((), ())), preferred_element_type=jnp.float32
    ).astype(jnp.bfloat16)


def combine_rows(weights, rows):
    rows_dev, tok_dev = weights.shape
    width = rows.shape[1]
    block = width // 4
    return pl.pallas_call(
        combine_kernel,
        grid=(4,),
        out_shape=jax.ShapeDtypeStruct((tok_dev, width), jnp.bfloat16),
        in_specs=[
            pl.BlockSpec((rows_dev, tok_dev), lambda j: (0, 0)),
            pl.BlockSpec((rows_dev, block), lambda j: (0, j)),
        ],
        out_specs=pl.BlockSpec((tok_dev, block), lambda j: (0, j)),
        compiler_params=grant(8),
        cost_estimate=cost(6 * rows_dev * tok_dev * width, 2 * (tok_dev + rows_dev) * width),
        name="combine_rows",
    )(weights, rows)


def hop(block, step, sections=0):
    count = lax.axis_size("section")
    nodes = lax.axis_size("node")
    n = lax.axis_size("local")
    pairs = []
    for s in range(count - sections):
        for node in range(nodes):
            way = step if node % 2 == 0 else -step
            for i in range(n):
                source = (s * nodes + node) * n + i
                pairs.append((source, ((s + sections) * nodes + node) * n + (i + way) % n))
    return lax.ppermute(block, ("section", "node", "local"), pairs)


def shards(tokens, routes, route_gates, replica_table, w_gate, w_up, w_down):
    n_node = lax.axis_size("node")
    far = lax.axis_size("local") // 2
    rows_dev = n_node * CAP
    width = tokens.shape[2]
    outgoing, combine = pick_rows(replica_table, routes[0].T, route_gates[0].T, tokens[0], rows_dev)
    weights = hop(combine, 0, 1)
    own = lax.all_to_all(
        outgoing.reshape(n_node, CAP, width), "node", split_axis=0, concat_axis=0, tiled=True
    ).reshape(rows_dev, width)
    blocks = {0: own}
    ahead, back = own, own
    for q in range(1, far):
        ahead, back = hop(ahead, 1), hop(back, -1)
        blocks[-q], blocks[q] = ahead, back
    blocks[far] = hop(ahead, 1)
    order = sorted(blocks)
    parts = experts([blocks[q] for q in order], w_gate[0], w_up[0], w_down[0], weights)
    part = dict(zip(order, parts))
    mine = hop(part[0], 0, 1)
    ahead, back = hop(part[far], 1), hop(part[1 - far], -1)
    for q in range(far - 1, 0, -1):
        last = q == 1
        ahead = plus(part[q], ahead, after=mine if last else None)
        if not last:
            back = hop(plus(part[1 - q], back), -1, 1 if q == 2 else 0)
        ahead = hop(ahead, 1, 1 if last else 0)
    expert_out = plus(mine, back, ahead)
    returned = lax.all_to_all(
        expert_out.reshape(n_node, CAP, width), "node", split_axis=0, concat_axis=0, tiled=True
    ).reshape(rows_dev, width)
    return combine_rows(weights, returned)[None]


def solution(mesh):
    placed = (
        P("section", ("node", "local"), None),
        P("section", ("node", "local"), None),
        P("section", ("node", "local"), None),
        P(),
        P("node", None, "local"),
        P("node", None, "local"),
        P("node", "local", None),
    )
    return jax.shard_map(
        shards,
        mesh=mesh,
        in_specs=placed,
        out_specs=P("section", ("node", "local"), None),
        check_vma=False,
    )
```

time: 167 us -> 122 us (0.73)
  waiting for transfers between devices: 104 us -> 36.5 us
  starting transfers between devices: 7.15 us -> 51.3 us
  between operations: 13.6 us -> 0.25 us
  matrix products: 11.2 us -> 0 us
  Pallas kernels: 0 us -> 5.4 us
  other arithmetic: 4.02 us -> 0 us
  local copies, waits for them, and re-layouts: 3.91 us -> 6.86 us
    all_gather x1 -> x0, waiting for transfers between devices: 53.5 us -> none  [shards(): rows = lax.all_gather(arrived, 'local', axis=0, tiled=True)]
    reduce_scatter x1 -> x0, waiting for transfers between devices: 48.7 us -> none  [shards(): lax.psum_scatter(parts, 'local', scatter_dimension=0, tiled=True)]
    ppermute x2 -> x16, starting transfers between devices: 7.11 us -> 51.3 us  [hop(): return lax.ppermute(block, ('section', 'node', 'local'), pairs)]
    ppermute x2 -> x16, waiting for transfers between devices: 1.99 us -> 36.5 us  [hop(): return lax.ppermute(block, ('section', 'node', 'local'), pairs)]
    dot_general x4 -> x0, matrix products: 11.2 us -> none  [the longest x1 4.52 us: shards(): jnp.dot(hidden, w_down[0], preferred_element_type=jnp.float32)]
    unnamed x5 -> x14, local copies, waits for them, and re-layouts: 0.92 us -> 6.5 us
    pallas_call x0 -> x9, Pallas kernels: none -> 5.4 us  [the longest x1 2.37 us: combine_rows(): pl.pallas_call(combine_kernel, grid=(4,), out_shape=jax.ShapeDtypeStruct(...]
    another operation x3 -> x0, other arithmetic: 1.88 us -> none
  transfers between devices with their start and end apart: 4 -> 16, of which waited for: 3 -> 9; matrix products, arithmetic and copies ran while one was open for 0% -> 0% of each run, Pallas kernels for 0% -> 0%
where the time goes in v2:
time: 122 us; the launch traced here: 121 us
  starting transfers between devices  51.3 us (42%)
  waiting for transfers between devices  36.5 us (30%)
  blocking collectives  20.8 us (17%)
  local copies, waits for them, and re-layouts  6.86 us (6%)
  Pallas kernels  5.4 us (4%)
    ppermute x16, starting transfers between devices, hop(): return lax.ppermute(block, ('section', 'node', 'local'), pairs)  51.3 us
    ppermute x16, waiting for transfers between devices, hop(): return lax.ppermute(block, ('section', 'node', 'local'), pairs)  36.5 us
    all_to_all x1, blocking collectives, shards(): lax.all_to_all(outgoing.reshape(n_node, CAP, width), 'node', split_axis=0...  11.3 us
    all_to_all x1, blocking collectives, shards(): lax.all_to_all(expert_out.reshape(n_node, CAP, width), 'node', split_axis...  9.56 us
    unnamed x14, local copies, waits for them, and re-layouts  6.5 us
  transfers between devices with their start and end apart: 16, of which 9 were waited for; matrix products, arithmetic and copies ran while one was open for 0% of the time, Pallas kernels for 0%

profile of v2, /device:TPU:64, one launch (start us, length us, event | category | flops | bytes accessed | tf_op | source)
XLA Modules:
  0.0 121.1 jit_solution(16147413205805823854)
XLA Ops:
  0.0 0.0 copy-start
  0.0 0.0 copy-start.3
  0.0 1.5 %copy-done.3 = bf16[1,96,7168]{2,1,0:T(8,128)(2,1)S(1)} copy-done((bf16[1,96,7168]{2,1,0:T(8,128)(2,1)S(1)}, bf16[1,96,7168]{2,1,0:T(8,128)(2,1)}, u32[]{:S(2)}) %copy-start.3) | copy-done | bytes 1376280
  1.5 0.0 copy-start.4
  1.5 0.7 copy-done.4
  2.2 0.0 copy-start.5
  2.2 0.7 copy-done.5
  2.9 0.0 copy-start.6
  2.9 0.7 copy-done.6
  3.5 0.9 pick_rows.1
  4.5 0.1 reshape.12
  4.6 11.3 %all_to_all.10 = bf16[8,2,7168]{2,1,0:T(2,128)(2,1)S(1)} all-to-all(bf16[8,2,7168]{2,1,0:T(2,128)(2,1)S(1)} %reshape.12), channel_id=1, replica_groups=mesh['section'=16,'node'=8,'local'=8] {'node'}, dimensions={0} | all-to-all | bytes 458752 | tf_op jit(solution)/shard_map/all_to_all | solution.py:188
  15.8 0.1 reshape.13.refs_3_
  15.9 3.5 %collective-permute-start.1 = (bf16[16,7168]{1,0:T(8,128)(2,1)S(1)}, bf16[16,7168]{1,0:T(8,128)(2,1)S(1)}, u32[]{:S(2)}, u32[]{:S(2)}) collective-permute-start(bf16[16,7168]{1,0:T(8,128)(2,1)S(1)} %reshape.13.refs_3_), channel_id=1, source_target_pairs={{0,1},{1,2},{2,3},{3,4},{4,5},{5,6},{6,7},{7,0},{8,15},{9,8},{10,9... | collective-permute-start | bytes 688136 | tf_op jit(solution)/shard_map/ppermute | solution.py:178
  19.4 3.8 %collective-permute-start.4 = (bf16[16,7168]{1,0:T(8,128)(2,1)S(1)}, bf16[16,7168]{1,0:T(8,128)(2,1)S(1)}, u32[]{:S(2)}, u32[]{:S(2)}) collective-permute-start(bf16[16,7168]{1,0:T(8,128)(2,1)S(1)} %reshape.13.refs_3_), channel_id=1, source_target_pairs={{0,7},{1,0},{2,1},{3,2},{4,3},{5,4},{6,5},{7,6},{8,9},{9,10},{10,1... | collective-permute-start | bytes 688136 | tf_op jit(solution)/shard_map/ppermute | solution.py:178
  23.2 2.1 %collective-permute-done.1.refs_2_ = bf16[16,7168]{1,0:T(8,128)(2,1)S(1)} collective-permute-done((bf16[16,7168]{1,0:T(8,128)(2,1)S(1)}, bf16[16,7168]{1,0:T(8,128)(2,1)S(1)}, u32[]{:S(2)}, u32[]{:S(2)}) %collective-permute-start.1) | collective-permute-done | bytes 229408 | tf_op jit(solution)/shard_map/ppermute | solution.py:178
  25.3 2.9 %collective-permute-start.2 = (bf16[16,7168]{1,0:T(8,128)(2,1)S(1)}, bf16[16,7168]{1,0:T(8,128)(2,1)S(1)}, u32[]{:S(2)}, u32[]{:S(2)}) collective-permute-start(bf16[16,7168]{1,0:T(8,128)(2,1)S(1)} %collective-permute-done.1.refs_2_), channel_id=1, source_target_pairs={{0,1},{1,2},{2,3},{3,4},{4,5},{5,6},{6,7},{7,0},{8,15},{9,8},{10,9... | collective-permute-start | bytes 688136 | tf_op jit(solution)/shard_map/ppermute | solution.py:178
  28.2 0.0 collective-permute-done.4.refs_4_
  28.2 4.1 %collective-permute-start.5 = (bf16[16,7168]{1,0:T(8,128)(2,1)S(1)}, bf16[16,7168]{1,0:T(8,128)(2,1)S(1)}, u32[]{:S(2)}, u32[]{:S(2)}) collective-permute-start(bf16[16,7168]{1,0:T(8,128)(2,1)S(1)} %collective-permute-done.4.refs_4_), channel_id=1, source_target_pairs={{0,7},{1,0},{2,1},{3,2},{4,3},{5,4},{6,5},{7,6},{8,9},{9,10},{10,1... | collective-permute-start | bytes 688136 | tf_op jit(solution)/shard_map/ppermute | solution.py:178
  32.4 2.2 %collective-permute-done.2.refs_1_ = bf16[16,7168]{1,0:T(8,128)(2,1)S(1)} collective-permute-done((bf16[16,7168]{1,0:T(8,128)(2,1)S(1)}, bf16[16,7168]{1,0:T(8,128)(2,1)S(1)}, u32[]{:S(2)}, u32[]{:S(2)}) %collective-permute-start.2) | collective-permute-done | bytes 229408 | tf_op jit(solution)/shard_map/ppermute | solution.py:178
  34.6 3.8 %collective-permute-start.3 = (bf16[16,7168]{1,0:T(8,128)(2,1)S(1)}, bf16[16,7168]{1,0:T(8,128)(2,1)S(1)}, u32[]{:S(2)}, u32[]{:S(2)}) collective-permute-start(bf16[16,7168]{1,0:T(8,128)(2,1)S(1)} %collective-permute-done.2.refs_1_), channel_id=1, source_target_pairs={{0,1},{1,2},{2,3},{3,4},{4,5},{5,6},{6,7},{7,0},{8,15},{9,8},{10,9... | collective-permute-start | bytes 688136 | tf_op jit(solution)/shard_map/ppermute | solution.py:178
  38.4 0.0 collective-permute-done.5.refs_5_
  38.4 3.4 %collective-permute-start.6 = (bf16[16,7168]{1,0:T(8,128)(2,1)S(1)}, bf16[16,7168]{1,0:T(8,128)(2,1)S(1)}, u32[]{:S(2)}, u32[]{:S(2)}) collective-permute-start(bf16[16,7168]{1,0:T(8,128)(2,1)S(1)} %collective-permute-done.5.refs_5_), channel_id=1, source_target_pairs={{0,7},{1,0},{2,1},{3,2},{4,3},{5,4},{6,5},{7,6},{8,9},{9,10},{10,1... | collective-permute-start | bytes 688136 | tf_op jit(solution)/shard_map/ppermute | solution.py:178
  41.8 3.5 %collective-permute-done.3.refs_0_ = bf16[16,7168]{1,0:T(8,128)(2,1)S(1)} collective-permute-done((bf16[16,7168]{1,0:T(8,128)(2,1)S(1)}, bf16[16,7168]{1,0:T(8,128)(2,1)S(1)}, u32[]{:S(2)}, u32[]{:S(2)}) %collective-permute-start.3) | collective-permute-done | bytes 229408 | tf_op jit(solution)/shard_map/ppermute | solution.py:178
  45.2 3.0 %collective-permute-start.7 = (bf16[16,7168]{1,0:T(8,128)(2,1)S(1)}, bf16[16,7168]{1,0:T(8,128)(2,1)S(1)}, u32[]{:S(2)}, u32[]{:S(2)}) collective-permute-start(bf16[16,7168]{1,0:T(8,128)(2,1)S(1)} %collective-permute-done.3.refs_0_), channel_id=1, source_target_pairs={{0,1},{1,2},{2,3},{3,4},{4,5},{5,6},{6,7},{7,0},{8,15},{9,8},{10,9... | collective-permute-start | bytes 688136 | tf_op jit(solution)/shard_map/ppermute | solution.py:178
  48.3 4.3 %collective-permute-start = (f32[16,96]{1,0:T(8,128)S(1)}, f32[16,96]{1,0:T(8,128)S(1)}, u32[]{:S(2)}, u32[]{:S(2)}) collective-permute-start(f32[16,96]{1,0:T(8,128)S(1)} %get-tuple-element.15), channel_id=1, source_target_pairs={{0,64},{1,65},{2,66},{3,67},{4,68},{5,69},{6,70},{7,71},{8,72},{9,... | collective-permute-start | bytes 18440 | tf_op jit(solution)/shard_map/ppermute | solution.py:178
  52.6 10.8 %collective-permute-done.refs_11_.weights_ref = f32[16,96]{1,0:T(8,128)S(1)} collective-permute-done((f32[16,96]{1,0:T(8,128)S(1)}, f32[16,96]{1,0:T(8,128)S(1)}, u32[]{:S(2)}, u32[]{:S(2)}) %collective-permute-start) | collective-permute-done | bytes 6176 | tf_op jit(solution)/shard_map/ppermute | solution.py:178
  63.4 0.0 collective-permute-done.6.refs_6_
  63.4 0.0 collective-permute-done.7.refs_7_
  63.4 0.0 copy-done
  63.4 0.0 copy-start.1
  63.4 1.5 %copy-done.1 = bf16[1,7168,128]{2,1,0:T(8,128)(2,1)S(1)} copy-done((bf16[1,7168,128]{2,1,0:T(8,128)(2,1)S(1)}, bf16[1,7168,128]{2,1,0:T(8,128)(2,1)}, u32[]{:S(2)}) %copy-start.1) | copy-done | bytes 1835032
  64.9 0.0 copy-start.2
  64.9 1.5 %copy-done.2 = bf16[1,128,7168]{2,1,0:T(8,128)(2,1)S(1)} copy-done((bf16[1,128,7168]{2,1,0:T(8,128)(2,1)S(1)}, bf16[1,128,7168]{2,1,0:T(8,128)(2,1)}, u32[]{:S(2)}) %copy-start.2) | copy-done | bytes 1835032
  66.4 1.7 %experts.1 = (bf16[16,7168]{1,0:T(8,128)(2,1)S(1)}, bf16[16,7168]{1,0:T(8,128)(2,1)S(1)}, bf16[16,7168]{1,0:T(8,128)(2,1)S(1)}, bf16[16,7168]{1,0:T(8,128)(2,1)S...) custom-call(bf16[16,7168]{1,0:T(8,128)(2,1)S(1)} %collective-permute, ...), custom_call_target="tpu_custom_call" | custom-call | flops 704643072 | bytes 5505024 | tf_op jit(solution)/shard_map/experts/pallas_call | solution.py:102
  68.1 1.9 %collective-permute-start.12 = (bf16[16,7168]{1,0:T(8,128)(2,1)S(1)}, bf16[16,7168]{1,0:T(8,128)(2,1)S(1)}, u32[]{:S(2)}, u32[]{:S(2)}) collective-permute-start(bf16[16,7168]{1,0:T(8,128)(2,1)S(1)} %get-tuple-element.24), channel_id=1, source_target_pairs={{0,1},{1,2},{2,3},{3,4},{4,5},{5,6},{6,7},{7,0},{8,15},{9,8},{10,9... | collective-permute-start | bytes 688136 | tf_op jit(solution)/shard_map/ppermute | solution.py:178
  70.0 5.2 %collective-permute-start.9 = (bf16[16,7168]{1,0:T(8,128)(2,1)S(1)}, bf16[16,7168]{1,0:T(8,128)(2,1)S(1)}, u32[]{:S(2)}, u32[]{:S(2)}) collective-permute-start(bf16[16,7168]{1,0:T(8,128)(2,1)S(1)} %get-tuple-element.20), channel_id=1, source_target_pairs={{0,7},{1,0},{2,1},{3,2},{4,3},{5,4},{6,5},{7,6},{8,9},{9,10},{10,1... | collective-permute-start | bytes 688136 | tf_op jit(solution)/shard_map/ppermute | solution.py:178
  75.2 2.1 %collective-permute-done.12.refs_1_ = bf16[16,7168]{1,0:T(8,128)(2,1)S(1)} collective-permute-done((bf16[16,7168]{1,0:T(8,128)(2,1)S(1)}, bf16[16,7168]{1,0:T(8,128)(2,1)S(1)}, u32[]{:S(2)}, u32[]{:S(2)}) %collective-permute-start.12) | collective-permute-done | bytes 229408 | tf_op jit(solution)/shard_map/ppermute | solution.py:178
  77.3 0.1 plus.8
  77.3 1.9 %collective-permute-start.13 = (bf16[16,7168]{1,0:T(8,128)(2,1)S(1)}, bf16[16,7168]{1,0:T(8,128)(2,1)S(1)}, u32[]{:S(2)}, u32[]{:S(2)}) collective-permute-start(bf16[16,7168]{1,0:T(8,128)(2,1)S(1)} %plus.8), channel_id=1, source_target_pairs={{0,1},{1,2},{2,3},{3,4},{4,5},{5,6},{6,7},{7,0},{8,15},{9,8},{10,9... | collective-permute-start | bytes 688136 | tf_op jit(solution)/shard_map/ppermute | solution.py:178
  79.3 0.0 collective-permute-done.9.refs_1_
  79.3 0.1 plus.6
  79.3 5.8 %collective-permute-start.10 = (bf16[16,7168]{1,0:T(8,128)(2,1)S(1)}, bf16[16,7168]{1,0:T(8,128)(2,1)S(1)}, u32[]{:S(2)}, u32[]{:S(2)}) collective-permute-start(bf16[16,7168]{1,0:T(8,128)(2,1)S(1)} %plus.6), channel_id=1, source_target_pairs={{0,7},{1,0},{2,1},{3,2},{4,3},{5,4},{6,5},{7,6},{8,9},{9,10},{10,1... | collective-permute-start | bytes 688136 | tf_op jit(solution)/shard_map/ppermute | solution.py:178
  85.2 1.9 %collective-permute-start.8 = (bf16[16,7168]{1,0:T(8,128)(2,1)S(1)}, bf16[16,7168]{1,0:T(8,128)(2,1)S(1)}, u32[]{:S(2)}, u32[]{:S(2)}) collective-permute-start(bf16[16,7168]{1,0:T(8,128)(2,1)S(1)} %get-tuple-element.17), channel_id=1, source_target_pairs={{0,64},{1,65},{2,66},{3,67},{4,68},{5,69},{6,70},{7,71},{8,72},{9,... | collective-permute-start | bytes 688136 | tf_op jit(solution)/shard_map/ppermute | solution.py:178
  87.1 2.5 %collective-permute-done.13.refs_1_ = bf16[16,7168]{1,0:T(8,128)(2,1)S(1)} collective-permute-done((bf16[16,7168]{1,0:T(8,128)(2,1)S(1)}, bf16[16,7168]{1,0:T(8,128)(2,1)S(1)}, u32[]{:S(2)}, u32[]{:S(2)}) %collective-permute-start.13) | collective-permute-done | bytes 229408 | tf_op jit(solution)/shard_map/ppermute | solution.py:178
  89.6 0.1 plus.9
  89.7 1.9 %collective-permute-start.14 = (bf16[16,7168]{1,0:T(8,128)(2,1)S(1)}, bf16[16,7168]{1,0:T(8,128)(2,1)S(1)}, u32[]{:S(2)}, u32[]{:S(2)}) collective-permute-start(bf16[16,7168]{1,0:T(8,128)(2,1)S(1)} %plus.9), channel_id=1, source_target_pairs={{0,1},{1,2},{2,3},{3,4},{4,5},{5,6},{6,7},{7,0},{8,15},{9,8},{10,9... | collective-permute-start | bytes 688136 | tf_op jit(solution)/shard_map/ppermute | solution.py:178
  91.6 0.0 collective-permute-done.10.refs_1_
  91.6 0.1 plus.7
  91.7 1.9 %collective-permute-start.11 = (bf16[16,7168]{1,0:T(8,128)(2,1)S(1)}, bf16[16,7168]{1,0:T(8,128)(2,1)S(1)}, u32[]{:S(2)}, u32[]{:S(2)}) collective-permute-start(bf16[16,7168]{1,0:T(8,128)(2,1)S(1)} %plus.7), channel_id=1, source_target_pairs={{0,71},{1,64},{2,65},{3,66},{4,67},{5,68},{6,69},{7,70},{8,73},{9,... | collective-permute-start | bytes 688136 | tf_op jit(solution)/shard_map/ppermute | solution.py:178
  93.6 1.6 %collective-permute-done.8.r_2_.refs_0_ = bf16[16,7168]{1,0:T(8,128)(2,1)S(1)} collective-permute-done((bf16[16,7168]{1,0:T(8,128)(2,1)S(1)}, bf16[16,7168]{1,0:T(8,128)(2,1)S(1)}, u32[]{:S(2)}, u32[]{:S(2)}) %collective-permute-start.8) | collective-permute-done | bytes 229408 | tf_op jit(solution)/shard_map/ppermute | solution.py:178
  95.3 3.5 %collective-permute-done.14.r_1_ = bf16[16,7168]{1,0:T(8,128)(2,1)S(1)} collective-permute-done((bf16[16,7168]{1,0:T(8,128)(2,1)S(1)}, bf16[16,7168]{1,0:T(8,128)(2,1)S(1)}, u32[]{:S(2)}, u32[]{:S(2)}) %collective-permute-start.14) | collective-permute-done | bytes 229408 | tf_op jit(solution)/shard_map/ppermute | solution.py:178
  98.8 0.1 plus.10
  98.9 1.9 %collective-permute-start.15 = (bf16[16,7168]{1,0:T(8,128)(2,1)S(1)}, bf16[16,7168]{1,0:T(8,128)(2,1)S(1)}, u32[]{:S(2)}, u32[]{:S(2)}) collective-permute-start(bf16[16,7168]{1,0:T(8,128)(2,1)S(1)} %plus.10), channel_id=1, source_target_pairs={{0,65},{1,66},{2,67},{3,68},{4,69},{5,70},{6,71},{7,64},{8,79},{9,... | collective-permute-start | bytes 688136 | tf_op jit(solution)/shard_map/ppermute | solution.py:178
  100.8 0.0 collective-permute-done.11.refs_1_
  100.8 8.1 %collective-permute-done.15.refs_2_ = bf16[16,7168]{1,0:T(8,128)(2,1)S(1)} collective-permute-done((bf16[16,7168]{1,0:T(8,128)(2,1)S(1)}, bf16[16,7168]{1,0:T(8,128)(2,1)S(1)}, u32[]{:S(2)}, u32[]{:S(2)}) %collective-permute-start.15) | collective-permute-done | bytes 229408 | tf_op jit(solution)/shard_map/ppermute | solution.py:178
  108.9 0.1 plus.11
  109.0 0.1 reshape.14
  109.1 9.6 %all_to_all.11 = bf16[8,2,7168]{2,1,0:T(2,128)(2,1)S(1)} all-to-all(bf16[8,2,7168]{2,1,0:T(2,128)(2,1)S(1)} %reshape.14), channel_id=1, replica_groups=mesh['section'=16,'node'=8,'local'=8] {'node'}, dimensions={0} | all-to-all | bytes 458752 | tf_op jit(solution)/shard_map/all_to_all | solution.py:209
  118.6 0.1 reshape.15.rows_ref
  118.7 2.4 %combine_rows.1 = bf16[96,7168]{1,0:T(8,128)(2,1)} custom-call(f32[16,96]{1,0:T(8,128)S(1)} %collective-permute-done.refs_11_.weights_ref, bf16[16,7168]{1,0:T(8,128)(2,1)S(1)} %reshape.15.rows_ref), custom_call_target="tpu_custom_call" | custom-call | flops 66060288 | bytes 1605632 | tf_op jit(solution)/shard_map/combine_rows/pallas_call | solution.py:152
Async XLA Ops:
  0.0 63.4 %copy-start = (bf16[1,7168,128]{2,1,0:T(8,128)(2,1)S(1)}, bf16[1,7168,128]{2,1,0:T(8,128)(2,1)}, u32[]{:S(2)}) copy-start(bf16[1,7168,128]{2,1,0:T(8,128)(2,1)} %param.11) | copy-start | bytes 5505028
  0.0 1.5 %copy-start.3 = (bf16[1,96,7168]{2,1,0:T(8,128)(2,1)S(1)}, bf16[1,96,7168]{2,1,0:T(8,128)(2,1)}, u32[]{:S(2)}) copy-start(bf16[1,96,7168]{2,1,0:T(8,128)(2,1)} %param.7) | copy-start | bytes 4128772
  1.5 0.7 copy-start.4
  2.2 0.7 copy-start.5
  2.9 0.7 copy-start.6
  15.9 9.4 %collective-permute-start.1 = (bf16[16,7168]{1,0:T(8,128)(2,1)S(1)}, bf16[16,7168]{1,0:T(8,128)(2,1)S(1)}, u32[]{:S(2)}, u32[]{:S(2)}) collective-permute-start(bf16[16,7168]{1,0:T(8,128)(2,1)S(1)} %reshape.13.refs_3_), channel_id=1, source_target_pairs={{0,1},{1,2},{2,3},{3,4},{4,5},{5,6},{6,7},{7,0},{8,15},{9,8},{10,9... | collective-permute-start | bytes 688136 | tf_op jit(solution)/shard_map/ppermute | solution.py:178
  19.4 8.8 %collective-permute-start.4 = (bf16[16,7168]{1,0:T(8,128)(2,1)S(1)}, bf16[16,7168]{1,0:T(8,128)(2,1)S(1)}, u32[]{:S(2)}, u32[]{:S(2)}) collective-permute-start(bf16[16,7168]{1,0:T(8,128)(2,1)S(1)} %reshape.13.refs_3_), channel_id=1, source_target_pairs={{0,7},{1,0},{2,1},{3,2},{4,3},{5,4},{6,5},{7,6},{8,9},{9,10},{10,1... | collective-permute-start | bytes 688136 | tf_op jit(solution)/shard_map/ppermute | solution.py:178
  25.3 9.3 %collective-permute-start.2 = (bf16[16,7168]{1,0:T(8,128)(2,1)S(1)}, bf16[16,7168]{1,0:T(8,128)(2,1)S(1)}, u32[]{:S(2)}, u32[]{:S(2)}) collective-permute-start(bf16[16,7168]{1,0:T(8,128)(2,1)S(1)} %collective-permute-done.1.refs_2_), channel_id=1, source_target_pairs={{0,1},{1,2},{2,3},{3,4},{4,5},{5,6},{6,7},{7,0},{8,15},{9,8},{10,9... | collective-permute-start | bytes 688136 | tf_op jit(solution)/shard_map/ppermute | solution.py:178
  28.2 10.1 %collective-permute-start.5 = (bf16[16,7168]{1,0:T(8,128)(2,1)S(1)}, bf16[16,7168]{1,0:T(8,128)(2,1)S(1)}, u32[]{:S(2)}, u32[]{:S(2)}) collective-permute-start(bf16[16,7168]{1,0:T(8,128)(2,1)S(1)} %collective-permute-done.4.refs_4_), channel_id=1, source_target_pairs={{0,7},{1,0},{2,1},{3,2},{4,3},{5,4},{6,5},{7,6},{8,9},{9,10},{10,1... | collective-permute-start | bytes 688136 | tf_op jit(solution)/shard_map/ppermute | solution.py:178
  34.6 10.6 %collective-permute-start.3 = (bf16[16,7168]{1,0:T(8,128)(2,1)S(1)}, bf16[16,7168]{1,0:T(8,128)(2,1)S(1)}, u32[]{:S(2)}, u32[]{:S(2)}) collective-permute-start(bf16[16,7168]{1,0:T(8,128)(2,1)S(1)} %collective-permute-done.2.refs_1_), channel_id=1, source_target_pairs={{0,1},{1,2},{2,3},{3,4},{4,5},{5,6},{6,7},{7,0},{8,15},{9,8},{10,9... | collective-permute-start | bytes 688136 | tf_op jit(solution)/shard_map/ppermute | solution.py:178
  38.4 25.0 %collective-permute-start.6 = (bf16[16,7168]{1,0:T(8,128)(2,1)S(1)}, bf16[16,7168]{1,0:T(8,128)(2,1)S(1)}, u32[]{:S(2)}, u32[]{:S(2)}) collective-permute-start(bf16[16,7168]{1,0:T(8,128)(2,1)S(1)} %collective-permute-done.5.refs_5_), channel_id=1, source_target_pairs={{0,7},{1,0},{2,1},{3,2},{4,3},{5,4},{6,5},{7,6},{8,9},{9,10},{10,1... | collective-permute-start | bytes 688136 | tf_op jit(solution)/shard_map/ppermute | solution.py:178
  45.2 18.1 %collective-permute-start.7 = (bf16[16,7168]{1,0:T(8,128)(2,1)S(1)}, bf16[16,7168]{1,0:T(8,128)(2,1)S(1)}, u32[]{:S(2)}, u32[]{:S(2)}) collective-permute-start(bf16[16,7168]{1,0:T(8,128)(2,1)S(1)} %collective-permute-done.3.refs_0_), channel_id=1, source_target_pairs={{0,1},{1,2},{2,3},{3,4},{4,5},{5,6},{6,7},{7,0},{8,15},{9,8},{10,9... | collective-permute-start | bytes 688136 | tf_op jit(solution)/shard_map/ppermute | solution.py:178
  48.3 15.1 %collective-permute-start = (f32[16,96]{1,0:T(8,128)S(1)}, f32[16,96]{1,0:T(8,128)S(1)}, u32[]{:S(2)}, u32[]{:S(2)}) collective-permute-start(f32[16,96]{1,0:T(8,128)S(1)} %get-tuple-element.15), channel_id=1, source_target_pairs={{0,64},{1,65},{2,66},{3,67},{4,68},{5,69},{6,70},{7,71},{8,72},{9,... | collective-permute-start | bytes 18440 | tf_op jit(solution)/shard_map/ppermute | solution.py:178
  63.4 1.5 %copy-start.1 = (bf16[1,7168,128]{2,1,0:T(8,128)(2,1)S(1)}, bf16[1,7168,128]{2,1,0:T(8,128)(2,1)}, u32[]{:S(2)}) copy-start(bf16[1,7168,128]{2,1,0:T(8,128)(2,1)} %param.12) | copy-start | bytes 5505028
  64.9 1.5 %copy-start.2 = (bf16[1,128,7168]{2,1,0:T(8,128)(2,1)S(1)}, bf16[1,128,7168]{2,1,0:T(8,128)(2,1)}, u32[]{:S(2)}) copy-start(bf16[1,128,7168]{2,1,0:T(8,128)(2,1)} %param.13) | copy-start | bytes 5505028
  68.1 9.2 %collective-permute-start.12 = (bf16[16,7168]{1,0:T(8,128)(2,1)S(1)}, bf16[16,7168]{1,0:T(8,128)(2,1)S(1)}, u32[]{:S(2)}, u32[]{:S(2)}) collective-permute-start(bf16[16,7168]{1,0:T(8,128)(2,1)S(1)} %get-tuple-element.24), channel_id=1, source_target_pairs={{0,1},{1,2},{2,3},{3,4},{4,5},{5,6},{6,7},{7,0},{8,15},{9,8},{10,9... | collective-permute-start | bytes 688136 | tf_op jit(solution)/shard_map/ppermute | solution.py:178
  70.0 9.2 %collective-permute-start.9 = (bf16[16,7168]{1,0:T(8,128)(2,1)S(1)}, bf16[16,7168]{1,0:T(8,128)(2,1)S(1)}, u32[]{:S(2)}, u32[]{:S(2)}) collective-permute-start(bf16[16,7168]{1,0:T(8,128)(2,1)S(1)} %get-tuple-element.20), channel_id=1, source_target_pairs={{0,7},{1,0},{2,1},{3,2},{4,3},{5,4},{6,5},{7,6},{8,9},{9,10},{10,1... | collective-permute-start | bytes 688136 | tf_op jit(solution)/shard_map/ppermute | solution.py:178
  77.3 12.3 %collective-permute-start.13 = (bf16[16,7168]{1,0:T(8,128)(2,1)S(1)}, bf16[16,7168]{1,0:T(8,128)(2,1)S(1)}, u32[]{:S(2)}, u32[]{:S(2)}) collective-permute-start(bf16[16,7168]{1,0:T(8,128)(2,1)S(1)} %plus.8), channel_id=1, source_target_pairs={{0,1},{1,2},{2,3},{3,4},{4,5},{5,6},{6,7},{7,0},{8,15},{9,8},{10,9... | collective-permute-start | bytes 688136 | tf_op jit(solution)/shard_map/ppermute | solution.py:178
  79.3 12.3 %collective-permute-start.10 = (bf16[16,7168]{1,0:T(8,128)(2,1)S(1)}, bf16[16,7168]{1,0:T(8,128)(2,1)S(1)}, u32[]{:S(2)}, u32[]{:S(2)}) collective-permute-start(bf16[16,7168]{1,0:T(8,128)(2,1)S(1)} %plus.6), channel_id=1, source_target_pairs={{0,7},{1,0},{2,1},{3,2},{4,3},{5,4},{6,5},{7,6},{8,9},{9,10},{10,1... | collective-permute-start | bytes 688136 | tf_op jit(solution)/shard_map/ppermute | solution.py:178
  85.2 10.1 %collective-permute-start.8 = (bf16[16,7168]{1,0:T(8,128)(2,1)S(1)}, bf16[16,7168]{1,0:T(8,128)(2,1)S(1)}, u32[]{:S(2)}, u32[]{:S(2)}) collective-permute-start(bf16[16,7168]{1,0:T(8,128)(2,1)S(1)} %get-tuple-element.17), channel_id=1, source_target_pairs={{0,64},{1,65},{2,66},{3,67},{4,68},{5,69},{6,70},{7,71},{8,72},{9,... | collective-permute-start | bytes 688136 | tf_op jit(solution)/shard_map/ppermute | solution.py:178
  89.7 9.1 %collective-permute-start.14 = (bf16[16,7168]{1,0:T(8,128)(2,1)S(1)}, bf16[16,7168]{1,0:T(8,128)(2,1)S(1)}, u32[]{:S(2)}, u32[]{:S(2)}) collective-permute-start(bf16[16,7168]{1,0:T(8,128)(2,1)S(1)} %plus.9), channel_id=1, source_target_pairs={{0,1},{1,2},{2,3},{3,4},{4,5},{5,6},{6,7},{7,0},{8,15},{9,8},{10,9... | collective-permute-start | bytes 688136 | tf_op jit(solution)/shard_map/ppermute | solution.py:178
  91.7 9.1 %collective-permute-start.11 = (bf16[16,7168]{1,0:T(8,128)(2,1)S(1)}, bf16[16,7168]{1,0:T(8,128)(2,1)S(1)}, u32[]{:S(2)}, u32[]{:S(2)}) collective-permute-start(bf16[16,7168]{1,0:T(8,128)(2,1)S(1)} %plus.7), channel_id=1, source_target_pairs={{0,71},{1,64},{2,65},{3,66},{4,67},{5,68},{6,69},{7,70},{8,73},{9,... | collective-permute-start | bytes 688136 | tf_op jit(solution)/shard_map/ppermute | solution.py:178
  98.9 10.0 %collective-permute-start.15 = (bf16[16,7168]{1,0:T(8,128)(2,1)S(1)}, bf16[16,7168]{1,0:T(8,128)(2,1)S(1)}, u32[]{:S(2)}, u32[]{:S(2)}) collective-permute-start(bf16[16,7168]{1,0:T(8,128)(2,1)S(1)} %plus.10), channel_id=1, source_target_pairs={{0,65},{1,66},{2,67},{3,68},{4,69},{5,70},{6,71},{7,64},{8,79},{9,... | collective-permute-start | bytes 688136 | tf_op jit(solution)/shard_map/ppermute | solution.py:178

commit v3 on v2

--- a/solution.py
+++ b/solution.py
@@ -7,8 +7,10 @@
 
 CAP = 2
 COLUMNS = 896
+PIECE = 1792
 VMEM = pl.BlockSpec(memory_space=pltpu.VMEM)
 ANY = pl.BlockSpec(memory_space=pl.ANY)
+HBM = pl.BlockSpec(memory_space=pltpu.HBM)
 
 
 def grant(mib):
@@ -19,10 +21,27 @@
     return pl.CostEstimate(flops=flops, bytes_accessed=moved, transcendentals=0)
 
 
-def pick_kernel(table_ref, routes_ref, gates_ref, tokens_ref, rows_ref, combine_ref):
+def pick_kernel(
+    table_ref, routes_hbm, gates_hbm, tokens_hbm, rows_ref, combine_ref, routes_ref, gates_ref, tokens_ref, arrived
+):
     slots = table_ref.shape[0]
     rows_dev = rows_ref.shape[0]
-    tok_dev = tokens_ref.shape[0]
+    tok_dev, width = tokens_ref.shape
+    starts = range(0, width, PIECE)
+    small = [
+        pltpu.make_async_copy(routes_hbm, routes_ref, arrived.at[0]),
+        pltpu.make_async_copy(gates_hbm, gates_ref, arrived.at[1]),
+    ]
+    pieces = []
+    for k, c in enumerate(starts):
+        cols = pl.ds(c, min(PIECE, width - c))
+        pieces.append(
+            pltpu.make_async_copy(tokens_hbm.at[:, cols], tokens_ref.at[:, cols], arrived.at[2 + k])
+        )
+    for copy in small + pieces:
+        copy.start()
+    for copy in small:
+        copy.wait()
     picks = routes_ref[...]
     gates = gates_ref[...]
     row_slot = lax.broadcasted_iota(jnp.int32, (rows_dev, tok_dev), 0) // CAP
@@ -53,9 +72,12 @@
     chosen = (named > 0.0) & (rank == want.astype(jnp.float32))
     combine_ref[...] = jnp.where(chosen, weight, 0.0)
     select = jnp.where(chosen, 1.0, 0.0).astype(jnp.bfloat16)
-    rows_ref[...] = jnp.dot(select, tokens_ref[...], preferred_element_type=jnp.float32).astype(
-        jnp.bfloat16
-    )
+    for copy, c in zip(pieces, starts):
+        copy.wait()
+        cols = slice(c, min(c + PIECE, width))
+        rows_ref[:, cols] = jnp.dot(
+            select, tokens_ref[:, cols], preferred_element_type=jnp.float32
+        ).astype(jnp.bfloat16)
 
 
 def pick_rows(table, picks, gates, tokens, rows_dev):
@@ -66,16 +88,47 @@
             jax.ShapeDtypeStruct((rows_dev, width), jnp.bfloat16),
             jax.ShapeDtypeStruct((rows_dev, tok_dev), jnp.float32),
         ),
-        in_specs=[pl.BlockSpec(memory_space=pltpu.SMEM), VMEM, VMEM, VMEM],
+        in_specs=[pl.BlockSpec(memory_space=pltpu.SMEM), HBM, HBM, HBM],
         out_specs=(VMEM, VMEM),
-        compiler_params=grant(8),
+        scratch_shapes=[
+            pltpu.VMEM(picks.shape, picks.dtype),
+            pltpu.VMEM(gates.shape, gates.dtype),
+            pltpu.VMEM(tokens.shape, tokens.dtype),
+            pltpu.SemaphoreType.DMA((2 + -(-width // PIECE),)),
+        ],
         cost_estimate=cost(2 * rows_dev * tok_dev * width, 2 * (tok_dev + rows_dev) * width),
         name="pick_rows",
     )(table, picks, gates, tokens)
 
 
+def load_kernel(n, *refs):
+    sources, targets, arrived = refs[:n], refs[n + 1 : 2 * n + 1], refs[2 * n + 1]
+    copies = [
+        pltpu.make_async_copy(source, target, arrived.at[k])
+        for k, (source, target) in enumerate(zip(sources, targets))
+    ]
+    for copy in copies:
+        copy.start()
+    for copy in copies:
+        copy.wait()
+
+
+def load(arrays, after):
+    n = len(arrays)
+    return pl.pallas_call(
+        lambda *refs: load_kernel(n, *refs),
+        out_shape=[jax.ShapeDtypeStruct(a.shape, a.dtype) for a in arrays],
+        in_specs=[HBM] * n + [ANY],
+        out_specs=[VMEM] * n,
+        scratch_shapes=[pltpu.SemaphoreType.DMA((n,))],
+        compiler_params=grant(16),
+        cost_estimate=cost(1_000_000_000, sum(2 * a.size * a.dtype.itemsize for a in arrays)),
+        name="load",
+    )(*arrays, after)
+
+
 def experts_kernel(n, *refs):
-    blocks, (gate_ref, up_ref, down_ref), outs = refs[:n], refs[n : n + 3], refs[n + 4 :]
+    blocks, (gate_ref, up_ref, down_ref), outs = refs[:n], refs[n : n + 3], refs[n + 3 :]
     rows_dev, width = blocks[0].shape
     hid = gate_ref.shape[1]
     gate_proj = jnp.zeros((n * rows_dev, hid), jnp.float32)
@@ -95,19 +148,19 @@
             outs[k][:, cols] = part[k * rows_dev : (k + 1) * rows_dev]
 
 
-def experts(blocks, w_gate, w_up, w_down, after):
+def experts(blocks, w_gate, w_up, w_down):
     n = len(blocks)
     rows_dev, width = blocks[0].shape
     hid = w_gate.shape[1]
     return pl.pallas_call(
         lambda *refs: experts_kernel(n, *refs),
         out_shape=[jax.ShapeDtypeStruct((rows_dev, width), jnp.bfloat16)] * n,
-        in_specs=[VMEM] * (n + 3) + [ANY],
+        in_specs=[VMEM] * (n + 3),
         out_specs=[VMEM] * n,
         compiler_params=grant(24),
         cost_estimate=cost(6 * n * rows_dev * width * hid, 6 * width * hid),
         name="experts",
-    )(*blocks, w_gate, w_up, w_down, after)
+    )(*blocks, w_gate, w_up, w_down)
 
 
 def plus_kernel(*refs):
@@ -189,13 +242,14 @@
         outgoing.reshape(n_node, CAP, width), "node", split_axis=0, concat_axis=0, tiled=True
     ).reshape(rows_dev, width)
     blocks = {0: own}
-    ahead, back = own, own
-    for q in range(1, far):
-        ahead, back = hop(ahead, 1), hop(back, -1)
-        blocks[-q], blocks[q] = ahead, back
-    blocks[far] = hop(ahead, 1)
+    for q in range(2, 0, -1):
+        blocks[-q], blocks[q] = hop(own, q), hop(own, -q)
+    for q in range(3, far):
+        blocks[-q], blocks[q] = hop(blocks[2 - q], 2), hop(blocks[q - 2], -2)
+    blocks[far] = hop(blocks[2 - far], 2)
     order = sorted(blocks)
-    parts = experts([blocks[q] for q in order], w_gate[0], w_up[0], w_down[0], weights)
+    up_mat, down_mat = load([w_up[0], w_down[0]], weights)
+    parts = experts([blocks[q] for q in order], w_gate[0], up_mat, down_mat)
     part = dict(zip(order, parts))
     mine = hop(part[0], 0, 1)
     ahead, back = hop(part[far], 1), hop(part[1 - far], -1)

time: 122 us -> 113 us (0.926)
  the two profiles are of different devices: /device:TPU:64 before, /device:TPU:216 now
where the time goes in v3:
time: 113 us; the launch traced here: 112 us
  starting transfers between devices  66.7 us (59%)
  blocking collectives  20.8 us (18%)
  waiting for transfers between devices  13.5 us (12%)
  Pallas kernels  7.96 us (7%)
  local copies, waits for them, and re-layouts  2.8 us (2%)
    ppermute x16, starting transfers between devices, hop(): return lax.ppermute(block, ('section', 'node', 'local'), pairs)  66.7 us
    ppermute x16, waiting for transfers between devices, hop(): return lax.ppermute(block, ('section', 'node', 'local'), pairs)  13.5 us
    all_to_all x1, blocking collectives, shards(): lax.all_to_all(outgoing.reshape(n_node, CAP, width), 'node', split_axis=0...  11.3 us
    all_to_all x1, blocking collectives, shards(): lax.all_to_all(expert_out.reshape(n_node, CAP, width), 'node', split_axis...  9.56 us
    pallas_call x1, Pallas kernels, pick_rows(): pl.pallas_call(pick_kernel, out_shape=(jax.ShapeDtypeStruct((rows_dev, wi...  3.24 us
    pallas_call x1, Pallas kernels, combine_rows(): pl.pallas_call(combine_kernel, grid=(4,), out_shape=jax.ShapeDtypeStruct(...  2.37 us
  transfers between devices with their start and end apart: 16, of which 6 were waited for; matrix products, arithmetic and copies ran while one was open for 0% of the time, Pallas kernels for 0%

profile of v3, /device:TPU:216, one launch (start us, length us, event | category | flops | bytes accessed | tf_op | source)
XLA Modules:
  0.0 112.1 jit_solution(12044170309057808269)
XLA Ops:
  0.0 0.0 copy-start.1
  0.0 3.2 %pick_rows.1 = (bf16[16,7168]{1,0:T(8,128)(2,1)}, f32[16,96]{1,0:T(8,128)}) custom-call(s32[8]{0:T(128)} %table_ref.1, s32[8,96]{1,0:T(8,128)} %bitcast.15, f32[8,96]{1,0:T(8,128)} %bitcast.16, bf16[96,7168]{1,0:T(8,128)(2,1)} %bitcast.14), custom_call_target="tpu_custom_call" | custom-call | flops 22020096 | bytes 1605632 | tf_op jit(solution)/shard_map/pick_rows/pallas_call | solution.py:85
  3.2 1.0 reshape.12
  4.3 11.3 %all_to_all.10 = bf16[8,2,7168]{2,1,0:T(2,128)(2,1)S(1)} all-to-all(bf16[8,2,7168]{2,1,0:T(2,128)(2,1)S(1)} %reshape.12), channel_id=1, replica_groups=mesh['section'=16,'node'=8,'local'=8] {'node'}, dimensions={0} | all-to-all | bytes 458752 | tf_op jit(solution)/shard_map/all_to_all | solution.py:241
  15.5 0.1 reshape.13.refs_3_
  15.6 2.4 %collective-permute-start.4 = (bf16[16,7168]{1,0:T(8,128)(2,1)S(1)}, bf16[16,7168]{1,0:T(8,128)(2,1)S(1)}, u32[]{:S(2)}, u32[]{:S(2)}) collective-permute-start(bf16[16,7168]{1,0:T(8,128)(2,1)S(1)} %reshape.13.refs_3_), channel_id=1, source_target_pairs={{0,7},{1,0},{2,1},{3,2},{4,3},{5,4},{6,5},{7,6},{8,9},{9,10},{10,1... | collective-permute-start | bytes 688136 | tf_op jit(solution)/shard_map/ppermute | solution.py:231
  18.0 5.7 %collective-permute-start.3 = (bf16[16,7168]{1,0:T(8,128)(2,1)S(1)}, bf16[16,7168]{1,0:T(8,128)(2,1)S(1)}, u32[]{:S(2)}, u32[]{:S(2)}) collective-permute-start(bf16[16,7168]{1,0:T(8,128)(2,1)S(1)} %reshape.13.refs_3_), channel_id=1, source_target_pairs={{0,2},{1,3},{2,4},{3,5},{4,6},{5,7},{6,0},{7,1},{8,14},{9,15},{10,... | collective-permute-start | bytes 688136 | tf_op jit(solution)/shard_map/ppermute | solution.py:231
  23.7 2.6 %collective-permute-start.1 = (bf16[16,7168]{1,0:T(8,128)(2,1)S(1)}, bf16[16,7168]{1,0:T(8,128)(2,1)S(1)}, u32[]{:S(2)}, u32[]{:S(2)}) collective-permute-start(bf16[16,7168]{1,0:T(8,128)(2,1)S(1)} %reshape.13.refs_3_), channel_id=1, source_target_pairs={{0,1},{1,2},{2,3},{3,4},{4,5},{5,6},{6,7},{7,0},{8,15},{9,8},{10,9... | collective-permute-start | bytes 688136 | tf_op jit(solution)/shard_map/ppermute | solution.py:231
  26.3 3.1 %collective-permute-start.5 = (bf16[16,7168]{1,0:T(8,128)(2,1)S(1)}, bf16[16,7168]{1,0:T(8,128)(2,1)S(1)}, u32[]{:S(2)}, u32[]{:S(2)}) collective-permute-start(bf16[16,7168]{1,0:T(8,128)(2,1)S(1)} %reshape.13.refs_3_), channel_id=1, source_target_pairs={{0,6},{1,7},{2,0},{3,1},{4,2},{5,3},{6,4},{7,5},{8,10},{9,11},{10,... | collective-permute-start | bytes 688136 | tf_op jit(solution)/shard_map/ppermute | solution.py:231
  29.4 0.0 collective-permute-done.4.refs_4_
  29.5 2.7 %collective-permute-start.6 = (bf16[16,7168]{1,0:T(8,128)(2,1)S(1)}, bf16[16,7168]{1,0:T(8,128)(2,1)S(1)}, u32[]{:S(2)}, u32[]{:S(2)}) collective-permute-start(bf16[16,7168]{1,0:T(8,128)(2,1)S(1)} %collective-permute-done.4.refs_4_), channel_id=1, source_target_pairs={{0,6},{1,7},{2,0},{3,1},{4,2},{5,3},{6,4},{7,5},{8,10},{9,11},{10,... | collective-permute-start | bytes 688136 | tf_op jit(solution)/shard_map/ppermute | solution.py:231
  32.2 0.0 collective-permute-done.3.refs_1_
  32.2 5.3 %collective-permute-start.7 = (bf16[16,7168]{1,0:T(8,128)(2,1)S(1)}, bf16[16,7168]{1,0:T(8,128)(2,1)S(1)}, u32[]{:S(2)}, u32[]{:S(2)}) collective-permute-start(bf16[16,7168]{1,0:T(8,128)(2,1)S(1)} %collective-permute-done.3.refs_1_), channel_id=1, source_target_pairs={{0,2},{1,3},{2,4},{3,5},{4,6},{5,7},{6,0},{7,1},{8,14},{9,15},{10,... | collective-permute-start | bytes 688136 | tf_op jit(solution)/shard_map/ppermute | solution.py:231
  37.4 0.3 collective-permute-done.1.refs_2_
  37.7 3.4 %collective-permute-start.2 = (bf16[16,7168]{1,0:T(8,128)(2,1)S(1)}, bf16[16,7168]{1,0:T(8,128)(2,1)S(1)}, u32[]{:S(2)}, u32[]{:S(2)}) collective-permute-start(bf16[16,7168]{1,0:T(8,128)(2,1)S(1)} %collective-permute-done.1.refs_2_), channel_id=1, source_target_pairs={{0,2},{1,3},{2,4},{3,5},{4,6},{5,7},{6,0},{7,1},{8,14},{9,15},{10,... | collective-permute-start | bytes 688136 | tf_op jit(solution)/shard_map/ppermute | solution.py:231
  41.1 5.5 %collective-permute-start = (f32[16,96]{1,0:T(8,128)}, f32[16,96]{1,0:T(8,128)S(1)}, u32[]{:S(2)}, u32[]{:S(2)}) collective-permute-start(f32[16,96]{1,0:T(8,128)} %get-tuple-element.17), channel_id=1, source_target_pairs={{0,64},{1,65},{2,66},{3,67},{4,68},{5,69},{6,70},{7,71},{8,72},{9,... | collective-permute-start | bytes 18440 | tf_op jit(solution)/shard_map/ppermute | solution.py:231
  46.6 1.6 %collective-permute-done.refs_2_.weights_ref = f32[16,96]{1,0:T(8,128)S(1)} collective-permute-done((f32[16,96]{1,0:T(8,128)}, f32[16,96]{1,0:T(8,128)S(1)}, u32[]{:S(2)}, u32[]{:S(2)}) %collective-permute-start) | collective-permute-done | bytes 6176 | tf_op jit(solution)/shard_map/ppermute | solution.py:231
  48.1 0.0 copy-done.1
  48.1 0.0 copy-start.2
  48.1 1.5 %copy-done.2 = bf16[1,128,7168]{2,1,0:T(8,128)(2,1)S(1)} copy-done((bf16[1,128,7168]{2,1,0:T(8,128)(2,1)S(1)}, bf16[1,128,7168]{2,1,0:T(8,128)(2,1)}, u32[]{:S(2)}) %copy-start.2) | copy-done | bytes 1835032
  49.6 0.0 copy-start
  49.6 0.3 load.1
  49.9 0.0 collective-permute-done.5.refs_5_
  49.9 0.0 collective-permute-done.6.refs_6_
  49.9 0.0 collective-permute-done.7.refs_7_
  49.9 1.8 %collective-permute-done.2.refs_0_ = bf16[16,7168]{1,0:T(8,128)(2,1)S(1)} collective-permute-done((bf16[16,7168]{1,0:T(8,128)(2,1)S(1)}, bf16[16,7168]{1,0:T(8,128)(2,1)S(1)}, u32[]{:S(2)}, u32[]{:S(2)}) %collective-permute-start.2) | collective-permute-done | bytes 229408 | tf_op jit(solution)/shard_map/ppermute | solution.py:231
  51.7 0.0 copy-done
  51.7 1.7 %experts.1 = (bf16[16,7168]{1,0:T(8,128)(2,1)S(1)}, bf16[16,7168]{1,0:T(8,128)(2,1)S(1)}, bf16[16,7168]{1,0:T(8,128)(2,1)S(1)}, bf16[16,7168]{1,0:T(8,128)(2,1)S...) custom-call(bf16[16,7168]{1,0:T(8,128)(2,1)S(1)} %collective-permute, ...), custom_call_target="tpu_custom_call" | custom-call | flops 704643072 | bytes 5505024 | tf_op jit(solution)/shard_map/experts/pallas_call | solution.py:155
  53.4 5.5 %collective-permute-start.12 = (bf16[16,7168]{1,0:T(8,128)(2,1)S(1)}, bf16[16,7168]{1,0:T(8,128)(2,1)S(1)}, u32[]{:S(2)}, u32[]{:S(2)}) collective-permute-start(bf16[16,7168]{1,0:T(8,128)(2,1)S(1)} %get-tuple-element.28), channel_id=1, source_target_pairs={{0,1},{1,2},{2,3},{3,4},{4,5},{5,6},{6,7},{7,0},{8,15},{9,8},{10,9... | collective-permute-start | bytes 688136 | tf_op jit(solution)/shard_map/ppermute | solution.py:231
  59.0 1.9 %collective-permute-start.9 = (bf16[16,7168]{1,0:T(8,128)(2,1)S(1)}, bf16[16,7168]{1,0:T(8,128)(2,1)S(1)}, u32[]{:S(2)}, u32[]{:S(2)}) collective-permute-start(bf16[16,7168]{1,0:T(8,128)(2,1)S(1)} %get-tuple-element.24), channel_id=1, source_target_pairs={{0,7},{1,0},{2,1},{3,2},{4,3},{5,4},{6,5},{7,6},{8,9},{9,10},{10,1... | collective-permute-start | bytes 688136 | tf_op jit(solution)/shard_map/ppermute | solution.py:231
  60.9 3.7 %collective-permute-done.12.refs_1_ = bf16[16,7168]{1,0:T(8,128)(2,1)S(1)} collective-permute-done((bf16[16,7168]{1,0:T(8,128)(2,1)S(1)}, bf16[16,7168]{1,0:T(8,128)(2,1)S(1)}, u32[]{:S(2)}, u32[]{:S(2)}) %collective-permute-start.12) | collective-permute-done | bytes 229408 | tf_op jit(solution)/shard_map/ppermute | solution.py:231
  64.6 0.1 plus.8
  64.7 5.6 %collective-permute-start.13 = (bf16[16,7168]{1,0:T(8,128)(2,1)S(1)}, bf16[16,7168]{1,0:T(8,128)(2,1)S(1)}, u32[]{:S(2)}, u32[]{:S(2)}) collective-permute-start(bf16[16,7168]{1,0:T(8,128)(2,1)S(1)} %plus.8), channel_id=1, source_target_pairs={{0,1},{1,2},{2,3},{3,4},{4,5},{5,6},{6,7},{7,0},{8,15},{9,8},{10,9... | collective-permute-start | bytes 688136 | tf_op jit(solution)/shard_map/ppermute | solution.py:231
  70.3 0.0 collective-permute-done.9.refs_1_
  70.3 0.1 plus.6
  70.3 1.9 %collective-permute-start.10 = (bf16[16,7168]{1,0:T(8,128)(2,1)S(1)}, bf16[16,7168]{1,0:T(8,128)(2,1)S(1)}, u32[]{:S(2)}, u32[]{:S(2)}) collective-permute-start(bf16[16,7168]{1,0:T(8,128)(2,1)S(1)} %plus.6), channel_id=1, source_target_pairs={{0,7},{1,0},{2,1},{3,2},{4,3},{5,4},{6,5},{7,6},{8,9},{9,10},{10,1... | collective-permute-start | bytes 688136 | tf_op jit(solution)/shard_map/ppermute | solution.py:231
  72.3 5.5 %collective-permute-start.8 = (bf16[16,7168]{1,0:T(8,128)(2,1)S(1)}, bf16[16,7168]{1,0:T(8,128)(2,1)S(1)}, u32[]{:S(2)}, u32[]{:S(2)}) collective-permute-start(bf16[16,7168]{1,0:T(8,128)(2,1)S(1)} %get-tuple-element.21), channel_id=1, source_target_pairs={{0,64},{1,65},{2,66},{3,67},{4,68},{5,69},{6,70},{7,71},{8,72},{9,... | collective-permute-start | bytes 688136 | tf_op jit(solution)/shard_map/ppermute | solution.py:231
  77.7 0.0 collective-permute-done.13.refs_1_
  77.7 0.1 plus.9
  77.8 5.1 %collective-permute-start.14 = (bf16[16,7168]{1,0:T(8,128)(2,1)S(1)}, bf16[16,7168]{1,0:T(8,128)(2,1)S(1)}, u32[]{:S(2)}, u32[]{:S(2)}) collective-permute-start(bf16[16,7168]{1,0:T(8,128)(2,1)S(1)} %plus.9), channel_id=1, source_target_pairs={{0,1},{1,2},{2,3},{3,4},{4,5},{5,6},{6,7},{7,0},{8,15},{9,8},{10,9... | collective-permute-start | bytes 688136 | tf_op jit(solution)/shard_map/ppermute | solution.py:231
  82.9 0.0 collective-permute-done.10.refs_1_
  82.9 0.1 plus.7
  83.0 2.5 %collective-permute-start.11 = (bf16[16,7168]{1,0:T(8,128)(2,1)S(1)}, bf16[16,7168]{1,0:T(8,128)(2,1)S(1)}, u32[]{:S(2)}, u32[]{:S(2)}) collective-permute-start(bf16[16,7168]{1,0:T(8,128)(2,1)S(1)} %plus.7), channel_id=1, source_target_pairs={{0,71},{1,64},{2,65},{3,66},{4,67},{5,68},{6,69},{7,70},{8,73},{9,... | collective-permute-start | bytes 688136 | tf_op jit(solution)/shard_map/ppermute | solution.py:231
  85.5 0.0 collective-permute-done.8.r_2_.refs_0_
  85.5 2.7 %collective-permute-done.14.r_1_ = bf16[16,7168]{1,0:T(8,128)(2,1)S(1)} collective-permute-done((bf16[16,7168]{1,0:T(8,128)(2,1)S(1)}, bf16[16,7168]{1,0:T(8,128)(2,1)S(1)}, u32[]{:S(2)}, u32[]{:S(2)}) %collective-permute-start.14) | collective-permute-done | bytes 229408 | tf_op jit(solution)/shard_map/ppermute | solution.py:231
  88.2 0.1 plus.10
  88.2 8.1 %collective-permute-start.15 = (bf16[16,7168]{1,0:T(8,128)(2,1)S(1)}, bf16[16,7168]{1,0:T(8,128)(2,1)S(1)}, u32[]{:S(2)}, u32[]{:S(2)}) collective-permute-start(bf16[16,7168]{1,0:T(8,128)(2,1)S(1)} %plus.10), channel_id=1, source_target_pairs={{0,65},{1,66},{2,67},{3,68},{4,69},{5,70},{6,71},{7,64},{8,79},{9,... | collective-permute-start | bytes 688136 | tf_op jit(solution)/shard_map/ppermute | solution.py:231
  96.4 0.0 collective-permute-done.11.refs_1_
  96.4 3.5 %collective-permute-done.15.refs_2_ = bf16[16,7168]{1,0:T(8,128)(2,1)S(1)} collective-permute-done((bf16[16,7168]{1,0:T(8,128)(2,1)S(1)}, bf16[16,7168]{1,0:T(8,128)(2,1)S(1)}, u32[]{:S(2)}, u32[]{:S(2)}) %collective-permute-start.15) | collective-permute-done | bytes 229408 | tf_op jit(solution)/shard_map/ppermute | solution.py:231
  99.9 0.1 plus.11
  100.0 0.1 reshape.14
  100.1 9.6 %all_to_all.11 = bf16[8,2,7168]{2,1,0:T(2,128)(2,1)S(1)} all-to-all(bf16[8,2,7168]{2,1,0:T(2,128)(2,1)S(1)} %reshape.14), channel_id=1, replica_groups=mesh['section'=16,'node'=8,'local'=8] {'node'}, dimensions={0} | all-to-all | bytes 458752 | tf_op jit(solution)/shard_map/all_to_all | solution.py:263
  109.6 0.1 reshape.15.rows_ref
  109.7 2.4 %combine_rows.1 = bf16[96,7168]{1,0:T(8,128)(2,1)} custom-call(f32[16,96]{1,0:T(8,128)S(1)} %collective-permute-done.refs_2_.weights_ref, bf16[16,7168]{1,0:T(8,128)(2,1)S(1)} %reshape.15.rows_ref), custom_call_target="tpu_custom_call" | custom-call | flops 66060288 | bytes 1605632 | tf_op jit(solution)/shard_map/combine_rows/pallas_call | solution.py:205
Async XLA Ops:
  0.0 48.1 %copy-start.1 = (bf16[1,7168,128]{2,1,0:T(8,128)(2,1)S(1)}, bf16[1,7168,128]{2,1,0:T(8,128)(2,1)}, u32[]{:S(2)}) copy-start(bf16[1,7168,128]{2,1,0:T(8,128)(2,1)} %param.12) | copy-start | bytes 5505028
  15.6 13.8 %collective-permute-start.4 = (bf16[16,7168]{1,0:T(8,128)(2,1)S(1)}, bf16[16,7168]{1,0:T(8,128)(2,1)S(1)}, u32[]{:S(2)}, u32[]{:S(2)}) collective-permute-start(bf16[16,7168]{1,0:T(8,128)(2,1)S(1)} %reshape.13.refs_3_), channel_id=1, source_target_pairs={{0,7},{1,0},{2,1},{3,2},{4,3},{5,4},{6,5},{7,6},{8,9},{9,10},{10,1... | collective-permute-start | bytes 688136 | tf_op jit(solution)/shard_map/ppermute | solution.py:231
  18.0 14.2 %collective-permute-start.3 = (bf16[16,7168]{1,0:T(8,128)(2,1)S(1)}, bf16[16,7168]{1,0:T(8,128)(2,1)S(1)}, u32[]{:S(2)}, u32[]{:S(2)}) collective-permute-start(bf16[16,7168]{1,0:T(8,128)(2,1)S(1)} %reshape.13.refs_3_), channel_id=1, source_target_pairs={{0,2},{1,3},{2,4},{3,5},{4,6},{5,7},{6,0},{7,1},{8,14},{9,15},{10,... | collective-permute-start | bytes 688136 | tf_op jit(solution)/shard_map/ppermute | solution.py:231
  23.7 14.0 %collective-permute-start.1 = (bf16[16,7168]{1,0:T(8,128)(2,1)S(1)}, bf16[16,7168]{1,0:T(8,128)(2,1)S(1)}, u32[]{:S(2)}, u32[]{:S(2)}) collective-permute-start(bf16[16,7168]{1,0:T(8,128)(2,1)S(1)} %reshape.13.refs_3_), channel_id=1, source_target_pairs={{0,1},{1,2},{2,3},{3,4},{4,5},{5,6},{6,7},{7,0},{8,15},{9,8},{10,9... | collective-permute-start | bytes 688136 | tf_op jit(solution)/shard_map/ppermute | solution.py:231
  26.3 23.6 %collective-permute-start.5 = (bf16[16,7168]{1,0:T(8,128)(2,1)S(1)}, bf16[16,7168]{1,0:T(8,128)(2,1)S(1)}, u32[]{:S(2)}, u32[]{:S(2)}) collective-permute-start(bf16[16,7168]{1,0:T(8,128)(2,1)S(1)} %reshape.13.refs_3_), channel_id=1, source_target_pairs={{0,6},{1,7},{2,0},{3,1},{4,2},{5,3},{6,4},{7,5},{8,10},{9,11},{10,... | collective-permute-start | bytes 688136 | tf_op jit(solution)/shard_map/ppermute | solution.py:231
  29.5 20.4 %collective-permute-start.6 = (bf16[16,7168]{1,0:T(8,128)(2,1)S(1)}, bf16[16,7168]{1,0:T(8,128)(2,1)S(1)}, u32[]{:S(2)}, u32[]{:S(2)}) collective-permute-start(bf16[16,7168]{1,0:T(8,128)(2,1)S(1)} %collective-permute-done.4.refs_4_), channel_id=1, source_target_pairs={{0,6},{1,7},{2,0},{3,1},{4,2},{5,3},{6,4},{7,5},{8,10},{9,11},{10,... | collective-permute-start | bytes 688136 | tf_op jit(solution)/shard_map/ppermute | solution.py:231
  32.2 17.7 %collective-permute-start.7 = (bf16[16,7168]{1,0:T(8,128)(2,1)S(1)}, bf16[16,7168]{1,0:T(8,128)(2,1)S(1)}, u32[]{:S(2)}, u32[]{:S(2)}) collective-permute-start(bf16[16,7168]{1,0:T(8,128)(2,1)S(1)} %collective-permute-done.3.refs_1_), channel_id=1, source_target_pairs={{0,2},{1,3},{2,4},{3,5},{4,6},{5,7},{6,0},{7,1},{8,14},{9,15},{10,... | collective-permute-start | bytes 688136 | tf_op jit(solution)/shard_map/ppermute | solution.py:231
  37.7 14.0 %collective-permute-start.2 = (bf16[16,7168]{1,0:T(8,128)(2,1)S(1)}, bf16[16,7168]{1,0:T(8,128)(2,1)S(1)}, u32[]{:S(2)}, u32[]{:S(2)}) collective-permute-start(bf16[16,7168]{1,0:T(8,128)(2,1)S(1)} %collective-permute-done.1.refs_2_), channel_id=1, source_target_pairs={{0,2},{1,3},{2,4},{3,5},{4,6},{5,7},{6,0},{7,1},{8,14},{9,15},{10,... | collective-permute-start | bytes 688136 | tf_op jit(solution)/shard_map/ppermute | solution.py:231
  41.1 7.1 %collective-permute-start = (f32[16,96]{1,0:T(8,128)}, f32[16,96]{1,0:T(8,128)S(1)}, u32[]{:S(2)}, u32[]{:S(2)}) collective-permute-start(f32[16,96]{1,0:T(8,128)} %get-tuple-element.17), channel_id=1, source_target_pairs={{0,64},{1,65},{2,66},{3,67},{4,68},{5,69},{6,70},{7,71},{8,72},{9,... | collective-permute-start | bytes 18440 | tf_op jit(solution)/shard_map/ppermute | solution.py:231
  48.1 1.5 %copy-start.2 = (bf16[1,128,7168]{2,1,0:T(8,128)(2,1)S(1)}, bf16[1,128,7168]{2,1,0:T(8,128)(2,1)}, u32[]{:S(2)}) copy-start(bf16[1,128,7168]{2,1,0:T(8,128)(2,1)} %param.13) | copy-start | bytes 5505028
  49.6 2.1 %copy-start = (bf16[1,7168,128]{2,1,0:T(8,128)(2,1)S(1)}, bf16[1,7168,128]{2,1,0:T(8,128)(2,1)}, u32[]{:S(2)}) copy-start(bf16[1,7168,128]{2,1,0:T(8,128)(2,1)} %param.11) | copy-start | bytes 5505028
  53.4 11.2 %collective-permute-start.12 = (bf16[16,7168]{1,0:T(8,128)(2,1)S(1)}, bf16[16,7168]{1,0:T(8,128)(2,1)S(1)}, u32[]{:S(2)}, u32[]{:S(2)}) collective-permute-start(bf16[16,7168]{1,0:T(8,128)(2,1)S(1)} %get-tuple-element.28), channel_id=1, source_target_pairs={{0,1},{1,2},{2,3},{3,4},{4,5},{5,6},{6,7},{7,0},{8,15},{9,8},{10,9... | collective-permute-start | bytes 688136 | tf_op jit(solution)/shard_map/ppermute | solution.py:231
  59.0 11.3 %collective-permute-start.9 = (bf16[16,7168]{1,0:T(8,128)(2,1)S(1)}, bf16[16,7168]{1,0:T(8,128)(2,1)S(1)}, u32[]{:S(2)}, u32[]{:S(2)}) collective-permute-start(bf16[16,7168]{1,0:T(8,128)(2,1)S(1)} %get-tuple-element.24), channel_id=1, source_target_pairs={{0,7},{1,0},{2,1},{3,2},{4,3},{5,4},{6,5},{7,6},{8,9},{9,10},{10,1... | collective-permute-start | bytes 688136 | tf_op jit(solution)/shard_map/ppermute | solution.py:231
  64.7 13.1 %collective-permute-start.13 = (bf16[16,7168]{1,0:T(8,128)(2,1)S(1)}, bf16[16,7168]{1,0:T(8,128)(2,1)S(1)}, u32[]{:S(2)}, u32[]{:S(2)}) collective-permute-start(bf16[16,7168]{1,0:T(8,128)(2,1)S(1)} %plus.8), channel_id=1, source_target_pairs={{0,1},{1,2},{2,3},{3,4},{4,5},{5,6},{6,7},{7,0},{8,15},{9,8},{10,9... | collective-permute-start | bytes 688136 | tf_op jit(solution)/shard_map/ppermute | solution.py:231
  70.3 12.6 %collective-permute-start.10 = (bf16[16,7168]{1,0:T(8,128)(2,1)S(1)}, bf16[16,7168]{1,0:T(8,128)(2,1)S(1)}, u32[]{:S(2)}, u32[]{:S(2)}) collective-permute-start(bf16[16,7168]{1,0:T(8,128)(2,1)S(1)} %plus.6), channel_id=1, source_target_pairs={{0,7},{1,0},{2,1},{3,2},{4,3},{5,4},{6,5},{7,6},{8,9},{9,10},{10,1... | collective-permute-start | bytes 688136 | tf_op jit(solution)/shard_map/ppermute | solution.py:231
  72.3 13.3 %collective-permute-start.8 = (bf16[16,7168]{1,0:T(8,128)(2,1)S(1)}, bf16[16,7168]{1,0:T(8,128)(2,1)S(1)}, u32[]{:S(2)}, u32[]{:S(2)}) collective-permute-start(bf16[16,7168]{1,0:T(8,128)(2,1)S(1)} %get-tuple-element.21), channel_id=1, source_target_pairs={{0,64},{1,65},{2,66},{3,67},{4,68},{5,69},{6,70},{7,71},{8,72},{9,... | collective-permute-start | bytes 688136 | tf_op jit(solution)/shard_map/ppermute | solution.py:231
  77.8 10.4 %collective-permute-start.14 = (bf16[16,7168]{1,0:T(8,128)(2,1)S(1)}, bf16[16,7168]{1,0:T(8,128)(2,1)S(1)}, u32[]{:S(2)}, u32[]{:S(2)}) collective-permute-start(bf16[16,7168]{1,0:T(8,128)(2,1)S(1)} %plus.9), channel_id=1, source_target_pairs={{0,1},{1,2},{2,3},{3,4},{4,5},{5,6},{6,7},{7,0},{8,15},{9,8},{10,9... | collective-permute-start | bytes 688136 | tf_op jit(solution)/shard_map/ppermute | solution.py:231
  83.0 13.4 %collective-permute-start.11 = (bf16[16,7168]{1,0:T(8,128)(2,1)S(1)}, bf16[16,7168]{1,0:T(8,128)(2,1)S(1)}, u32[]{:S(2)}, u32[]{:S(2)}) collective-permute-start(bf16[16,7168]{1,0:T(8,128)(2,1)S(1)} %plus.7), channel_id=1, source_target_pairs={{0,71},{1,64},{2,65},{3,66},{4,67},{5,68},{6,69},{7,70},{8,73},{9,... | collective-permute-start | bytes 688136 | tf_op jit(solution)/shard_map/ppermute | solution.py:231
  88.2 11.6 %collective-permute-start.15 = (bf16[16,7168]{1,0:T(8,128)(2,1)S(1)}, bf16[16,7168]{1,0:T(8,128)(2,1)S(1)}, u32[]{:S(2)}, u32[]{:S(2)}) collective-permute-start(bf16[16,7168]{1,0:T(8,128)(2,1)S(1)} %plus.10), channel_id=1, source_target_pairs={{0,65},{1,66},{2,67},{3,68},{4,69},{5,70},{6,71},{7,64},{8,79},{9,... | collective-permute-start | bytes 688136 | tf_op jit(solution)/shard_map/ppermute | solution.py:231

commit v4 on v3

--- a/solution.py
+++ b/solution.py
@@ -8,6 +8,8 @@
 CAP = 2
 COLUMNS = 896
 PIECE = 1792
+LANES = 128
+SPLIT = 3
 VMEM = pl.BlockSpec(memory_space=pltpu.VMEM)
 ANY = pl.BlockSpec(memory_space=pl.ANY)
 HBM = pl.BlockSpec(memory_space=pltpu.HBM)
@@ -70,7 +72,12 @@
     triangle = (before < after).astype(jnp.float32).astype(jnp.bfloat16)
     rank = jnp.dot(named.astype(jnp.bfloat16), triangle, preferred_element_type=jnp.float32)
     chosen = (named > 0.0) & (rank == want.astype(jnp.float32))
-    combine_ref[...] = jnp.where(chosen, weight, 0.0)
+    weight = jnp.where(chosen, weight, 0.0)
+    combine_ref[...] = jnp.zeros_like(combine_ref)
+    for k in range(SPLIT):
+        piece = weight.astype(jnp.bfloat16)
+        weight = weight - piece.astype(jnp.float32)
+        combine_ref[:, k * LANES : k * LANES + tok_dev] = piece
     select = jnp.where(chosen, 1.0, 0.0).astype(jnp.bfloat16)
     for copy, c in zip(pieces, starts):
         copy.wait()
@@ -86,7 +93,7 @@
         pick_kernel,
         out_shape=(
             jax.ShapeDtypeStruct((rows_dev, width), jnp.bfloat16),
-            jax.ShapeDtypeStruct((rows_dev, tok_dev), jnp.float32),
+            jax.ShapeDtypeStruct((rows_dev, SPLIT * LANES), jnp.bfloat16),
         ),
         in_specs=[pl.BlockSpec(memory_space=pltpu.SMEM), HBM, HBM, HBM],
         out_specs=(VMEM, VMEM),
@@ -127,8 +134,8 @@
     )(*arrays, after)
 
 
-def experts_kernel(n, *refs):
-    blocks, (gate_ref, up_ref, down_ref), outs = refs[:n], refs[n : n + 3], refs[n + 3 :]
+def experts_kernel(n, own, *refs):
+    blocks, (gate_ref, up_ref, down_ref, tail_ref), outs = refs[:n], refs[n : n + 4], refs[n + 4 :]
     rows_dev, width = blocks[0].shape
     hid = gate_ref.shape[1]
     gate_proj = jnp.zeros((n * rows_dev, hid), jnp.float32)
@@ -146,75 +153,74 @@
         part = part.astype(jnp.bfloat16)
         for k in range(n):
             outs[k][:, cols] = part[k * rows_dev : (k + 1) * rows_dev]
-
-
-def experts(blocks, w_gate, w_up, w_down):
+    outs[own][:, width:] = tail_ref[...]
+
+
+def experts(blocks, w_gate, w_up, w_down, tail, own):
     n = len(blocks)
     rows_dev, width = blocks[0].shape
     hid = w_gate.shape[1]
-    return pl.pallas_call(
-        lambda *refs: experts_kernel(n, *refs),
-        out_shape=[jax.ShapeDtypeStruct((rows_dev, width), jnp.bfloat16)] * n,
-        in_specs=[VMEM] * (n + 3),
+    widths = [width + (tail.shape[1] if k == own else 0) for k in range(n)]
+    return pl.pallas_call(
+        lambda *refs: experts_kernel(n, own, *refs),
+        out_shape=[jax.ShapeDtypeStruct((rows_dev, w), jnp.bfloat16) for w in widths],
+        in_specs=[VMEM] * (n + 4),
         out_specs=[VMEM] * n,
         compiler_params=grant(24),
         cost_estimate=cost(6 * n * rows_dev * width * hid, 6 * width * hid),
         name="experts",
-    )(*blocks, w_gate, w_up, w_down)
+    )(*blocks, w_gate, w_up, w_down, tail)
 
 
 def plus_kernel(*refs):
-    total = refs[0][...].astype(jnp.float32)
+    out_ref = refs[-1]
+    width = out_ref.shape[1]
+    total = refs[0][:, :width].astype(jnp.float32)
     for ref in refs[1:-1]:
-        total = total + ref[...].astype(jnp.float32)
-    refs[-1][...] = total.astype(jnp.bfloat16)
-
-
-def plus(*terms, after=None):
-    held = () if after is None else (after,)
-    body = plus_kernel if after is None else (lambda *r: plus_kernel(*r[:-2], r[-1]))
-    return pl.pallas_call(
-        body,
-        out_shape=jax.ShapeDtypeStruct(terms[0].shape, jnp.bfloat16),
-        in_specs=[VMEM] * len(terms) + [ANY] * len(held),
+        total = total + ref[:, :width].astype(jnp.float32)
+    out_ref[...] = total.astype(jnp.bfloat16)
+
+
+def plus(*terms):
+    shape = terms[-1].shape
+    size = shape[0] * shape[1]
+    return pl.pallas_call(
+        plus_kernel,
+        out_shape=jax.ShapeDtypeStruct(shape, jnp.bfloat16),
+        in_specs=[VMEM] * len(terms),
         out_specs=VMEM,
         compiler_params=grant(4),
-        cost_estimate=cost(len(terms) * terms[0].size, 2 * (len(terms) + 1) * terms[0].size),
+        cost_estimate=cost(len(terms) * size, 2 * (len(terms) + 1) * size),
         name="plus",
-    )(*terms, *held)
-
-
-def combine_kernel(weights_ref, rows_ref, out_ref):
-    weights = weights_ref[...]
-    high = weights.astype(jnp.bfloat16)
-    rest = weights - high.astype(jnp.float32)
-    middle = rest.astype(jnp.bfloat16)
-    low = (rest - middle.astype(jnp.float32)).astype(jnp.bfloat16)
-    split = jnp.concatenate([high, middle, low], axis=0)
+    )(*terms)
+
+
+def combine_kernel(*refs):
+    pieces, rows_ref, out_ref = refs[:SPLIT], refs[SPLIT], refs[SPLIT + 1]
+    tok_dev = out_ref.shape[0]
+    split = jnp.concatenate([piece[...] for piece in pieces], axis=0)
     rows = rows_ref[...]
-    rows = jnp.concatenate([rows, rows, rows], axis=0)
-    out_ref[...] = lax.dot_general(
-        split, rows, (((0,), (0,)), ((), ())), preferred_element_type=jnp.float32
-    ).astype(jnp.bfloat16)
-
-
-def combine_rows(weights, rows):
-    rows_dev, tok_dev = weights.shape
-    width = rows.shape[1]
+    rows = jnp.concatenate([rows] * SPLIT, axis=0)
+    out = lax.dot_general(split, rows, (((0,), (0,)), ((), ())), preferred_element_type=jnp.float32)
+    out_ref[...] = out[:tok_dev].astype(jnp.bfloat16)
+
+
+def combine_rows(carrier, rows, tok_dev):
+    rows_dev, width = rows.shape
     block = width // 4
+    tail = [
+        pl.BlockSpec((rows_dev, LANES), lambda j, k=k: (0, width // LANES + k)) for k in range(SPLIT)
+    ]
     return pl.pallas_call(
         combine_kernel,
         grid=(4,),
         out_shape=jax.ShapeDtypeStruct((tok_dev, width), jnp.bfloat16),
-        in_specs=[
-            pl.BlockSpec((rows_dev, tok_dev), lambda j: (0, 0)),
-            pl.BlockSpec((rows_dev, block), lambda j: (0, j)),
-        ],
+        in_specs=tail + [pl.BlockSpec((rows_dev, block), lambda j: (0, j))],
         out_specs=pl.BlockSpec((tok_dev, block), lambda j: (0, j)),
         compiler_params=grant(8),
         cost_estimate=cost(6 * rows_dev * tok_dev * width, 2 * (tok_dev + rows_dev) * width),
         name="combine_rows",
-    )(weights, rows)
+    )(*([carrier] * SPLIT), rows)
 
 
 def hop(block, step, sections=0):
@@ -236,34 +242,30 @@
     far = lax.axis_size("local") // 2
     rows_dev = n_node * CAP
     width = tokens.shape[2]
-    outgoing, combine = pick_rows(replica_table, routes[0].T, route_gates[0].T, tokens[0], rows_dev)
-    weights = hop(combine, 0, 1)
+    outgoing, tail = pick_rows(replica_table, routes[0].T, route_gates[0].T, tokens[0], rows_dev)
     own = lax.all_to_all(
         outgoing.reshape(n_node, CAP, width), "node", split_axis=0, concat_axis=0, tiled=True
     ).reshape(rows_dev, width)
     blocks = {0: own}
-    for q in range(2, 0, -1):
-        blocks[-q], blocks[q] = hop(own, q), hop(own, -q)
-    for q in range(3, far):
-        blocks[-q], blocks[q] = hop(blocks[2 - q], 2), hop(blocks[q - 2], -2)
-    blocks[far] = hop(blocks[2 - far], 2)
+    blocks[-2], blocks[2] = hop(own, 2), hop(own, -2)
+    blocks[-1], blocks[1] = hop(own, 1), hop(own, -1)
+    blocks[far] = hop(blocks[-2], 2)
+    blocks[-3], blocks[3] = hop(blocks[-2], 1), hop(blocks[2], -1)
     order = sorted(blocks)
-    up_mat, down_mat = load([w_up[0], w_down[0]], weights)
-    parts = experts([blocks[q] for q in order], w_gate[0], up_mat, down_mat)
+    up_mat, down_mat = load([w_up[0], w_down[0]], blocks[-1])
+    parts = experts(
+        [blocks[q] for q in order], w_gate[0], up_mat, down_mat, tail, order.index(0)
+    )
     part = dict(zip(order, parts))
-    mine = hop(part[0], 0, 1)
-    ahead, back = hop(part[far], 1), hop(part[1 - far], -1)
-    for q in range(far - 1, 0, -1):
-        last = q == 1
-        ahead = plus(part[q], ahead, after=mine if last else None)
-        if not last:
-            back = hop(plus(part[1 - q], back), -1, 1 if q == 2 else 0)
-        ahead = hop(ahead, 1, 1 if last else 0)
-    expert_out = plus(mine, back, ahead)
+    ahead = plus(part[2], hop(part[far], 2), hop(part[3], 1))
+    back = plus(part[-2], hop(part[-3], -1))
+    carrier = hop(part[0], 0, 1)
+    near = [hop(part[1], 1, 1), hop(part[-1], -1, 1)]
+    expert_out = plus(carrier, *near, hop(ahead, 2, 1), hop(back, -2, 1))
     returned = lax.all_to_all(
         expert_out.reshape(n_node, CAP, width), "node", split_axis=0, concat_axis=0, tiled=True
     ).reshape(rows_dev, width)
-    return combine_rows(weights, returned)[None]
+    return combine_rows(carrier, returned, tokens.shape[1])[None]
 
 
 def solution(mesh):

time: 113 us -> 113 us (level)
  the two profiles are of different devices: /device:TPU:216 before, /device:TPU:200 now
where the time goes in v4:
time: 113 us; the launch traced here: 112 us
  starting transfers between devices  65.8 us (58%)
  blocking collectives  20.8 us (18%)
  waiting for transfers between devices  14.2 us (13%)
  Pallas kernels  7.99 us (7%)
  local copies, waits for them, and re-layouts  2.8 us (2%)
    ppermute x15, starting transfers between devices, hop(): return lax.ppermute(block, ('section', 'node', 'local'), pairs)  65.8 us
    ppermute x15, waiting for transfers between devices, hop(): return lax.ppermute(block, ('section', 'node', 'local'), pairs)  14.2 us
    all_to_all x1, blocking collectives, shards(): lax.all_to_all(outgoing.reshape(n_node, CAP, width), 'node', split_axis=0...  11.3 us
    all_to_all x1, blocking collectives, shards(): lax.all_to_all(expert_out.reshape(n_node, CAP, width), 'node', split_axis...  9.56 us
    pallas_call x1, Pallas kernels, pick_rows(): pl.pallas_call(pick_kernel, out_shape=(jax.ShapeDtypeStruct((rows_dev, wi...  3.24 us
    pallas_call x1, Pallas kernels, combine_rows(): pl.pallas_call(combine_kernel, grid=(4,), out_shape=jax.ShapeDtypeStruct(...  2.45 us
  transfers between devices with their start and end apart: 15, of which 4 were waited for; matrix products, arithmetic and copies ran while one was open for 0% of the time, Pallas kernels for 0%

profile of v4, /device:TPU:200, one launch (start us, length us, event | category | flops | bytes accessed | tf_op | source)
XLA Modules:
  0.0 111.9 jit_solution(13987871933324060512)
XLA Ops:
  0.0 0.0 copy-start
  0.0 3.2 %pick_rows.1 = (bf16[16,7168]{1,0:T(8,128)(2,1)}, bf16[16,384]{1,0:T(8,128)(2,1)}) custom-call(s32[8]{0:T(128)} %table_ref.1, s32[8,96]{1,0:T(8,128)} %bitcast.15, f32[8,96]{1,0:T(8,128)} %bitcast.16, bf16[96,7168]{1,0:T(8,128)(2,1)} %bitcast.14), custom_call_target="tpu_custom_call" | custom-call | flops 22020096 | bytes 1605632 | tf_op jit(solution)/shard_map/pick_rows/pallas_call | solution.py:92
  3.2 1.0 reshape.12
  4.3 11.3 %all_to_all.10 = bf16[8,2,7168]{2,1,0:T(2,128)(2,1)S(1)} all-to-all(bf16[8,2,7168]{2,1,0:T(2,128)(2,1)S(1)} %reshape.12), channel_id=1, replica_groups=mesh['section'=16,'node'=8,'local'=8] {'node'}, dimensions={0} | all-to-all | bytes 458752 | tf_op jit(solution)/shard_map/all_to_all | solution.py:246
  15.5 0.1 reshape.13.refs_3_
  15.6 5.3 %collective-permute-start.4 = (bf16[16,7168]{1,0:T(8,128)(2,1)S(1)}, bf16[16,7168]{1,0:T(8,128)(2,1)S(1)}, u32[]{:S(2)}, u32[]{:S(2)}) collective-permute-start(bf16[16,7168]{1,0:T(8,128)(2,1)S(1)} %reshape.13.refs_3_), channel_id=1, source_target_pairs={{0,6},{1,7},{2,0},{3,1},{4,2},{5,3},{6,4},{7,5},{8,10},{9,11},{10,... | collective-permute-start | bytes 688136 | tf_op jit(solution)/shard_map/ppermute | solution.py:237
  20.9 1.9 %collective-permute-start = (bf16[16,7168]{1,0:T(8,128)(2,1)S(1)}, bf16[16,7168]{1,0:T(8,128)(2,1)S(1)}, u32[]{:S(2)}, u32[]{:S(2)}) collective-permute-start(bf16[16,7168]{1,0:T(8,128)(2,1)S(1)} %reshape.13.refs_3_), channel_id=1, source_target_pairs={{0,2},{1,3},{2,4},{3,5},{4,6},{5,7},{6,0},{7,1},{8,14},{9,15},{10,... | collective-permute-start | bytes 688136 | tf_op jit(solution)/shard_map/ppermute | solution.py:237
  22.8 4.3 %collective-permute-start.2 = (bf16[16,7168]{1,0:T(8,128)(2,1)S(1)}, bf16[16,7168]{1,0:T(8,128)(2,1)S(1)}, u32[]{:S(2)}, u32[]{:S(2)}) collective-permute-start(bf16[16,7168]{1,0:T(8,128)(2,1)S(1)} %reshape.13.refs_3_), channel_id=1, source_target_pairs={{0,1},{1,2},{2,3},{3,4},{4,5},{5,6},{6,7},{7,0},{8,15},{9,8},{10,9... | collective-permute-start | bytes 688136 | tf_op jit(solution)/shard_map/ppermute | solution.py:237
  27.1 1.9 %collective-permute-start.3 = (bf16[16,7168]{1,0:T(8,128)(2,1)S(1)}, bf16[16,7168]{1,0:T(8,128)(2,1)S(1)}, u32[]{:S(2)}, u32[]{:S(2)}) collective-permute-start(bf16[16,7168]{1,0:T(8,128)(2,1)S(1)} %reshape.13.refs_3_), channel_id=1, source_target_pairs={{0,7},{1,0},{2,1},{3,2},{4,3},{5,4},{6,5},{7,6},{8,9},{9,10},{10,1... | collective-permute-start | bytes 688136 | tf_op jit(solution)/shard_map/ppermute | solution.py:237
  29.0 0.0 collective-permute-done.4.refs_5_
  29.0 5.3 %collective-permute-start.5 = (bf16[16,7168]{1,0:T(8,128)(2,1)S(1)}, bf16[16,7168]{1,0:T(8,128)(2,1)S(1)}, u32[]{:S(2)}, u32[]{:S(2)}) collective-permute-start(bf16[16,7168]{1,0:T(8,128)(2,1)S(1)} %collective-permute-done.4.refs_5_), channel_id=1, source_target_pairs={{0,7},{1,0},{2,1},{3,2},{4,3},{5,4},{6,5},{7,6},{8,9},{9,10},{10,1... | collective-permute-start | bytes 688136 | tf_op jit(solution)/shard_map/ppermute | solution.py:237
  34.3 0.0 collective-permute-done.refs_1_
  34.3 4.1 %collective-permute-start.6 = (bf16[16,7168]{1,0:T(8,128)(2,1)S(1)}, bf16[16,7168]{1,0:T(8,128)(2,1)S(1)}, u32[]{:S(2)}, u32[]{:S(2)}) collective-permute-start(bf16[16,7168]{1,0:T(8,128)(2,1)S(1)} %collective-permute-done.refs_1_), channel_id=1, source_target_pairs={{0,2},{1,3},{2,4},{3,5},{4,6},{5,7},{6,0},{7,1},{8,14},{9,15},{10,... | collective-permute-start | bytes 688136 | tf_op jit(solution)/shard_map/ppermute | solution.py:237
  38.5 4.4 %collective-permute-start.1 = (bf16[16,7168]{1,0:T(8,128)(2,1)S(1)}, bf16[16,7168]{1,0:T(8,128)(2,1)S(1)}, u32[]{:S(2)}, u32[]{:S(2)}) collective-permute-start(bf16[16,7168]{1,0:T(8,128)(2,1)S(1)} %collective-permute-done.refs_1_), channel_id=1, source_target_pairs={{0,1},{1,2},{2,3},{3,4},{4,5},{5,6},{6,7},{7,0},{8,15},{9,8},{10,9... | collective-permute-start | bytes 688136 | tf_op jit(solution)/shard_map/ppermute | solution.py:237
  42.8 0.0 collective-permute-done.2.refs_2_
  42.8 0.0 copy-done
  42.9 0.0 copy-start.1
  42.9 1.5 %copy-done.1 = bf16[1,128,7168]{2,1,0:T(8,128)(2,1)S(1)} copy-done((bf16[1,128,7168]{2,1,0:T(8,128)(2,1)S(1)}, bf16[1,128,7168]{2,1,0:T(8,128)(2,1)}, u32[]{:S(2)}) %copy-start.1) | copy-done | bytes 1835032
  44.4 0.0 copy-start.2
  44.4 0.0 copy-start.3
  44.4 0.3 load.1
  44.6 0.0 collective-permute-done.3.refs_4_
  44.6 0.0 collective-permute-done.5.refs_6_
  44.7 2.7 %collective-permute-done.6.refs_7_ = bf16[16,7168]{1,0:T(8,128)(2,1)S(1)} collective-permute-done((bf16[16,7168]{1,0:T(8,128)(2,1)S(1)}, bf16[16,7168]{1,0:T(8,128)(2,1)S(1)}, u32[]{:S(2)}, u32[]{:S(2)}) %collective-permute-start.6) | collective-permute-done | bytes 229408 | tf_op jit(solution)/shard_map/ppermute | solution.py:237
  47.3 1.4 %collective-permute-done.1.refs_0_ = bf16[16,7168]{1,0:T(8,128)(2,1)S(1)} collective-permute-done((bf16[16,7168]{1,0:T(8,128)(2,1)S(1)}, bf16[16,7168]{1,0:T(8,128)(2,1)S(1)}, u32[]{:S(2)}, u32[]{:S(2)}) %collective-permute-start.1) | collective-permute-done | bytes 229408 | tf_op jit(solution)/shard_map/ppermute | solution.py:237
  48.7 0.0 copy-done.2
  48.7 0.0 copy-done.3
  48.7 1.7 %experts.1 = (bf16[16,7168]{1,0:T(8,128)(2,1)S(1)}, bf16[16,7168]{1,0:T(8,128)(2,1)S(1)}, bf16[16,7168]{1,0:T(8,128)(2,1)S(1)}, bf16[16,7552]{1,0:T(8,128)(2,1)S...) custom-call(bf16[16,7168]{1,0:T(8,128)(2,1)S(1)} %collective-permute, ...), custom_call_target="tpu_custom_call" | custom-call | flops 704643072 | bytes 5505024 | tf_op jit(solution)/shard_map/experts/pallas_call | solution.py:164
  50.5 4.4 %collective-permute-start.10 = (bf16[16,7168]{1,0:T(8,128)(2,1)S(1)}, bf16[16,7168]{1,0:T(8,128)(2,1)S(1)}, u32[]{:S(2)}, u32[]{:S(2)}) collective-permute-start(bf16[16,7168]{1,0:T(8,128)(2,1)S(1)} %get-tuple-element.25), channel_id=1, source_target_pairs={{0,2},{1,3},{2,4},{3,5},{4,6},{5,7},{6,0},{7,1},{8,14},{9,15},{10,... | collective-permute-start | bytes 688136 | tf_op jit(solution)/shard_map/ppermute | solution.py:237
  54.9 4.7 %collective-permute-start.11 = (bf16[16,7168]{1,0:T(8,128)(2,1)S(1)}, bf16[16,7168]{1,0:T(8,128)(2,1)S(1)}, u32[]{:S(2)}, u32[]{:S(2)}) collective-permute-start(bf16[16,7168]{1,0:T(8,128)(2,1)S(1)} %get-tuple-element.26), channel_id=1, source_target_pairs={{0,1},{1,2},{2,3},{3,4},{4,5},{5,6},{6,7},{7,0},{8,15},{9,8},{10,9... | collective-permute-start | bytes 688136 | tf_op jit(solution)/shard_map/ppermute | solution.py:237
  59.5 1.9 %collective-permute-start.13 = (bf16[16,7168]{1,0:T(8,128)(2,1)S(1)}, bf16[16,7168]{1,0:T(8,128)(2,1)S(1)}, u32[]{:S(2)}, u32[]{:S(2)}) collective-permute-start(bf16[16,7168]{1,0:T(8,128)(2,1)S(1)} %get-tuple-element.28), channel_id=1, source_target_pairs={{0,7},{1,0},{2,1},{3,2},{4,3},{5,4},{6,5},{7,6},{8,9},{9,10},{10,1... | collective-permute-start | bytes 688136 | tf_op jit(solution)/shard_map/ppermute | solution.py:237
  61.5 5.5 %collective-permute-start.7 = (bf16[16,7552]{1,0:T(8,128)(2,1)S(1)}, bf16[16,7552]{1,0:T(8,128)(2,1)S(1)}, u32[]{:S(2)}, u32[]{:S(2)}) collective-permute-start(bf16[16,7552]{1,0:T(8,128)(2,1)S(1)} %get-tuple-element.21), channel_id=1, source_target_pairs={{0,64},{1,65},{2,66},{3,67},{4,68},{5,69},{6,70},{7,71},{8,72},{9,... | collective-permute-start | bytes 725000 | tf_op jit(solution)/shard_map/ppermute | solution.py:237
  67.0 5.8 %collective-permute-start.8 = (bf16[16,7168]{1,0:T(8,128)(2,1)S(1)}, bf16[16,7168]{1,0:T(8,128)(2,1)S(1)}, u32[]{:S(2)}, u32[]{:S(2)}) collective-permute-start(bf16[16,7168]{1,0:T(8,128)(2,1)S(1)} %get-tuple-element.22), channel_id=1, source_target_pairs={{0,65},{1,66},{2,67},{3,68},{4,69},{5,70},{6,71},{7,64},{8,79},{9,... | collective-permute-start | bytes 688136 | tf_op jit(solution)/shard_map/ppermute | solution.py:237
  72.7 0.0 collective-permute-done.10.refs_1_
  72.7 3.7 %collective-permute-start.9 = (bf16[16,7168]{1,0:T(8,128)(2,1)S(1)}, bf16[16,7168]{1,0:T(8,128)(2,1)S(1)}, u32[]{:S(2)}, u32[]{:S(2)}) collective-permute-start(bf16[16,7168]{1,0:T(8,128)(2,1)S(1)} %get-tuple-element.23), channel_id=1, source_target_pairs={{0,71},{1,64},{2,65},{3,66},{4,67},{5,68},{6,69},{7,70},{8,73},{9,... | collective-permute-start | bytes 688136 | tf_op jit(solution)/shard_map/ppermute | solution.py:237
  76.5 0.0 collective-permute-done.11.refs_2_
  76.5 0.1 plus.3
  76.6 5.3 %collective-permute-start.12 = (bf16[16,7168]{1,0:T(8,128)(2,1)S(1)}, bf16[16,7168]{1,0:T(8,128)(2,1)S(1)}, u32[]{:S(2)}, u32[]{:S(2)}) collective-permute-start(bf16[16,7168]{1,0:T(8,128)(2,1)S(1)} %plus.3), channel_id=1, source_target_pairs={{0,66},{1,67},{2,68},{3,69},{4,70},{5,71},{6,64},{7,65},{8,78},{9,... | collective-permute-start | bytes 688136 | tf_op jit(solution)/shard_map/ppermute | solution.py:237
  81.8 0.0 collective-permute-done.13.refs_1_
  81.9 0.1 plus.4
  81.9 7.5 %collective-permute-start.14 = (bf16[16,7168]{1,0:T(8,128)(2,1)S(1)}, bf16[16,7168]{1,0:T(8,128)(2,1)S(1)}, u32[]{:S(2)}, u32[]{:S(2)}) collective-permute-start(bf16[16,7168]{1,0:T(8,128)(2,1)S(1)} %plus.4), channel_id=1, source_target_pairs={{0,70},{1,71},{2,64},{3,65},{4,66},{5,67},{6,68},{7,69},{8,74},{9,... | collective-permute-start | bytes 688136 | tf_op jit(solution)/shard_map/ppermute | solution.py:237
  89.4 0.0 collective-permute-done.8.refs_1_
  89.5 0.0 collective-permute-done.9.refs_2_
  89.5 0.0 collective-permute-done.7.refs_0_.refs_1_.refs_2_
  89.5 0.5 collective-permute-done.12.refs_3_
  90.0 9.5 %collective-permute-done.14.refs_4_ = bf16[16,7168]{1,0:T(8,128)(2,1)S(1)} collective-permute-done((bf16[16,7168]{1,0:T(8,128)(2,1)S(1)}, bf16[16,7168]{1,0:T(8,128)(2,1)S(1)}, u32[]{:S(2)}, u32[]{:S(2)}) %collective-permute-start.14) | collective-permute-done | bytes 229408 | tf_op jit(solution)/shard_map/ppermute | solution.py:237
  99.5 0.1 plus.5
  99.7 0.1 reshape.14
  99.8 9.6 %all_to_all.11 = bf16[8,2,7168]{2,1,0:T(2,128)(2,1)S(1)} all-to-all(bf16[8,2,7168]{2,1,0:T(2,128)(2,1)S(1)} %reshape.14), channel_id=1, replica_groups=mesh['section'=16,'node'=8,'local'=8] {'node'}, dimensions={0} | all-to-all | bytes 458752 | tf_op jit(solution)/shard_map/all_to_all | solution.py:265
  109.3 0.1 reshape.15.refs_3_
  109.4 2.5 %combine_rows.1 = bf16[96,7168]{1,0:T(8,128)(2,1)} custom-call(bf16[16,7552]{1,0:T(8,128)(2,1)S(1)} %collective-permute-done.7.refs_0_.refs_1_.refs_2_, bf16[16,7552]{1,0:T(8,128)(2,1)S(1)} %collective-permute-done.7.refs_0_.refs_1_.refs_2_, bf16[16,7552]{1,0:T(8,128)(2,1)S(1)} %collective-permute-done.7.refs_0_.refs_1_.refs_2_, ...), custom_call_target="tpu_custom_call" | custom-call | flops 66060288 | bytes 1605632 | tf_op jit(solution)/shard_map/combine_rows/pallas_call | solution.py:214
Async XLA Ops:
  0.0 42.8 %copy-start = (bf16[1,7168,128]{2,1,0:T(8,128)(2,1)S(1)}, bf16[1,7168,128]{2,1,0:T(8,128)(2,1)}, u32[]{:S(2)}) copy-start(bf16[1,7168,128]{2,1,0:T(8,128)(2,1)} %param.12) | copy-start | bytes 5505028
  15.6 13.4 %collective-permute-start.4 = (bf16[16,7168]{1,0:T(8,128)(2,1)S(1)}, bf16[16,7168]{1,0:T(8,128)(2,1)S(1)}, u32[]{:S(2)}, u32[]{:S(2)}) collective-permute-start(bf16[16,7168]{1,0:T(8,128)(2,1)S(1)} %reshape.13.refs_3_), channel_id=1, source_target_pairs={{0,6},{1,7},{2,0},{3,1},{4,2},{5,3},{6,4},{7,5},{8,10},{9,11},{10,... | collective-permute-start | bytes 688136 | tf_op jit(solution)/shard_map/ppermute | solution.py:237
  20.9 13.4 %collective-permute-start = (bf16[16,7168]{1,0:T(8,128)(2,1)S(1)}, bf16[16,7168]{1,0:T(8,128)(2,1)S(1)}, u32[]{:S(2)}, u32[]{:S(2)}) collective-permute-start(bf16[16,7168]{1,0:T(8,128)(2,1)S(1)} %reshape.13.refs_3_), channel_id=1, source_target_pairs={{0,2},{1,3},{2,4},{3,5},{4,6},{5,7},{6,0},{7,1},{8,14},{9,15},{10,... | collective-permute-start | bytes 688136 | tf_op jit(solution)/shard_map/ppermute | solution.py:237
  22.8 20.0 %collective-permute-start.2 = (bf16[16,7168]{1,0:T(8,128)(2,1)S(1)}, bf16[16,7168]{1,0:T(8,128)(2,1)S(1)}, u32[]{:S(2)}, u32[]{:S(2)}) collective-permute-start(bf16[16,7168]{1,0:T(8,128)(2,1)S(1)} %reshape.13.refs_3_), channel_id=1, source_target_pairs={{0,1},{1,2},{2,3},{3,4},{4,5},{5,6},{6,7},{7,0},{8,15},{9,8},{10,9... | collective-permute-start | bytes 688136 | tf_op jit(solution)/shard_map/ppermute | solution.py:237
  27.1 17.6 %collective-permute-start.3 = (bf16[16,7168]{1,0:T(8,128)(2,1)S(1)}, bf16[16,7168]{1,0:T(8,128)(2,1)S(1)}, u32[]{:S(2)}, u32[]{:S(2)}) collective-permute-start(bf16[16,7168]{1,0:T(8,128)(2,1)S(1)} %reshape.13.refs_3_), channel_id=1, source_target_pairs={{0,7},{1,0},{2,1},{3,2},{4,3},{5,4},{6,5},{7,6},{8,9},{9,10},{10,1... | collective-permute-start | bytes 688136 | tf_op jit(solution)/shard_map/ppermute | solution.py:237
  29.0 15.6 %collective-permute-start.5 = (bf16[16,7168]{1,0:T(8,128)(2,1)S(1)}, bf16[16,7168]{1,0:T(8,128)(2,1)S(1)}, u32[]{:S(2)}, u32[]{:S(2)}) collective-permute-start(bf16[16,7168]{1,0:T(8,128)(2,1)S(1)} %collective-permute-done.4.refs_5_), channel_id=1, source_target_pairs={{0,7},{1,0},{2,1},{3,2},{4,3},{5,4},{6,5},{7,6},{8,9},{9,10},{10,1... | collective-permute-start | bytes 688136 | tf_op jit(solution)/shard_map/ppermute | solution.py:237
  34.3 13.0 %collective-permute-start.6 = (bf16[16,7168]{1,0:T(8,128)(2,1)S(1)}, bf16[16,7168]{1,0:T(8,128)(2,1)S(1)}, u32[]{:S(2)}, u32[]{:S(2)}) collective-permute-start(bf16[16,7168]{1,0:T(8,128)(2,1)S(1)} %collective-permute-done.refs_1_), channel_id=1, source_target_pairs={{0,2},{1,3},{2,4},{3,5},{4,6},{5,7},{6,0},{7,1},{8,14},{9,15},{10,... | collective-permute-start | bytes 688136 | tf_op jit(solution)/shard_map/ppermute | solution.py:237
  38.5 10.3 %collective-permute-start.1 = (bf16[16,7168]{1,0:T(8,128)(2,1)S(1)}, bf16[16,7168]{1,0:T(8,128)(2,1)S(1)}, u32[]{:S(2)}, u32[]{:S(2)}) collective-permute-start(bf16[16,7168]{1,0:T(8,128)(2,1)S(1)} %collective-permute-done.refs_1_), channel_id=1, source_target_pairs={{0,1},{1,2},{2,3},{3,4},{4,5},{5,6},{6,7},{7,0},{8,15},{9,8},{10,9... | collective-permute-start | bytes 688136 | tf_op jit(solution)/shard_map/ppermute | solution.py:237
  42.9 1.5 %copy-start.1 = (bf16[1,128,7168]{2,1,0:T(8,128)(2,1)S(1)}, bf16[1,128,7168]{2,1,0:T(8,128)(2,1)}, u32[]{:S(2)}) copy-start(bf16[1,128,7168]{2,1,0:T(8,128)(2,1)} %param.13) | copy-start | bytes 5505028
  44.4 4.4 %copy-start.2 = (bf16[1,7168,128]{2,1,0:T(8,128)(2,1)S(1)}, bf16[1,7168,128]{2,1,0:T(8,128)(2,1)}, u32[]{:S(2)}) copy-start(bf16[1,7168,128]{2,1,0:T(8,128)(2,1)} %param.11) | copy-start | bytes 5505028
  44.4 4.4 %copy-start.3 = (bf16[16,384]{1,0:T(8,128)(2,1)S(1)}, bf16[16,384]{1,0:T(8,128)(2,1)}, u32[]{:S(2)}) copy-start(bf16[16,384]{1,0:T(8,128)(2,1)} %get-tuple-element.20.refs_11_) | copy-start | bytes 36868
  50.5 22.2 %collective-permute-start.10 = (bf16[16,7168]{1,0:T(8,128)(2,1)S(1)}, bf16[16,7168]{1,0:T(8,128)(2,1)S(1)}, u32[]{:S(2)}, u32[]{:S(2)}) collective-permute-start(bf16[16,7168]{1,0:T(8,128)(2,1)S(1)} %get-tuple-element.25), channel_id=1, source_target_pairs={{0,2},{1,3},{2,4},{3,5},{4,6},{5,7},{6,0},{7,1},{8,14},{9,15},{10,... | collective-permute-start | bytes 688136 | tf_op jit(solution)/shard_map/ppermute | solution.py:237
  54.9 21.6 %collective-permute-start.11 = (bf16[16,7168]{1,0:T(8,128)(2,1)S(1)}, bf16[16,7168]{1,0:T(8,128)(2,1)S(1)}, u32[]{:S(2)}, u32[]{:S(2)}) collective-permute-start(bf16[16,7168]{1,0:T(8,128)(2,1)S(1)} %get-tuple-element.26), channel_id=1, source_target_pairs={{0,1},{1,2},{2,3},{3,4},{4,5},{5,6},{6,7},{7,0},{8,15},{9,8},{10,9... | collective-permute-start | bytes 688136 | tf_op jit(solution)/shard_map/ppermute | solution.py:237
  59.5 22.3 %collective-permute-start.13 = (bf16[16,7168]{1,0:T(8,128)(2,1)S(1)}, bf16[16,7168]{1,0:T(8,128)(2,1)S(1)}, u32[]{:S(2)}, u32[]{:S(2)}) collective-permute-start(bf16[16,7168]{1,0:T(8,128)(2,1)S(1)} %get-tuple-element.28), channel_id=1, source_target_pairs={{0,7},{1,0},{2,1},{3,2},{4,3},{5,4},{6,5},{7,6},{8,9},{9,10},{10,1... | collective-permute-start | bytes 688136 | tf_op jit(solution)/shard_map/ppermute | solution.py:237
  61.5 28.0 %collective-permute-start.7 = (bf16[16,7552]{1,0:T(8,128)(2,1)S(1)}, bf16[16,7552]{1,0:T(8,128)(2,1)S(1)}, u32[]{:S(2)}, u32[]{:S(2)}) collective-permute-start(bf16[16,7552]{1,0:T(8,128)(2,1)S(1)} %get-tuple-element.21), channel_id=1, source_target_pairs={{0,64},{1,65},{2,66},{3,67},{4,68},{5,69},{6,70},{7,71},{8,72},{9,... | collective-permute-start | bytes 725000 | tf_op jit(solution)/shard_map/ppermute | solution.py:237
  67.0 22.5 %collective-permute-start.8 = (bf16[16,7168]{1,0:T(8,128)(2,1)S(1)}, bf16[16,7168]{1,0:T(8,128)(2,1)S(1)}, u32[]{:S(2)}, u32[]{:S(2)}) collective-permute-start(bf16[16,7168]{1,0:T(8,128)(2,1)S(1)} %get-tuple-element.22), channel_id=1, source_target_pairs={{0,65},{1,66},{2,67},{3,68},{4,69},{5,70},{6,71},{7,64},{8,79},{9,... | collective-permute-start | bytes 688136 | tf_op jit(solution)/shard_map/ppermute | solution.py:237
  72.7 16.7 %collective-permute-start.9 = (bf16[16,7168]{1,0:T(8,128)(2,1)S(1)}, bf16[16,7168]{1,0:T(8,128)(2,1)S(1)}, u32[]{:S(2)}, u32[]{:S(2)}) collective-permute-start(bf16[16,7168]{1,0:T(8,128)(2,1)S(1)} %get-tuple-element.23), channel_id=1, source_target_pairs={{0,71},{1,64},{2,65},{3,66},{4,67},{5,68},{6,69},{7,70},{8,73},{9,... | collective-permute-start | bytes 688136 | tf_op jit(solution)/shard_map/ppermute | solution.py:237
  76.6 13.4 %collective-permute-start.12 = (bf16[16,7168]{1,0:T(8,128)(2,1)S(1)}, bf16[16,7168]{1,0:T(8,128)(2,1)S(1)}, u32[]{:S(2)}, u32[]{:S(2)}) collective-permute-start(bf16[16,7168]{1,0:T(8,128)(2,1)S(1)} %plus.3), channel_id=1, source_target_pairs={{0,66},{1,67},{2,68},{3,69},{4,70},{5,71},{6,64},{7,65},{8,78},{9,... | collective-permute-start | bytes 688136 | tf_op jit(solution)/shard_map/ppermute | solution.py:237
  81.9 17.6 %collective-permute-start.14 = (bf16[16,7168]{1,0:T(8,128)(2,1)S(1)}, bf16[16,7168]{1,0:T(8,128)(2,1)S(1)}, u32[]{:S(2)}, u32[]{:S(2)}) collective-permute-start(bf16[16,7168]{1,0:T(8,128)(2,1)S(1)} %plus.4), channel_id=1, source_target_pairs={{0,70},{1,71},{2,64},{3,65},{4,66},{5,67},{6,68},{7,69},{8,74},{9,... | collective-permute-start | bytes 688136 | tf_op jit(solution)/shard_map/ppermute | solution.py:237

commit v5 on v4

--- a/solution.py
+++ b/solution.py
@@ -27,7 +27,7 @@
     table_ref, routes_hbm, gates_hbm, tokens_hbm, rows_ref, combine_ref, routes_ref, gates_ref, tokens_ref, arrived
 ):
     slots = table_ref.shape[0]
-    rows_dev = rows_ref.shape[0]
+    rows_dev = combine_ref.shape[0]
     tok_dev, width = tokens_ref.shape
     starts = range(0, width, PIECE)
     small = [
@@ -82,9 +82,8 @@
     for copy, c in zip(pieces, starts):
         copy.wait()
         cols = slice(c, min(c + PIECE, width))
-        rows_ref[:, cols] = jnp.dot(
-            select, tokens_ref[:, cols], preferred_element_type=jnp.float32
-        ).astype(jnp.bfloat16)
+        rows = jnp.dot(select, tokens_ref[:, cols], preferred_element_type=jnp.float32)
+        rows_ref[:, :, cols] = rows.reshape(slots, CAP, rows.shape[1]).astype(jnp.bfloat16)
 
 
 def pick_rows(table, picks, gates, tokens, rows_dev):
@@ -92,7 +91,7 @@
     return pl.pallas_call(
         pick_kernel,
         out_shape=(
-            jax.ShapeDtypeStruct((rows_dev, width), jnp.bfloat16),
+            jax.ShapeDtypeStruct((rows_dev // CAP, CAP, width), jnp.bfloat16),
             jax.ShapeDtypeStruct((rows_dev, SPLIT * LANES), jnp.bfloat16),
         ),
         in_specs=[pl.BlockSpec(memory_space=pltpu.SMEM), HBM, HBM, HBM],
@@ -174,15 +173,17 @@
 
 def plus_kernel(*refs):
     out_ref = refs[-1]
-    width = out_ref.shape[1]
+    width = min(ref.shape[1] for ref in refs)
     total = refs[0][:, :width].astype(jnp.float32)
     for ref in refs[1:-1]:
         total = total + ref[:, :width].astype(jnp.float32)
-    out_ref[...] = total.astype(jnp.bfloat16)
-
-
-def plus(*terms):
-    shape = terms[-1].shape
+    out_ref[:, :width] = total.astype(jnp.bfloat16)
+    if out_ref.shape[1] > width:
+        out_ref[:, width:] = refs[0][:, width:]
+
+
+def plus(*terms, width=None):
+    shape = (terms[0].shape[0], width or terms[0].shape[1])
     size = shape[0] * shape[1]
     return pl.pallas_call(
         plus_kernel,
@@ -243,9 +244,9 @@
     rows_dev = n_node * CAP
     width = tokens.shape[2]
     outgoing, tail = pick_rows(replica_table, routes[0].T, route_gates[0].T, tokens[0], rows_dev)
-    own = lax.all_to_all(
-        outgoing.reshape(n_node, CAP, width), "node", split_axis=0, concat_axis=0, tiled=True
-    ).reshape(rows_dev, width)
+    own = lax.all_to_all(outgoing, "node", split_axis=0, concat_axis=0, tiled=True).reshape(
+        rows_dev, width
+    )
     blocks = {0: own}
     blocks[-2], blocks[2] = hop(own, 2), hop(own, -2)
     blocks[-1], blocks[1] = hop(own, 1), hop(own, -1)
@@ -253,15 +254,14 @@
     blocks[-3], blocks[3] = hop(blocks[-2], 1), hop(blocks[2], -1)
     order = sorted(blocks)
     up_mat, down_mat = load([w_up[0], w_down[0]], blocks[-1])
-    parts = experts(
-        [blocks[q] for q in order], w_gate[0], up_mat, down_mat, tail, order.index(0)
-    )
+    parts = experts([blocks[q] for q in order], w_gate[0], up_mat, down_mat, tail, order.index(0))
     part = dict(zip(order, parts))
     ahead = plus(part[2], hop(part[far], 2), hop(part[3], 1))
     back = plus(part[-2], hop(part[-3], -1))
-    carrier = hop(part[0], 0, 1)
-    near = [hop(part[1], 1, 1), hop(part[-1], -1, 1)]
-    expert_out = plus(carrier, *near, hop(ahead, 2, 1), hop(back, -2, 1))
+    middle = plus(part[0], hop(part[1], 1), hop(part[-1], -1))
+    ahead, back = hop(ahead, 2, 1), hop(back, -2, 1)
+    carrier = hop(middle, 0, 1)
+    expert_out = plus(carrier, ahead, back, width=width)
     returned = lax.all_to_all(
         expert_out.reshape(n_node, CAP, width), "node", split_axis=0, concat_axis=0, tiled=True
     ).reshape(rows_dev, width)

time: 113 us -> 109 us (0.965)
  the two profiles are of different devices: /device:TPU:200 before, /device:TPU:64 now
where the time goes in v5:
time: 109 us; the launch traced here: 108 us
  starting transfers between devices  57 us (52%)
  blocking collectives  21 us (19%)
  waiting for transfers between devices  20.2 us (19%)
  Pallas kernels  8.09 us (7%)
  local copies, waits for them, and re-layouts  1.77 us (2%)
    ppermute x15, starting transfers between devices, hop(): return lax.ppermute(block, ('section', 'node', 'local'), pairs)  57 us
    ppermute x15, waiting for transfers between devices, hop(): return lax.ppermute(block, ('section', 'node', 'local'), pairs)  20.2 us
    all_to_all x1, blocking collectives, shards(): lax.all_to_all(outgoing, 'node', split_axis=0, concat_axis=0, tiled=True)  11.5 us
    all_to_all x1, blocking collectives, shards(): lax.all_to_all(expert_out.reshape(n_node, CAP, width), 'node', split_axis...  9.56 us
    pallas_call x1, Pallas kernels, pick_rows(): pl.pallas_call(pick_kernel, out_shape=(jax.ShapeDtypeStruct((rows_dev //...  3.31 us
    pallas_call x1, Pallas kernels, combine_rows(): pl.pallas_call(combine_kernel, grid=(4,), out_shape=jax.ShapeDtypeStruct(...  2.45 us
  transfers between devices with their start and end apart: 15, of which 6 were waited for; matrix products, arithmetic and copies ran while one was open for 0% of the time, Pallas kernels for 0%

profile of v5, /device:TPU:64, one launch (start us, length us, event | category | flops | bytes accessed | tf_op | source)
XLA Modules:
  0.0 108.4 jit_solution(16056349655590001497)
XLA Ops:
  0.0 0.0 copy-start
  0.0 3.3 %pick_rows.1 = (bf16[8,2,7168]{2,1,0:T(2,128)(2,1)}, bf16[16,384]{1,0:T(8,128)(2,1)}) custom-call(s32[8]{0:T(128)} %table_ref.1, s32[8,96]{1,0:T(8,128)} %bitcast.15, f32[8,96]{1,0:T(8,128)} %bitcast.16, bf16[96,7168]{1,0:T(8,128)(2,1)} %bitcast.14), custom_call_target="tpu_custom_call" | custom-call | flops 22020096 | bytes 1605632 | tf_op jit(solution)/shard_map/pick_rows/pallas_call | solution.py:91
  3.3 11.5 %all_to_all.10 = bf16[8,2,7168]{2,1,0:T(2,128)(2,1)S(1)} all-to-all(bf16[8,2,7168]{2,1,0:T(2,128)(2,1)} %get-tuple-element.17), channel_id=1, replica_groups=mesh['section'=16,'node'=8,'local'=8] {'node'}, dimensions={0} | all-to-all | bytes 458752 | tf_op jit(solution)/shard_map/all_to_all | solution.py:247
  14.8 0.1 reshape.9.refs_3_
  14.9 6.2 %collective-permute-start.4 = (bf16[16,7168]{1,0:T(8,128)(2,1)S(1)}, bf16[16,7168]{1,0:T(8,128)(2,1)S(1)}, u32[]{:S(2)}, u32[]{:S(2)}) collective-permute-start(bf16[16,7168]{1,0:T(8,128)(2,1)S(1)} %reshape.9.refs_3_), channel_id=1, source_target_pairs={{0,6},{1,7},{2,0},{3,1},{4,2},{5,3},{6,4},{7,5},{8,10},{9,11},{10,... | collective-permute-start | bytes 688136 | tf_op jit(solution)/shard_map/ppermute | solution.py:238
  21.0 1.9 %collective-permute-start = (bf16[16,7168]{1,0:T(8,128)(2,1)S(1)}, bf16[16,7168]{1,0:T(8,128)(2,1)S(1)}, u32[]{:S(2)}, u32[]{:S(2)}) collective-permute-start(bf16[16,7168]{1,0:T(8,128)(2,1)S(1)} %reshape.9.refs_3_), channel_id=1, source_target_pairs={{0,2},{1,3},{2,4},{3,5},{4,6},{5,7},{6,0},{7,1},{8,14},{9,15},{10,... | collective-permute-start | bytes 688136 | tf_op jit(solution)/shard_map/ppermute | solution.py:238
  23.0 2.6 %collective-permute-start.2 = (bf16[16,7168]{1,0:T(8,128)(2,1)S(1)}, bf16[16,7168]{1,0:T(8,128)(2,1)S(1)}, u32[]{:S(2)}, u32[]{:S(2)}) collective-permute-start(bf16[16,7168]{1,0:T(8,128)(2,1)S(1)} %reshape.9.refs_3_), channel_id=1, source_target_pairs={{0,1},{1,2},{2,3},{3,4},{4,5},{5,6},{6,7},{7,0},{8,15},{9,8},{10,9... | collective-permute-start | bytes 688136 | tf_op jit(solution)/shard_map/ppermute | solution.py:238
  25.6 4.6 %collective-permute-start.3 = (bf16[16,7168]{1,0:T(8,128)(2,1)S(1)}, bf16[16,7168]{1,0:T(8,128)(2,1)S(1)}, u32[]{:S(2)}, u32[]{:S(2)}) collective-permute-start(bf16[16,7168]{1,0:T(8,128)(2,1)S(1)} %reshape.9.refs_3_), channel_id=1, source_target_pairs={{0,7},{1,0},{2,1},{3,2},{4,3},{5,4},{6,5},{7,6},{8,9},{9,10},{10,1... | collective-permute-start | bytes 688136 | tf_op jit(solution)/shard_map/ppermute | solution.py:238
  30.2 1.1 collective-permute-done.4.refs_5_
  31.2 2.9 %collective-permute-start.5 = (bf16[16,7168]{1,0:T(8,128)(2,1)S(1)}, bf16[16,7168]{1,0:T(8,128)(2,1)S(1)}, u32[]{:S(2)}, u32[]{:S(2)}) collective-permute-start(bf16[16,7168]{1,0:T(8,128)(2,1)S(1)} %collective-permute-done.4.refs_5_), channel_id=1, source_target_pairs={{0,7},{1,0},{2,1},{3,2},{4,3},{5,4},{6,5},{7,6},{8,9},{9,10},{10,1... | collective-permute-start | bytes 688136 | tf_op jit(solution)/shard_map/ppermute | solution.py:238
  34.1 0.0 collective-permute-done.refs_1_
  34.1 3.2 %collective-permute-start.6 = (bf16[16,7168]{1,0:T(8,128)(2,1)S(1)}, bf16[16,7168]{1,0:T(8,128)(2,1)S(1)}, u32[]{:S(2)}, u32[]{:S(2)}) collective-permute-start(bf16[16,7168]{1,0:T(8,128)(2,1)S(1)} %collective-permute-done.refs_1_), channel_id=1, source_target_pairs={{0,2},{1,3},{2,4},{3,5},{4,6},{5,7},{6,0},{7,1},{8,14},{9,15},{10,... | collective-permute-start | bytes 688136 | tf_op jit(solution)/shard_map/ppermute | solution.py:238
  37.3 3.9 %collective-permute-start.1 = (bf16[16,7168]{1,0:T(8,128)(2,1)S(1)}, bf16[16,7168]{1,0:T(8,128)(2,1)S(1)}, u32[]{:S(2)}, u32[]{:S(2)}) collective-permute-start(bf16[16,7168]{1,0:T(8,128)(2,1)S(1)} %collective-permute-done.refs_1_), channel_id=1, source_target_pairs={{0,1},{1,2},{2,3},{3,4},{4,5},{5,6},{6,7},{7,0},{8,15},{9,8},{10,9... | collective-permute-start | bytes 688136 | tf_op jit(solution)/shard_map/ppermute | solution.py:238
  41.2 0.0 collective-permute-done.2.refs_2_
  41.2 0.0 copy-done
  41.2 0.0 copy-start.1
  41.2 1.5 %copy-done.1 = bf16[1,128,7168]{2,1,0:T(8,128)(2,1)S(1)} copy-done((bf16[1,128,7168]{2,1,0:T(8,128)(2,1)S(1)}, bf16[1,128,7168]{2,1,0:T(8,128)(2,1)}, u32[]{:S(2)}) %copy-start.1) | copy-done | bytes 1835032
  42.7 0.0 copy-start.2
  42.7 0.0 copy-start.3
  42.7 0.3 load.1
  43.0 0.0 collective-permute-done.3.refs_4_
  43.0 0.0 collective-permute-done.5.refs_6_
  43.0 1.2 %collective-permute-done.6.refs_7_ = bf16[16,7168]{1,0:T(8,128)(2,1)S(1)} collective-permute-done((bf16[16,7168]{1,0:T(8,128)(2,1)S(1)}, bf16[16,7168]{1,0:T(8,128)(2,1)S(1)}, u32[]{:S(2)}, u32[]{:S(2)}) %collective-permute-start.6) | collective-permute-done | bytes 229408 | tf_op jit(solution)/shard_map/ppermute | solution.py:238
  44.2 4.9 %collective-permute-done.1.refs_0_ = bf16[16,7168]{1,0:T(8,128)(2,1)S(1)} collective-permute-done((bf16[16,7168]{1,0:T(8,128)(2,1)S(1)}, bf16[16,7168]{1,0:T(8,128)(2,1)S(1)}, u32[]{:S(2)}, u32[]{:S(2)}) %collective-permute-start.1) | collective-permute-done | bytes 229408 | tf_op jit(solution)/shard_map/ppermute | solution.py:238
  49.1 0.0 copy-done.2
  49.1 0.0 copy-done.3
  49.1 1.8 %experts.1 = (bf16[16,7168]{1,0:T(8,128)(2,1)S(1)}, bf16[16,7168]{1,0:T(8,128)(2,1)S(1)}, bf16[16,7168]{1,0:T(8,128)(2,1)S(1)}, bf16[16,7552]{1,0:T(8,128)(2,1)S...) custom-call(bf16[16,7168]{1,0:T(8,128)(2,1)S(1)} %collective-permute, ...), custom_call_target="tpu_custom_call" | custom-call | flops 704643072 | bytes 5505024 | tf_op jit(solution)/shard_map/experts/pallas_call | solution.py:163
  50.9 2.4 %collective-permute-start.7 = (bf16[16,7168]{1,0:T(8,128)(2,1)S(1)}, bf16[16,7168]{1,0:T(8,128)(2,1)S(1)}, u32[]{:S(2)}, u32[]{:S(2)}) collective-permute-start(bf16[16,7168]{1,0:T(8,128)(2,1)S(1)} %get-tuple-element.22), channel_id=1, source_target_pairs={{0,1},{1,2},{2,3},{3,4},{4,5},{5,6},{6,7},{7,0},{8,15},{9,8},{10,9... | collective-permute-start | bytes 688136 | tf_op jit(solution)/shard_map/ppermute | solution.py:238
  53.2 4.7 %collective-permute-start.8 = (bf16[16,7168]{1,0:T(8,128)(2,1)S(1)}, bf16[16,7168]{1,0:T(8,128)(2,1)S(1)}, u32[]{:S(2)}, u32[]{:S(2)}) collective-permute-start(bf16[16,7168]{1,0:T(8,128)(2,1)S(1)} %get-tuple-element.23), channel_id=1, source_target_pairs={{0,7},{1,0},{2,1},{3,2},{4,3},{5,4},{6,5},{7,6},{8,9},{9,10},{10,1... | collective-permute-start | bytes 688136 | tf_op jit(solution)/shard_map/ppermute | solution.py:238
  57.9 1.9 %collective-permute-start.10 = (bf16[16,7168]{1,0:T(8,128)(2,1)S(1)}, bf16[16,7168]{1,0:T(8,128)(2,1)S(1)}, u32[]{:S(2)}, u32[]{:S(2)}) collective-permute-start(bf16[16,7168]{1,0:T(8,128)(2,1)S(1)} %get-tuple-element.25), channel_id=1, source_target_pairs={{0,2},{1,3},{2,4},{3,5},{4,6},{5,7},{6,0},{7,1},{8,14},{9,15},{10,... | collective-permute-start | bytes 688136 | tf_op jit(solution)/shard_map/ppermute | solution.py:238
  59.9 4.3 %collective-permute-start.11 = (bf16[16,7168]{1,0:T(8,128)(2,1)S(1)}, bf16[16,7168]{1,0:T(8,128)(2,1)S(1)}, u32[]{:S(2)}, u32[]{:S(2)}) collective-permute-start(bf16[16,7168]{1,0:T(8,128)(2,1)S(1)} %get-tuple-element.26), channel_id=1, source_target_pairs={{0,1},{1,2},{2,3},{3,4},{4,5},{5,6},{6,7},{7,0},{8,15},{9,8},{10,9... | collective-permute-start | bytes 688136 | tf_op jit(solution)/shard_map/ppermute | solution.py:238
  64.2 2.7 %collective-permute-start.13 = (bf16[16,7168]{1,0:T(8,128)(2,1)S(1)}, bf16[16,7168]{1,0:T(8,128)(2,1)S(1)}, u32[]{:S(2)}, u32[]{:S(2)}) collective-permute-start(bf16[16,7168]{1,0:T(8,128)(2,1)S(1)} %get-tuple-element.28), channel_id=1, source_target_pairs={{0,7},{1,0},{2,1},{3,2},{4,3},{5,4},{6,5},{7,6},{8,9},{9,10},{10,1... | collective-permute-start | bytes 688136 | tf_op jit(solution)/shard_map/ppermute | solution.py:238
  66.9 0.0 collective-permute-done.7.refs_1_
  66.9 0.0 collective-permute-done.8.refs_2_
  67.0 0.1 plus.4
  67.1 4.3 %collective-permute-start.9 = (bf16[16,7552]{1,0:T(8,128)(2,1)S(1)}, bf16[16,7552]{1,0:T(8,128)(2,1)S(1)}, u32[]{:S(2)}, u32[]{:S(2)}) collective-permute-start(bf16[16,7552]{1,0:T(8,128)(2,1)S(1)} %plus.4), channel_id=1, source_target_pairs={{0,64},{1,65},{2,66},{3,67},{4,68},{5,69},{6,70},{7,71},{8,72},{9,... | collective-permute-start | bytes 725000 | tf_op jit(solution)/shard_map/ppermute | solution.py:238
  71.3 0.0 collective-permute-done.10.refs_1_
  71.3 1.5 %collective-permute-done.11.refs_2_ = bf16[16,7168]{1,0:T(8,128)(2,1)S(1)} collective-permute-done((bf16[16,7168]{1,0:T(8,128)(2,1)S(1)}, bf16[16,7168]{1,0:T(8,128)(2,1)S(1)}, u32[]{:S(2)}, u32[]{:S(2)}) %collective-permute-start.11) | collective-permute-done | bytes 229408 | tf_op jit(solution)/shard_map/ppermute | solution.py:238
  72.9 0.1 plus.5
  73.0 6.1 %collective-permute-start.12 = (bf16[16,7168]{1,0:T(8,128)(2,1)S(1)}, bf16[16,7168]{1,0:T(8,128)(2,1)S(1)}, u32[]{:S(2)}, u32[]{:S(2)}) collective-permute-start(bf16[16,7168]{1,0:T(8,128)(2,1)S(1)} %plus.5), channel_id=1, source_target_pairs={{0,66},{1,67},{2,68},{3,69},{4,70},{5,71},{6,64},{7,65},{8,78},{9,... | collective-permute-start | bytes 688136 | tf_op jit(solution)/shard_map/ppermute | solution.py:238
  79.1 0.0 collective-permute-done.13.refs_1_
  79.1 0.1 plus.6
  79.1 5.5 %collective-permute-start.14 = (bf16[16,7168]{1,0:T(8,128)(2,1)S(1)}, bf16[16,7168]{1,0:T(8,128)(2,1)S(1)}, u32[]{:S(2)}, u32[]{:S(2)}) collective-permute-start(bf16[16,7168]{1,0:T(8,128)(2,1)S(1)} %plus.6), channel_id=1, source_target_pairs={{0,70},{1,71},{2,64},{3,65},{4,66},{5,67},{6,68},{7,69},{8,74},{9,... | collective-permute-start | bytes 688136 | tf_op jit(solution)/shard_map/ppermute | solution.py:238
  84.6 10.3 %collective-permute-done.12.refs_1_ = bf16[16,7168]{1,0:T(8,128)(2,1)S(1)} collective-permute-done((bf16[16,7168]{1,0:T(8,128)(2,1)S(1)}, bf16[16,7168]{1,0:T(8,128)(2,1)S(1)}, u32[]{:S(2)}, u32[]{:S(2)}) %collective-permute-start.12) | collective-permute-done | bytes 229408 | tf_op jit(solution)/shard_map/ppermute | solution.py:238
  94.9 1.2 %collective-permute-done.14.refs_2_ = bf16[16,7168]{1,0:T(8,128)(2,1)S(1)} collective-permute-done((bf16[16,7168]{1,0:T(8,128)(2,1)S(1)}, bf16[16,7168]{1,0:T(8,128)(2,1)S(1)}, u32[]{:S(2)}, u32[]{:S(2)}) %collective-permute-start.14) | collective-permute-done | bytes 229408 | tf_op jit(solution)/shard_map/ppermute | solution.py:238
  96.1 0.0 collective-permute-done.9.refs_0_.refs_1_.refs_2_
  96.1 0.1 plus.7
  96.2 0.1 reshape.10
  96.3 9.6 %all_to_all.11 = bf16[8,2,7168]{2,1,0:T(2,128)(2,1)S(1)} all-to-all(bf16[8,2,7168]{2,1,0:T(2,128)(2,1)S(1)} %reshape.10), channel_id=1, replica_groups=mesh['section'=16,'node'=8,'local'=8] {'node'}, dimensions={0} | all-to-all | bytes 458752 | tf_op jit(solution)/shard_map/all_to_all | solution.py:265
  105.8 0.1 reshape.11.refs_3_
  105.9 2.5 %combine_rows.1 = bf16[96,7168]{1,0:T(8,128)(2,1)} custom-call(bf16[16,7552]{1,0:T(8,128)(2,1)S(1)} %collective-permute-done.9.refs_0_.refs_1_.refs_2_, bf16[16,7552]{1,0:T(8,128)(2,1)S(1)} %collective-permute-done.9.refs_0_.refs_1_.refs_2_, bf16[16,7552]{1,0:T(8,128)(2,1)S(1)} %collective-permute-done.9.refs_0_.refs_1_.refs_2_, ...), custom_call_target="tpu_custom_call" | custom-call | flops 66060288 | bytes 1605632 | tf_op jit(solution)/shard_map/combine_rows/pallas_call | solution.py:215
Async XLA Ops:
  0.0 41.2 %copy-start = (bf16[1,7168,128]{2,1,0:T(8,128)(2,1)S(1)}, bf16[1,7168,128]{2,1,0:T(8,128)(2,1)}, u32[]{:S(2)}) copy-start(bf16[1,7168,128]{2,1,0:T(8,128)(2,1)} %param.12) | copy-start | bytes 5505028
  14.9 16.4 %collective-permute-start.4 = (bf16[16,7168]{1,0:T(8,128)(2,1)S(1)}, bf16[16,7168]{1,0:T(8,128)(2,1)S(1)}, u32[]{:S(2)}, u32[]{:S(2)}) collective-permute-start(bf16[16,7168]{1,0:T(8,128)(2,1)S(1)} %reshape.9.refs_3_), channel_id=1, source_target_pairs={{0,6},{1,7},{2,0},{3,1},{4,2},{5,3},{6,4},{7,5},{8,10},{9,11},{10,... | collective-permute-start | bytes 688136 | tf_op jit(solution)/shard_map/ppermute | solution.py:238
  21.0 13.1 %collective-permute-start = (bf16[16,7168]{1,0:T(8,128)(2,1)S(1)}, bf16[16,7168]{1,0:T(8,128)(2,1)S(1)}, u32[]{:S(2)}, u32[]{:S(2)}) collective-permute-start(bf16[16,7168]{1,0:T(8,128)(2,1)S(1)} %reshape.9.refs_3_), channel_id=1, source_target_pairs={{0,2},{1,3},{2,4},{3,5},{4,6},{5,7},{6,0},{7,1},{8,14},{9,15},{10,... | collective-permute-start | bytes 688136 | tf_op jit(solution)/shard_map/ppermute | solution.py:238
  23.0 18.2 %collective-permute-start.2 = (bf16[16,7168]{1,0:T(8,128)(2,1)S(1)}, bf16[16,7168]{1,0:T(8,128)(2,1)S(1)}, u32[]{:S(2)}, u32[]{:S(2)}) collective-permute-start(bf16[16,7168]{1,0:T(8,128)(2,1)S(1)} %reshape.9.refs_3_), channel_id=1, source_target_pairs={{0,1},{1,2},{2,3},{3,4},{4,5},{5,6},{6,7},{7,0},{8,15},{9,8},{10,9... | collective-permute-start | bytes 688136 | tf_op jit(solution)/shard_map/ppermute | solution.py:238
  25.6 17.4 %collective-permute-start.3 = (bf16[16,7168]{1,0:T(8,128)(2,1)S(1)}, bf16[16,7168]{1,0:T(8,128)(2,1)S(1)}, u32[]{:S(2)}, u32[]{:S(2)}) collective-permute-start(bf16[16,7168]{1,0:T(8,128)(2,1)S(1)} %reshape.9.refs_3_), channel_id=1, source_target_pairs={{0,7},{1,0},{2,1},{3,2},{4,3},{5,4},{6,5},{7,6},{8,9},{9,10},{10,1... | collective-permute-start | bytes 688136 | tf_op jit(solution)/shard_map/ppermute | solution.py:238
  31.2 11.8 %collective-permute-start.5 = (bf16[16,7168]{1,0:T(8,128)(2,1)S(1)}, bf16[16,7168]{1,0:T(8,128)(2,1)S(1)}, u32[]{:S(2)}, u32[]{:S(2)}) collective-permute-start(bf16[16,7168]{1,0:T(8,128)(2,1)S(1)} %collective-permute-done.4.refs_5_), channel_id=1, source_target_pairs={{0,7},{1,0},{2,1},{3,2},{4,3},{5,4},{6,5},{7,6},{8,9},{9,10},{10,1... | collective-permute-start | bytes 688136 | tf_op jit(solution)/shard_map/ppermute | solution.py:238
  34.1 10.1 %collective-permute-start.6 = (bf16[16,7168]{1,0:T(8,128)(2,1)S(1)}, bf16[16,7168]{1,0:T(8,128)(2,1)S(1)}, u32[]{:S(2)}, u32[]{:S(2)}) collective-permute-start(bf16[16,7168]{1,0:T(8,128)(2,1)S(1)} %collective-permute-done.refs_1_), channel_id=1, source_target_pairs={{0,2},{1,3},{2,4},{3,5},{4,6},{5,7},{6,0},{7,1},{8,14},{9,15},{10,... | collective-permute-start | bytes 688136 | tf_op jit(solution)/shard_map/ppermute | solution.py:238
  37.3 11.8 %collective-permute-start.1 = (bf16[16,7168]{1,0:T(8,128)(2,1)S(1)}, bf16[16,7168]{1,0:T(8,128)(2,1)S(1)}, u32[]{:S(2)}, u32[]{:S(2)}) collective-permute-start(bf16[16,7168]{1,0:T(8,128)(2,1)S(1)} %collective-permute-done.refs_1_), channel_id=1, source_target_pairs={{0,1},{1,2},{2,3},{3,4},{4,5},{5,6},{6,7},{7,0},{8,15},{9,8},{10,9... | collective-permute-start | bytes 688136 | tf_op jit(solution)/shard_map/ppermute | solution.py:238
  41.2 1.5 %copy-start.1 = (bf16[1,128,7168]{2,1,0:T(8,128)(2,1)S(1)}, bf16[1,128,7168]{2,1,0:T(8,128)(2,1)}, u32[]{:S(2)}) copy-start(bf16[1,128,7168]{2,1,0:T(8,128)(2,1)} %param.13) | copy-start | bytes 5505028
  42.7 6.4 %copy-start.2 = (bf16[1,7168,128]{2,1,0:T(8,128)(2,1)S(1)}, bf16[1,7168,128]{2,1,0:T(8,128)(2,1)}, u32[]{:S(2)}) copy-start(bf16[1,7168,128]{2,1,0:T(8,128)(2,1)} %param.11) | copy-start | bytes 5505028
  42.7 6.4 %copy-start.3 = (bf16[16,384]{1,0:T(8,128)(2,1)S(1)}, bf16[16,384]{1,0:T(8,128)(2,1)}, u32[]{:S(2)}) copy-start(bf16[16,384]{1,0:T(8,128)(2,1)} %get-tuple-element.20.refs_11_) | copy-start | bytes 36868
  50.9 16.1 %collective-permute-start.7 = (bf16[16,7168]{1,0:T(8,128)(2,1)S(1)}, bf16[16,7168]{1,0:T(8,128)(2,1)S(1)}, u32[]{:S(2)}, u32[]{:S(2)}) collective-permute-start(bf16[16,7168]{1,0:T(8,128)(2,1)S(1)} %get-tuple-element.22), channel_id=1, source_target_pairs={{0,1},{1,2},{2,3},{3,4},{4,5},{5,6},{6,7},{7,0},{8,15},{9,8},{10,9... | collective-permute-start | bytes 688136 | tf_op jit(solution)/shard_map/ppermute | solution.py:238
  53.2 13.7 %collective-permute-start.8 = (bf16[16,7168]{1,0:T(8,128)(2,1)S(1)}, bf16[16,7168]{1,0:T(8,128)(2,1)S(1)}, u32[]{:S(2)}, u32[]{:S(2)}) collective-permute-start(bf16[16,7168]{1,0:T(8,128)(2,1)S(1)} %get-tuple-element.23), channel_id=1, source_target_pairs={{0,7},{1,0},{2,1},{3,2},{4,3},{5,4},{6,5},{7,6},{8,9},{9,10},{10,1... | collective-permute-start | bytes 688136 | tf_op jit(solution)/shard_map/ppermute | solution.py:238
  57.9 13.4 %collective-permute-start.10 = (bf16[16,7168]{1,0:T(8,128)(2,1)S(1)}, bf16[16,7168]{1,0:T(8,128)(2,1)S(1)}, u32[]{:S(2)}, u32[]{:S(2)}) collective-permute-start(bf16[16,7168]{1,0:T(8,128)(2,1)S(1)} %get-tuple-element.25), channel_id=1, source_target_pairs={{0,2},{1,3},{2,4},{3,5},{4,6},{5,7},{6,0},{7,1},{8,14},{9,15},{10,... | collective-permute-start | bytes 688136 | tf_op jit(solution)/shard_map/ppermute | solution.py:238
  59.9 13.0 %collective-permute-start.11 = (bf16[16,7168]{1,0:T(8,128)(2,1)S(1)}, bf16[16,7168]{1,0:T(8,128)(2,1)S(1)}, u32[]{:S(2)}, u32[]{:S(2)}) collective-permute-start(bf16[16,7168]{1,0:T(8,128)(2,1)S(1)} %get-tuple-element.26), channel_id=1, source_target_pairs={{0,1},{1,2},{2,3},{3,4},{4,5},{5,6},{6,7},{7,0},{8,15},{9,8},{10,9... | collective-permute-start | bytes 688136 | tf_op jit(solution)/shard_map/ppermute | solution.py:238
  64.2 14.8 %collective-permute-start.13 = (bf16[16,7168]{1,0:T(8,128)(2,1)S(1)}, bf16[16,7168]{1,0:T(8,128)(2,1)S(1)}, u32[]{:S(2)}, u32[]{:S(2)}) collective-permute-start(bf16[16,7168]{1,0:T(8,128)(2,1)S(1)} %get-tuple-element.28), channel_id=1, source_target_pairs={{0,7},{1,0},{2,1},{3,2},{4,3},{5,4},{6,5},{7,6},{8,9},{9,10},{10,1... | collective-permute-start | bytes 688136 | tf_op jit(solution)/shard_map/ppermute | solution.py:238
  67.1 29.0 %collective-permute-start.9 = (bf16[16,7552]{1,0:T(8,128)(2,1)S(1)}, bf16[16,7552]{1,0:T(8,128)(2,1)S(1)}, u32[]{:S(2)}, u32[]{:S(2)}) collective-permute-start(bf16[16,7552]{1,0:T(8,128)(2,1)S(1)} %plus.4), channel_id=1, source_target_pairs={{0,64},{1,65},{2,66},{3,67},{4,68},{5,69},{6,70},{7,71},{8,72},{9,... | collective-permute-start | bytes 725000 | tf_op jit(solution)/shard_map/ppermute | solution.py:238
  73.0 21.9 %collective-permute-start.12 = (bf16[16,7168]{1,0:T(8,128)(2,1)S(1)}, bf16[16,7168]{1,0:T(8,128)(2,1)S(1)}, u32[]{:S(2)}, u32[]{:S(2)}) collective-permute-start(bf16[16,7168]{1,0:T(8,128)(2,1)S(1)} %plus.5), channel_id=1, source_target_pairs={{0,66},{1,67},{2,68},{3,69},{4,70},{5,71},{6,64},{7,65},{8,78},{9,... | collective-permute-start | bytes 688136 | tf_op jit(solution)/shard_map/ppermute | solution.py:238
  79.1 17.0 %collective-permute-start.14 = (bf16[16,7168]{1,0:T(8,128)(2,1)S(1)}, bf16[16,7168]{1,0:T(8,128)(2,1)S(1)}, u32[]{:S(2)}, u32[]{:S(2)}) collective-permute-start(bf16[16,7168]{1,0:T(8,128)(2,1)S(1)} %plus.6), channel_id=1, source_target_pairs={{0,70},{1,71},{2,64},{3,65},{4,66},{5,67},{6,68},{7,69},{8,74},{9,... | collective-permute-start | bytes 688136 | tf_op jit(solution)/shard_map/ppermute | solution.py:238

commit v6 on v5

--- a/solution.py
+++ b/solution.py
@@ -10,6 +10,7 @@
 PIECE = 1792
 LANES = 128
 SPLIT = 3
+STAGE = 1024
 VMEM = pl.BlockSpec(memory_space=pltpu.VMEM)
 ANY = pl.BlockSpec(memory_space=pl.ANY)
 HBM = pl.BlockSpec(memory_space=pltpu.HBM)
@@ -196,32 +197,43 @@
     )(*terms)
 
 
-def combine_kernel(*refs):
-    pieces, rows_ref, out_ref = refs[:SPLIT], refs[SPLIT], refs[SPLIT + 1]
-    tok_dev = out_ref.shape[0]
-    split = jnp.concatenate([piece[...] for piece in pieces], axis=0)
-    rows = rows_ref[...]
-    rows = jnp.concatenate([rows] * SPLIT, axis=0)
-    out = lax.dot_general(split, rows, (((0,), (0,)), ((), ())), preferred_element_type=jnp.float32)
-    out_ref[...] = out[:tok_dev].astype(jnp.bfloat16)
+def combine_kernel(carrier_ref, rows_ref, out_hbm, stage_ref, sent):
+    tok_dev, width = stage_ref.shape
+    pieces = [
+        carrier_ref[:, width + k * LANES : width + k * LANES + tok_dev] for k in range(SPLIT)
+    ]
+    split = jnp.concatenate(pieces, axis=0)
+    copies = []
+    for k, c in enumerate(range(0, width, STAGE)):
+        cols = slice(c, min(c + STAGE, width))
+        rows = jnp.concatenate([rows_ref[:, cols]] * SPLIT, axis=0)
+        stage_ref[:, cols] = lax.dot_general(
+            split, rows, (((0,), (0,)), ((), ())), preferred_element_type=jnp.float32
+        ).astype(jnp.bfloat16)
+        span = pl.ds(c, min(STAGE, width - c))
+        copies.append(
+            pltpu.make_async_copy(stage_ref.at[:, span], out_hbm.at[:, span], sent.at[k])
+        )
+        copies[-1].start()
+    for copy in copies:
+        copy.wait()
 
 
 def combine_rows(carrier, rows, tok_dev):
     rows_dev, width = rows.shape
-    block = width // 4
-    tail = [
-        pl.BlockSpec((rows_dev, LANES), lambda j, k=k: (0, width // LANES + k)) for k in range(SPLIT)
-    ]
     return pl.pallas_call(
         combine_kernel,
-        grid=(4,),
         out_shape=jax.ShapeDtypeStruct((tok_dev, width), jnp.bfloat16),
-        in_specs=tail + [pl.BlockSpec((rows_dev, block), lambda j: (0, j))],
-        out_specs=pl.BlockSpec((tok_dev, block), lambda j: (0, j)),
+        in_specs=[VMEM, VMEM],
+        out_specs=ANY,
+        scratch_shapes=[
+            pltpu.VMEM((tok_dev, width), jnp.bfloat16),
+            pltpu.SemaphoreType.DMA((-(-width // STAGE),)),
+        ],
         compiler_params=grant(8),
         cost_estimate=cost(6 * rows_dev * tok_dev * width, 2 * (tok_dev + rows_dev) * width),
         name="combine_rows",
-    )(*([carrier] * SPLIT), rows)
+    )(carrier, rows)
 
 
 def hop(block, step, sections=0):

time: 109 us -> 108 us (level)
    pallas_call x1, Pallas kernels: 2.45 us -> 1.35 us  [combine_rows(): pl.pallas_call(combine_kernel, out_shape=jax.ShapeDtypeStruct((tok_dev, w...]
where the time goes in v6:
time: 108 us; the launch traced here: 107 us
  starting transfers between devices  57 us (53%)
  blocking collectives  21 us (19%)
  waiting for transfers between devices  20.2 us (19%)
  Pallas kernels  7 us (6%)
  local copies, waits for them, and re-layouts  1.77 us (2%)
    ppermute x15, starting transfers between devices, hop(): return lax.ppermute(block, ('section', 'node', 'local'), pairs)  57 us
    ppermute x15, waiting for transfers between devices, hop(): return lax.ppermute(block, ('section', 'node', 'local'), pairs)  20.2 us
    all_to_all x1, blocking collectives, shards(): lax.all_to_all(outgoing, 'node', split_axis=0, concat_axis=0, tiled=True)  11.5 us
    all_to_all x1, blocking collectives, shards(): lax.all_to_all(expert_out.reshape(n_node, CAP, width), 'node', split_axis...  9.56 us
    pallas_call x1, Pallas kernels, pick_rows(): pl.pallas_call(pick_kernel, out_shape=(jax.ShapeDtypeStruct((rows_dev //...  3.31 us
  transfers between devices with their start and end apart: 15, of which 6 were waited for; matrix products, arithmetic and copies ran while one was open for 0% of the time, Pallas kernels for 0%

profile of v6, /device:TPU:64, one launch (start us, length us, event | category | flops | bytes accessed | tf_op | source)
XLA Modules:
  0.0 107.3 jit_solution(18235416176366504564)
XLA Ops:
  0.0 0.0 copy-start
  0.0 3.3 %pick_rows.1 = (bf16[8,2,7168]{2,1,0:T(2,128)(2,1)}, bf16[16,384]{1,0:T(8,128)(2,1)}) custom-call(s32[8]{0:T(128)} %table_ref.1, s32[8,96]{1,0:T(8,128)} %bitcast.15, f32[8,96]{1,0:T(8,128)} %bitcast.16, bf16[96,7168]{1,0:T(8,128)(2,1)} %bitcast.14), custom_call_target="tpu_custom_call" | custom-call | flops 22020096 | bytes 1605632 | tf_op jit(solution)/shard_map/pick_rows/pallas_call | solution.py:92
  3.3 11.5 %all_to_all.10 = bf16[8,2,7168]{2,1,0:T(2,128)(2,1)S(1)} all-to-all(bf16[8,2,7168]{2,1,0:T(2,128)(2,1)} %get-tuple-element.17), channel_id=1, replica_groups=mesh['section'=16,'node'=8,'local'=8] {'node'}, dimensions={0} | all-to-all | bytes 458752 | tf_op jit(solution)/shard_map/all_to_all | solution.py:259
  14.8 0.1 reshape.9.refs_3_
  14.9 6.2 %collective-permute-start.4 = (bf16[16,7168]{1,0:T(8,128)(2,1)S(1)}, bf16[16,7168]{1,0:T(8,128)(2,1)S(1)}, u32[]{:S(2)}, u32[]{:S(2)}) collective-permute-start(bf16[16,7168]{1,0:T(8,128)(2,1)S(1)} %reshape.9.refs_3_), channel_id=1, source_target_pairs={{0,6},{1,7},{2,0},{3,1},{4,2},{5,3},{6,4},{7,5},{8,10},{9,11},{10,... | collective-permute-start | bytes 688136 | tf_op jit(solution)/shard_map/ppermute | solution.py:250
  21.0 1.9 %collective-permute-start = (bf16[16,7168]{1,0:T(8,128)(2,1)S(1)}, bf16[16,7168]{1,0:T(8,128)(2,1)S(1)}, u32[]{:S(2)}, u32[]{:S(2)}) collective-permute-start(bf16[16,7168]{1,0:T(8,128)(2,1)S(1)} %reshape.9.refs_3_), channel_id=1, source_target_pairs={{0,2},{1,3},{2,4},{3,5},{4,6},{5,7},{6,0},{7,1},{8,14},{9,15},{10,... | collective-permute-start | bytes 688136 | tf_op jit(solution)/shard_map/ppermute | solution.py:250
  23.0 2.6 %collective-permute-start.2 = (bf16[16,7168]{1,0:T(8,128)(2,1)S(1)}, bf16[16,7168]{1,0:T(8,128)(2,1)S(1)}, u32[]{:S(2)}, u32[]{:S(2)}) collective-permute-start(bf16[16,7168]{1,0:T(8,128)(2,1)S(1)} %reshape.9.refs_3_), channel_id=1, source_target_pairs={{0,1},{1,2},{2,3},{3,4},{4,5},{5,6},{6,7},{7,0},{8,15},{9,8},{10,9... | collective-permute-start | bytes 688136 | tf_op jit(solution)/shard_map/ppermute | solution.py:250
  25.6 4.6 %collective-permute-start.3 = (bf16[16,7168]{1,0:T(8,128)(2,1)S(1)}, bf16[16,7168]{1,0:T(8,128)(2,1)S(1)}, u32[]{:S(2)}, u32[]{:S(2)}) collective-permute-start(bf16[16,7168]{1,0:T(8,128)(2,1)S(1)} %reshape.9.refs_3_), channel_id=1, source_target_pairs={{0,7},{1,0},{2,1},{3,2},{4,3},{5,4},{6,5},{7,6},{8,9},{9,10},{10,1... | collective-permute-start | bytes 688136 | tf_op jit(solution)/shard_map/ppermute | solution.py:250
  30.2 1.1 %collective-permute-done.4.refs_5_ = bf16[16,7168]{1,0:T(8,128)(2,1)S(1)} collective-permute-done((bf16[16,7168]{1,0:T(8,128)(2,1)S(1)}, bf16[16,7168]{1,0:T(8,128)(2,1)S(1)}, u32[]{:S(2)}, u32[]{:S(2)}) %collective-permute-start.4) | collective-permute-done | bytes 229408 | tf_op jit(solution)/shard_map/ppermute | solution.py:250
  31.2 2.9 %collective-permute-start.5 = (bf16[16,7168]{1,0:T(8,128)(2,1)S(1)}, bf16[16,7168]{1,0:T(8,128)(2,1)S(1)}, u32[]{:S(2)}, u32[]{:S(2)}) collective-permute-start(bf16[16,7168]{1,0:T(8,128)(2,1)S(1)} %collective-permute-done.4.refs_5_), channel_id=1, source_target_pairs={{0,7},{1,0},{2,1},{3,2},{4,3},{5,4},{6,5},{7,6},{8,9},{9,10},{10,1... | collective-permute-start | bytes 688136 | tf_op jit(solution)/shard_map/ppermute | solution.py:250
  34.1 0.0 collective-permute-done.refs_1_
  34.1 3.2 %collective-permute-start.6 = (bf16[16,7168]{1,0:T(8,128)(2,1)S(1)}, bf16[16,7168]{1,0:T(8,128)(2,1)S(1)}, u32[]{:S(2)}, u32[]{:S(2)}) collective-permute-start(bf16[16,7168]{1,0:T(8,128)(2,1)S(1)} %collective-permute-done.refs_1_), channel_id=1, source_target_pairs={{0,2},{1,3},{2,4},{3,5},{4,6},{5,7},{6,0},{7,1},{8,14},{9,15},{10,... | collective-permute-start | bytes 688136 | tf_op jit(solution)/shard_map/ppermute | solution.py:250
  37.3 3.9 %collective-permute-start.1 = (bf16[16,7168]{1,0:T(8,128)(2,1)S(1)}, bf16[16,7168]{1,0:T(8,128)(2,1)S(1)}, u32[]{:S(2)}, u32[]{:S(2)}) collective-permute-start(bf16[16,7168]{1,0:T(8,128)(2,1)S(1)} %collective-permute-done.refs_1_), channel_id=1, source_target_pairs={{0,1},{1,2},{2,3},{3,4},{4,5},{5,6},{6,7},{7,0},{8,15},{9,8},{10,9... | collective-permute-start | bytes 688136 | tf_op jit(solution)/shard_map/ppermute | solution.py:250
  41.2 0.0 collective-permute-done.2.refs_2_
  41.2 0.0 copy-done
  41.2 0.0 copy-start.1
  41.2 1.5 %copy-done.1 = bf16[1,128,7168]{2,1,0:T(8,128)(2,1)S(1)} copy-done((bf16[1,128,7168]{2,1,0:T(8,128)(2,1)S(1)}, bf16[1,128,7168]{2,1,0:T(8,128)(2,1)}, u32[]{:S(2)}) %copy-start.1) | copy-done | bytes 1835032
  42.7 0.0 copy-start.2
  42.7 0.0 copy-start.3
  42.7 0.3 load.1
  43.0 0.0 collective-permute-done.3.refs_4_
  43.0 0.0 collective-permute-done.5.refs_6_
  43.0 1.2 %collective-permute-done.6.refs_7_ = bf16[16,7168]{1,0:T(8,128)(2,1)S(1)} collective-permute-done((bf16[16,7168]{1,0:T(8,128)(2,1)S(1)}, bf16[16,7168]{1,0:T(8,128)(2,1)S(1)}, u32[]{:S(2)}, u32[]{:S(2)}) %collective-permute-start.6) | collective-permute-done | bytes 229408 | tf_op jit(solution)/shard_map/ppermute | solution.py:250
  44.2 4.9 %collective-permute-done.1.refs_0_ = bf16[16,7168]{1,0:T(8,128)(2,1)S(1)} collective-permute-done((bf16[16,7168]{1,0:T(8,128)(2,1)S(1)}, bf16[16,7168]{1,0:T(8,128)(2,1)S(1)}, u32[]{:S(2)}, u32[]{:S(2)}) %collective-permute-start.1) | collective-permute-done | bytes 229408 | tf_op jit(solution)/shard_map/ppermute | solution.py:250
  49.1 0.0 copy-done.2
  49.1 0.0 copy-done.3
  49.1 1.8 %experts.1 = (bf16[16,7168]{1,0:T(8,128)(2,1)S(1)}, bf16[16,7168]{1,0:T(8,128)(2,1)S(1)}, bf16[16,7168]{1,0:T(8,128)(2,1)S(1)}, bf16[16,7552]{1,0:T(8,128)(2,1)S...) custom-call(bf16[16,7168]{1,0:T(8,128)(2,1)S(1)} %collective-permute, ...), custom_call_target="tpu_custom_call" | custom-call | flops 704643072 | bytes 5505024 | tf_op jit(solution)/shard_map/experts/pallas_call | solution.py:164
  50.9 2.4 %collective-permute-start.7 = (bf16[16,7168]{1,0:T(8,128)(2,1)S(1)}, bf16[16,7168]{1,0:T(8,128)(2,1)S(1)}, u32[]{:S(2)}, u32[]{:S(2)}) collective-permute-start(bf16[16,7168]{1,0:T(8,128)(2,1)S(1)} %get-tuple-element.22), channel_id=1, source_target_pairs={{0,1},{1,2},{2,3},{3,4},{4,5},{5,6},{6,7},{7,0},{8,15},{9,8},{10,9... | collective-permute-start | bytes 688136 | tf_op jit(solution)/shard_map/ppermute | solution.py:250
  53.2 4.7 %collective-permute-start.8 = (bf16[16,7168]{1,0:T(8,128)(2,1)S(1)}, bf16[16,7168]{1,0:T(8,128)(2,1)S(1)}, u32[]{:S(2)}, u32[]{:S(2)}) collective-permute-start(bf16[16,7168]{1,0:T(8,128)(2,1)S(1)} %get-tuple-element.23), channel_id=1, source_target_pairs={{0,7},{1,0},{2,1},{3,2},{4,3},{5,4},{6,5},{7,6},{8,9},{9,10},{10,1... | collective-permute-start | bytes 688136 | tf_op jit(solution)/shard_map/ppermute | solution.py:250
  57.9 1.9 %collective-permute-start.10 = (bf16[16,7168]{1,0:T(8,128)(2,1)S(1)}, bf16[16,7168]{1,0:T(8,128)(2,1)S(1)}, u32[]{:S(2)}, u32[]{:S(2)}) collective-permute-start(bf16[16,7168]{1,0:T(8,128)(2,1)S(1)} %get-tuple-element.25), channel_id=1, source_target_pairs={{0,2},{1,3},{2,4},{3,5},{4,6},{5,7},{6,0},{7,1},{8,14},{9,15},{10,... | collective-permute-start | bytes 688136 | tf_op jit(solution)/shard_map/ppermute | solution.py:250
  59.9 4.3 %collective-permute-start.11 = (bf16[16,7168]{1,0:T(8,128)(2,1)S(1)}, bf16[16,7168]{1,0:T(8,128)(2,1)S(1)}, u32[]{:S(2)}, u32[]{:S(2)}) collective-permute-start(bf16[16,7168]{1,0:T(8,128)(2,1)S(1)} %get-tuple-element.26), channel_id=1, source_target_pairs={{0,1},{1,2},{2,3},{3,4},{4,5},{5,6},{6,7},{7,0},{8,15},{9,8},{10,9... | collective-permute-start | bytes 688136 | tf_op jit(solution)/shard_map/ppermute | solution.py:250
  64.2 2.7 %collective-permute-start.13 = (bf16[16,7168]{1,0:T(8,128)(2,1)S(1)}, bf16[16,7168]{1,0:T(8,128)(2,1)S(1)}, u32[]{:S(2)}, u32[]{:S(2)}) collective-permute-start(bf16[16,7168]{1,0:T(8,128)(2,1)S(1)} %get-tuple-element.28), channel_id=1, source_target_pairs={{0,7},{1,0},{2,1},{3,2},{4,3},{5,4},{6,5},{7,6},{8,9},{9,10},{10,1... | collective-permute-start | bytes 688136 | tf_op jit(solution)/shard_map/ppermute | solution.py:250
  66.9 0.0 collective-permute-done.7.refs_1_
  66.9 0.0 collective-permute-done.8.refs_2_
  67.0 0.1 plus.4
  67.1 4.3 %collective-permute-start.9 = (bf16[16,7552]{1,0:T(8,128)(2,1)S(1)}, bf16[16,7552]{1,0:T(8,128)(2,1)S(1)}, u32[]{:S(2)}, u32[]{:S(2)}) collective-permute-start(bf16[16,7552]{1,0:T(8,128)(2,1)S(1)} %plus.4), channel_id=1, source_target_pairs={{0,64},{1,65},{2,66},{3,67},{4,68},{5,69},{6,70},{7,71},{8,72},{9,... | collective-permute-start | bytes 725000 | tf_op jit(solution)/shard_map/ppermute | solution.py:250
  71.3 0.0 collective-permute-done.10.refs_1_
  71.3 1.5 %collective-permute-done.11.refs_2_ = bf16[16,7168]{1,0:T(8,128)(2,1)S(1)} collective-permute-done((bf16[16,7168]{1,0:T(8,128)(2,1)S(1)}, bf16[16,7168]{1,0:T(8,128)(2,1)S(1)}, u32[]{:S(2)}, u32[]{:S(2)}) %collective-permute-start.11) | collective-permute-done | bytes 229408 | tf_op jit(solution)/shard_map/ppermute | solution.py:250
  72.9 0.1 plus.5
  73.0 6.1 %collective-permute-start.12 = (bf16[16,7168]{1,0:T(8,128)(2,1)S(1)}, bf16[16,7168]{1,0:T(8,128)(2,1)S(1)}, u32[]{:S(2)}, u32[]{:S(2)}) collective-permute-start(bf16[16,7168]{1,0:T(8,128)(2,1)S(1)} %plus.5), channel_id=1, source_target_pairs={{0,66},{1,67},{2,68},{3,69},{4,70},{5,71},{6,64},{7,65},{8,78},{9,... | collective-permute-start | bytes 688136 | tf_op jit(solution)/shard_map/ppermute | solution.py:250
  79.1 0.0 collective-permute-done.13.refs_1_
  79.1 0.1 plus.6
  79.1 5.5 %collective-permute-start.14 = (bf16[16,7168]{1,0:T(8,128)(2,1)S(1)}, bf16[16,7168]{1,0:T(8,128)(2,1)S(1)}, u32[]{:S(2)}, u32[]{:S(2)}) collective-permute-start(bf16[16,7168]{1,0:T(8,128)(2,1)S(1)} %plus.6), channel_id=1, source_target_pairs={{0,70},{1,71},{2,64},{3,65},{4,66},{5,67},{6,68},{7,69},{8,74},{9,... | collective-permute-start | bytes 688136 | tf_op jit(solution)/shard_map/ppermute | solution.py:250
  84.6 10.3 %collective-permute-done.12.refs_1_ = bf16[16,7168]{1,0:T(8,128)(2,1)S(1)} collective-permute-done((bf16[16,7168]{1,0:T(8,128)(2,1)S(1)}, bf16[16,7168]{1,0:T(8,128)(2,1)S(1)}, u32[]{:S(2)}, u32[]{:S(2)}) %collective-permute-start.12) | collective-permute-done | bytes 229408 | tf_op jit(solution)/shard_map/ppermute | solution.py:250
  94.9 1.2 %collective-permute-done.14.refs_2_ = bf16[16,7168]{1,0:T(8,128)(2,1)S(1)} collective-permute-done((bf16[16,7168]{1,0:T(8,128)(2,1)S(1)}, bf16[16,7168]{1,0:T(8,128)(2,1)S(1)}, u32[]{:S(2)}, u32[]{:S(2)}) %collective-permute-start.14) | collective-permute-done | bytes 229408 | tf_op jit(solution)/shard_map/ppermute | solution.py:250
  96.1 0.0 collective-permute-done.9.refs_0_.carrier_ref
  96.1 0.1 plus.7
  96.2 0.1 reshape.10
  96.3 9.6 %all_to_all.11 = bf16[8,2,7168]{2,1,0:T(2,128)(2,1)S(1)} all-to-all(bf16[8,2,7168]{2,1,0:T(2,128)(2,1)S(1)} %reshape.10), channel_id=1, replica_groups=mesh['section'=16,'node'=8,'local'=8] {'node'}, dimensions={0} | all-to-all | bytes 458752 | tf_op jit(solution)/shard_map/all_to_all | solution.py:277
  105.8 0.1 reshape.11.rows_ref
  105.9 1.4 %combine_rows.1 = bf16[96,7168]{1,0:T(8,128)(2,1)} custom-call(bf16[16,7552]{1,0:T(8,128)(2,1)S(1)} %collective-permute-done.9.refs_0_.carrier_ref, bf16[16,7168]{1,0:T(8,128)(2,1)S(1)} %reshape.11.rows_ref), custom_call_target="tpu_custom_call" | custom-call | flops 66060288 | bytes 1605632 | tf_op jit(solution)/shard_map/combine_rows/pallas_call | solution.py:224
Async XLA Ops:
  0.0 41.2 %copy-start = (bf16[1,7168,128]{2,1,0:T(8,128)(2,1)S(1)}, bf16[1,7168,128]{2,1,0:T(8,128)(2,1)}, u32[]{:S(2)}) copy-start(bf16[1,7168,128]{2,1,0:T(8,128)(2,1)} %param.12) | copy-start | bytes 5505028
  14.9 16.4 %collective-permute-start.4 = (bf16[16,7168]{1,0:T(8,128)(2,1)S(1)}, bf16[16,7168]{1,0:T(8,128)(2,1)S(1)}, u32[]{:S(2)}, u32[]{:S(2)}) collective-permute-start(bf16[16,7168]{1,0:T(8,128)(2,1)S(1)} %reshape.9.refs_3_), channel_id=1, source_target_pairs={{0,6},{1,7},{2,0},{3,1},{4,2},{5,3},{6,4},{7,5},{8,10},{9,11},{10,... | collective-permute-start | bytes 688136 | tf_op jit(solution)/shard_map/ppermute | solution.py:250
  21.0 13.1 %collective-permute-start = (bf16[16,7168]{1,0:T(8,128)(2,1)S(1)}, bf16[16,7168]{1,0:T(8,128)(2,1)S(1)}, u32[]{:S(2)}, u32[]{:S(2)}) collective-permute-start(bf16[16,7168]{1,0:T(8,128)(2,1)S(1)} %reshape.9.refs_3_), channel_id=1, source_target_pairs={{0,2},{1,3},{2,4},{3,5},{4,6},{5,7},{6,0},{7,1},{8,14},{9,15},{10,... | collective-permute-start | bytes 688136 | tf_op jit(solution)/shard_map/ppermute | solution.py:250
  23.0 18.2 %collective-permute-start.2 = (bf16[16,7168]{1,0:T(8,128)(2,1)S(1)}, bf16[16,7168]{1,0:T(8,128)(2,1)S(1)}, u32[]{:S(2)}, u32[]{:S(2)}) collective-permute-start(bf16[16,7168]{1,0:T(8,128)(2,1)S(1)} %reshape.9.refs_3_), channel_id=1, source_target_pairs={{0,1},{1,2},{2,3},{3,4},{4,5},{5,6},{6,7},{7,0},{8,15},{9,8},{10,9... | collective-permute-start | bytes 688136 | tf_op jit(solution)/shard_map/ppermute | solution.py:250
  25.6 17.4 %collective-permute-start.3 = (bf16[16,7168]{1,0:T(8,128)(2,1)S(1)}, bf16[16,7168]{1,0:T(8,128)(2,1)S(1)}, u32[]{:S(2)}, u32[]{:S(2)}) collective-permute-start(bf16[16,7168]{1,0:T(8,128)(2,1)S(1)} %reshape.9.refs_3_), channel_id=1, source_target_pairs={{0,7},{1,0},{2,1},{3,2},{4,3},{5,4},{6,5},{7,6},{8,9},{9,10},{10,1... | collective-permute-start | bytes 688136 | tf_op jit(solution)/shard_map/ppermute | solution.py:250
  31.2 11.8 %collective-permute-start.5 = (bf16[16,7168]{1,0:T(8,128)(2,1)S(1)}, bf16[16,7168]{1,0:T(8,128)(2,1)S(1)}, u32[]{:S(2)}, u32[]{:S(2)}) collective-permute-start(bf16[16,7168]{1,0:T(8,128)(2,1)S(1)} %collective-permute-done.4.refs_5_), channel_id=1, source_target_pairs={{0,7},{1,0},{2,1},{3,2},{4,3},{5,4},{6,5},{7,6},{8,9},{9,10},{10,1... | collective-permute-start | bytes 688136 | tf_op jit(solution)/shard_map/ppermute | solution.py:250
  34.1 10.1 %collective-permute-start.6 = (bf16[16,7168]{1,0:T(8,128)(2,1)S(1)}, bf16[16,7168]{1,0:T(8,128)(2,1)S(1)}, u32[]{:S(2)}, u32[]{:S(2)}) collective-permute-start(bf16[16,7168]{1,0:T(8,128)(2,1)S(1)} %collective-permute-done.refs_1_), channel_id=1, source_target_pairs={{0,2},{1,3},{2,4},{3,5},{4,6},{5,7},{6,0},{7,1},{8,14},{9,15},{10,... | collective-permute-start | bytes 688136 | tf_op jit(solution)/shard_map/ppermute | solution.py:250
  37.3 11.8 %collective-permute-start.1 = (bf16[16,7168]{1,0:T(8,128)(2,1)S(1)}, bf16[16,7168]{1,0:T(8,128)(2,1)S(1)}, u32[]{:S(2)}, u32[]{:S(2)}) collective-permute-start(bf16[16,7168]{1,0:T(8,128)(2,1)S(1)} %collective-permute-done.refs_1_), channel_id=1, source_target_pairs={{0,1},{1,2},{2,3},{3,4},{4,5},{5,6},{6,7},{7,0},{8,15},{9,8},{10,9... | collective-permute-start | bytes 688136 | tf_op jit(solution)/shard_map/ppermute | solution.py:250
  41.2 1.5 %copy-start.1 = (bf16[1,128,7168]{2,1,0:T(8,128)(2,1)S(1)}, bf16[1,128,7168]{2,1,0:T(8,128)(2,1)}, u32[]{:S(2)}) copy-start(bf16[1,128,7168]{2,1,0:T(8,128)(2,1)} %param.13) | copy-start | bytes 5505028
  42.7 6.4 %copy-start.2 = (bf16[1,7168,128]{2,1,0:T(8,128)(2,1)S(1)}, bf16[1,7168,128]{2,1,0:T(8,128)(2,1)}, u32[]{:S(2)}) copy-start(bf16[1,7168,128]{2,1,0:T(8,128)(2,1)} %param.11) | copy-start | bytes 5505028
  42.7 6.4 %copy-start.3 = (bf16[16,384]{1,0:T(8,128)(2,1)S(1)}, bf16[16,384]{1,0:T(8,128)(2,1)}, u32[]{:S(2)}) copy-start(bf16[16,384]{1,0:T(8,128)(2,1)} %get-tuple-element.20.refs_11_) | copy-start | bytes 36868
  50.9 16.1 %collective-permute-start.7 = (bf16[16,7168]{1,0:T(8,128)(2,1)S(1)}, bf16[16,7168]{1,0:T(8,128)(2,1)S(1)}, u32[]{:S(2)}, u32[]{:S(2)}) collective-permute-start(bf16[16,7168]{1,0:T(8,128)(2,1)S(1)} %get-tuple-element.22), channel_id=1, source_target_pairs={{0,1},{1,2},{2,3},{3,4},{4,5},{5,6},{6,7},{7,0},{8,15},{9,8},{10,9... | collective-permute-start | bytes 688136 | tf_op jit(solution)/shard_map/ppermute | solution.py:250
  53.2 13.7 %collective-permute-start.8 = (bf16[16,7168]{1,0:T(8,128)(2,1)S(1)}, bf16[16,7168]{1,0:T(8,128)(2,1)S(1)}, u32[]{:S(2)}, u32[]{:S(2)}) collective-permute-start(bf16[16,7168]{1,0:T(8,128)(2,1)S(1)} %get-tuple-element.23), channel_id=1, source_target_pairs={{0,7},{1,0},{2,1},{3,2},{4,3},{5,4},{6,5},{7,6},{8,9},{9,10},{10,1... | collective-permute-start | bytes 688136 | tf_op jit(solution)/shard_map/ppermute | solution.py:250
  57.9 13.4 %collective-permute-start.10 = (bf16[16,7168]{1,0:T(8,128)(2,1)S(1)}, bf16[16,7168]{1,0:T(8,128)(2,1)S(1)}, u32[]{:S(2)}, u32[]{:S(2)}) collective-permute-start(bf16[16,7168]{1,0:T(8,128)(2,1)S(1)} %get-tuple-element.25), channel_id=1, source_target_pairs={{0,2},{1,3},{2,4},{3,5},{4,6},{5,7},{6,0},{7,1},{8,14},{9,15},{10,... | collective-permute-start | bytes 688136 | tf_op jit(solution)/shard_map/ppermute | solution.py:250
  59.9 13.0 %collective-permute-start.11 = (bf16[16,7168]{1,0:T(8,128)(2,1)S(1)}, bf16[16,7168]{1,0:T(8,128)(2,1)S(1)}, u32[]{:S(2)}, u32[]{:S(2)}) collective-permute-start(bf16[16,7168]{1,0:T(8,128)(2,1)S(1)} %get-tuple-element.26), channel_id=1, source_target_pairs={{0,1},{1,2},{2,3},{3,4},{4,5},{5,6},{6,7},{7,0},{8,15},{9,8},{10,9... | collective-permute-start | bytes 688136 | tf_op jit(solution)/shard_map/ppermute | solution.py:250
  64.2 14.8 %collective-permute-start.13 = (bf16[16,7168]{1,0:T(8,128)(2,1)S(1)}, bf16[16,7168]{1,0:T(8,128)(2,1)S(1)}, u32[]{:S(2)}, u32[]{:S(2)}) collective-permute-start(bf16[16,7168]{1,0:T(8,128)(2,1)S(1)} %get-tuple-element.28), channel_id=1, source_target_pairs={{0,7},{1,0},{2,1},{3,2},{4,3},{5,4},{6,5},{7,6},{8,9},{9,10},{10,1... | collective-permute-start | bytes 688136 | tf_op jit(solution)/shard_map/ppermute | solution.py:250
  67.1 29.0 %collective-permute-start.9 = (bf16[16,7552]{1,0:T(8,128)(2,1)S(1)}, bf16[16,7552]{1,0:T(8,128)(2,1)S(1)}, u32[]{:S(2)}, u32[]{:S(2)}) collective-permute-start(bf16[16,7552]{1,0:T(8,128)(2,1)S(1)} %plus.4), channel_id=1, source_target_pairs={{0,64},{1,65},{2,66},{3,67},{4,68},{5,69},{6,70},{7,71},{8,72},{9,... | collective-permute-start | bytes 725000 | tf_op jit(solution)/shard_map/ppermute | solution.py:250
  73.0 21.9 %collective-permute-start.12 = (bf16[16,7168]{1,0:T(8,128)(2,1)S(1)}, bf16[16,7168]{1,0:T(8,128)(2,1)S(1)}, u32[]{:S(2)}, u32[]{:S(2)}) collective-permute-start(bf16[16,7168]{1,0:T(8,128)(2,1)S(1)} %plus.5), channel_id=1, source_target_pairs={{0,66},{1,67},{2,68},{3,69},{4,70},{5,71},{6,64},{7,65},{8,78},{9,... | collective-permute-start | bytes 688136 | tf_op jit(solution)/shard_map/ppermute | solution.py:250
  79.1 17.0 %collective-permute-start.14 = (bf16[16,7168]{1,0:T(8,128)(2,1)S(1)}, bf16[16,7168]{1,0:T(8,128)(2,1)S(1)}, u32[]{:S(2)}, u32[]{:S(2)}) collective-permute-start(bf16[16,7168]{1,0:T(8,128)(2,1)S(1)} %plus.6), channel_id=1, source_target_pairs={{0,70},{1,71},{2,64},{3,65},{4,66},{5,67},{6,68},{7,69},{8,74},{9,... | collective-permute-start | bytes 688136 | tf_op jit(solution)/shard_map/ppermute | solution.py:250
